TPU v7x, 32 devices: a whole 2x2x4 slice. The times are simulated.
32 devices in a mesh: row: 4 (over z), col: 8 (over y, x, core).
Axes of the slice: x: 2, y: 2, z: 4, core: 2. Of those that a mesh axis runs over, the one named last changes fastest.
Arguments:
- hidden_in: bfloat16 [8192, 1536], P(('row', 'col')), may hold values from -6 to 6
- out_grad: bfloat16 [8192, 1536], P(('row', 'col')), may hold values from -6 to 6
- seq_lengths: int32 [4, 16], P('row'), may hold values from 1 to 1024, 2048 in all within a row
- norm1_gain: bfloat16 [1536], P(('row', 'col')), may hold values from 0.25 to 1.75
- q_weight: bfloat16 [1536, 1536], P('row', 'col'), may hold values from -0.15625 to 0.15625
- q_bias: bfloat16 [1536], P(('row', 'col')), may hold values from -3 to 3
- k_weight: bfloat16 [1536, 256], P('row', 'col'), may hold values from -0.15625 to 0.15625
- k_bias: bfloat16 [256], P(('row', 'col')), may hold values from -3 to 3
- v_weight: bfloat16 [1536, 256], P('row', 'col'), may hold values from -0.15625 to 0.15625
- v_bias: bfloat16 [256], P(('row', 'col')), may hold values from -3 to 3
- o_weight: bfloat16 [1536, 1536], P('row', 'col'), may hold values from -0.625 to 0.625
- norm2_gain: bfloat16 [1536], P(('row', 'col')), may hold values from 0.25 to 1.75
- gate_weight: bfloat16 [1536, 8960], P('row', 'col'), may hold values from -0.15625 to 0.15625
- up_weight: bfloat16 [1536, 8960], P('row', 'col'), may hold values from -0.15625 to 0.15625
- down_weight: bfloat16 [8960, 1536], P('col', 'row'), may hold values from -0.375 to 0.375
Outputs:
- layer_out: float32 [8192, 1536], P(('row', 'col'))
- input_grad: float32 [8192, 1536], P(('row', 'col'))
- norm1_gain_grad: float32 [1536], P(('row', 'col'))
- q_weight_grad: float32 [1536, 1536], P('row', 'col')
- q_bias_grad: float32 [1536], P(('row', 'col'))
- k_weight_grad: float32 [1536, 256], P('row', 'col')
- k_bias_grad: float32 [256], P(('row', 'col'))
- v_weight_grad: float32 [1536, 256], P('row', 'col')
- v_bias_grad: float32 [256], P(('row', 'col'))
- o_weight_grad: float32 [1536, 1536], P('row', 'col')
- norm2_gain_grad: float32 [1536], P(('row', 'col'))
- gate_weight_grad: float32 [1536, 8960], P('row', 'col')
- up_weight_grad: float32 [1536, 8960], P('row', 'col')
- down_weight_grad: float32 [8960, 1536], P('col', 'row')
Inputs may be any that keep to these rules, and one draw needn't show every extreme that they name: `seq_lengths`: row r lists the lengths of the 16 sequences packed in order into block r of 2048 tokens; they sum to 2048, and the longest is exactly 1024 in every row.
All inputs are finite; a program needn't handle non-finite values.
Results may differ from a plain program's by a relative error of at most 0.03.
Values may be sent and summed in bfloat16 or wider, within the bound.
A program may use at most 192 MiB of HBM per device.

v0:
```python
import math

import jax
import jax.numpy as jnp
from jax import lax
from jax.sharding import PartitionSpec as P

HQ = 12
KVH = 2
HD = 128
MAXLEN = 1024


EPSILON = 1e-06
ROPE_BASE = 1000000.0


def seq_starts(slots, lengths):
    bounds = jnp.cumsum(lengths)
    picked = jnp.where(bounds[None, :] <= slots[:, None], lengths[None, :], 0)
    return jnp.sum(picked, axis=1)


def rope_tables(positions, head_dim):
    steps_up = jnp.arange(head_dim // 2, dtype=jnp.float32)
    freqs = jnp.exp(-math.log(ROPE_BASE) * (2.0 * steps_up / head_dim))
    angles = positions.astype(jnp.float32)[:, None] * freqs[None, :]
    angles = jnp.concatenate([angles, angles], axis=1)
    return (jnp.cos(angles)[:, None, :], jnp.sin(angles)[:, None, :])


def rotate_pairs(values, cosines, sines):
    half_dim = values.shape[-1] // 2
    turned = jnp.concatenate([-values[..., half_dim:], values[..., :half_dim]], axis=-1)
    return values * cosines + turned * sines


def rotate_back(grads_in, cosines, sines):
    half_dim = grads_in.shape[-1] // 2
    moved = grads_in * sines
    return grads_in * cosines + jnp.concatenate(
        [moved[..., half_dim:], -moved[..., :half_dim]], axis=-1
    )


def rms_scale(values):
    return lax.rsqrt(jnp.mean(values * values, axis=-1, keepdims=True) + EPSILON)


def product(left, right):
    return jnp.dot(left, right, preferred_element_type=jnp.float32)


def contract_rows(left, right):
    return lax.dot_general(
        left, right, (((0,), (0,)), ((), ())), preferred_element_type=jnp.float32
    )


def contract_cols(left, right):
    return lax.dot_general(
        left, right, (((1,), (1,)), ((), ())), preferred_element_type=jnp.float32
    )


def rounded_wide(values):
    return lax.optimization_barrier(values.astype(jnp.bfloat16)).astype(jnp.float32)


def assemble(stacked, row_parts, col_parts):
    height, width = (stacked.shape[1], stacked.shape[2])
    grid = stacked.reshape(row_parts, col_parts, height, width).transpose(0, 2, 1, 3)
    return grid.reshape(row_parts * height, col_parts * width)


def split_blocks(full, row_parts, col_parts):
    height = full.shape[0] // row_parts
    width = full.shape[1] // col_parts
    grid = full.reshape(row_parts, height, col_parts, width).transpose(0, 2, 1, 3)
    return grid.reshape(row_parts * col_parts, height, width)


def unpack_attention(stacked, row_parts, col_parts):
    matrices = tuple((assemble(member, row_parts, col_parts) for member in stacked[:4]))
    return matrices + tuple(stacked[4:])


def masked_scores(query_heads, keys_window, visible, score_scale):
    scores = jnp.einsum(
        "tkgd,skd->kgts", query_heads, keys_window, preferred_element_type=jnp.float32
    )
    return jnp.where(visible, scores * score_scale, -jnp.inf)


def shards(
    hidden_in,
    out_grad,
    seq_lengths,
    norm1_gain,
    q_weight,
    q_bias,
    k_weight,
    k_bias,
    v_weight,
    v_bias,
    o_weight,
    norm2_gain,
    gate_weight,
    up_weight,
    down_weight,
):
    row_parts = lax.axis_size("row")
    col_parts = lax.axis_size("col")
    col_place = lax.axis_index("col")
    stacked = (
        lax.all_gather(q_weight[None], ("row", "col"), axis=0, tiled=True),
        lax.all_gather(k_weight[None], ("row", "col"), axis=0, tiled=True),
        lax.all_gather(v_weight[None], ("row", "col"), axis=0, tiled=True),
        lax.all_gather(o_weight[None], ("row", "col"), axis=0, tiled=True),
        lax.all_gather(q_bias, ("row", "col"), axis=0, tiled=True),
        lax.all_gather(k_bias, ("row", "col"), axis=0, tiled=True),
        lax.all_gather(v_bias, ("row", "col"), axis=0, tiled=True),
        lax.all_gather(norm1_gain, ("row", "col"), axis=0, tiled=True),
        lax.all_gather(norm2_gain, ("row", "col"), axis=0, tiled=True),
    )
    attention = unpack_attention(stacked, row_parts, col_parts)
    gate_block, up_block, down_block = (
        lax.all_gather(gate_weight, "row", axis=0, tiled=True),
        lax.all_gather(up_weight, "row", axis=0, tiled=True),
        lax.all_gather(down_weight, "row", axis=1, tiled=True),
    )
    (
        query_matrix,
        key_matrix,
        value_matrix,
        output_matrix,
        query_offset,
        key_offset,
        value_offset,
        first_gain,
        second_gain,
    ) = attention
    own_rows = hidden_in.shape[0]
    row_tokens = own_rows * col_parts
    lengths = seq_lengths[0]
    query_slots = col_place * own_rows + jnp.arange(own_rows, dtype=jnp.int32)
    query_starts = seq_starts(query_slots, lengths)
    cosines, sines = rope_tables(query_slots - query_starts, HD)
    group_size = HQ // KVH
    score_scale = 1.0 / math.sqrt(HD)
    inputs_wide = hidden_in.astype(jnp.float32)
    first_rms = rms_scale(inputs_wide)
    first_unit = inputs_wide * first_rms
    first_normed = (first_unit * first_gain.astype(jnp.float32)).astype(jnp.bfloat16)
    query_base = product(first_normed, query_matrix) + query_offset.astype(jnp.float32)
    key_base = product(first_normed, key_matrix) + key_offset.astype(jnp.float32)
    value_own = (product(first_normed, value_matrix) + value_offset.astype(jnp.float32)).astype(
        jnp.bfloat16
    )
    queries = rotate_pairs(query_base.reshape(own_rows, HQ, HD), cosines, sines).astype(
        jnp.bfloat16
    )
    keys_own = rotate_pairs(key_base.reshape(own_rows, KVH, HD), cosines, sines).astype(
        jnp.bfloat16
    )
    keys_all, values_all = (
        lax.all_gather(keys_own.reshape(own_rows, KVH * HD), "col", axis=0, tiled=True),
        lax.all_gather(value_own, "col", axis=0, tiled=True),
    )
    window = min(own_rows + MAXLEN, row_tokens)
    window_start = jnp.clip(col_place * own_rows - MAXLEN, 0, row_tokens - window)
    key_slots = window_start + jnp.arange(window, dtype=jnp.int32)
    key_starts = seq_starts(key_slots, lengths)
    visible = (query_starts[:, None] == key_starts[None, :]) & (
        key_slots[None, :] <= query_slots[:, None]
    )
    keys_window = lax.dynamic_slice_in_dim(keys_all, window_start, window, 0).reshape(
        window, KVH, HD
    )
    values_window = lax.dynamic_slice_in_dim(values_all, window_start, window, 0).reshape(
        window, KVH, HD
    )
    query_heads = queries.reshape(own_rows, KVH, group_size, HD)
    scores = masked_scores(query_heads, keys_window, visible, score_scale)
    peak = jnp.max(scores, axis=-1, keepdims=True)
    expanded = jnp.exp(scores - peak)
    totals = jnp.sum(expanded, axis=-1, keepdims=True)
    probs = expanded / totals
    log_total = peak + jnp.log(totals)
    mixed = jnp.einsum(
        "kgts,skd->tkgd",
        probs.astype(jnp.bfloat16),
        values_window,
        preferred_element_type=jnp.float32,
    )
    mixed = mixed.reshape(own_rows, HQ * HD).astype(jnp.bfloat16)
    residual = inputs_wide + product(mixed, output_matrix)
    second_rms = rms_scale(residual)
    second_unit = residual * second_rms
    second_normed = (second_unit * second_gain.astype(jnp.float32)).astype(jnp.bfloat16)
    normed_rows = lax.all_gather(second_normed, "col", axis=0, tiled=True)
    gate_act = product(normed_rows, gate_block)
    up_act = product(normed_rows, up_block)
    sigmoid_gate = jax.nn.sigmoid(gate_act)
    silu_gate = gate_act * sigmoid_gate
    hidden = (silu_gate * up_act).astype(jnp.bfloat16)
    branch_out = lax.psum_scatter(
        product(hidden, down_block), "col", scatter_dimension=0, tiled=True
    )
    layer_out = residual + branch_out
    stacked_again = (
        lax.all_gather(q_weight[None], ("row", "col"), axis=0, tiled=True),
        lax.all_gather(k_weight[None], ("row", "col"), axis=0, tiled=True),
        lax.all_gather(v_weight[None], ("row", "col"), axis=0, tiled=True),
        lax.all_gather(o_weight[None], ("row", "col"), axis=0, tiled=True),
        lax.all_gather(q_bias, ("row", "col"), axis=0, tiled=True),
        lax.all_gather(k_bias, ("row", "col"), axis=0, tiled=True),
        lax.all_gather(v_bias, ("row", "col"), axis=0, tiled=True),
        lax.all_gather(norm1_gain, ("row", "col"), axis=0, tiled=True),
        lax.all_gather(norm2_gain, ("row", "col"), axis=0, tiled=True),
    )
    (
        query_matrix,
        key_matrix,
        value_matrix,
        output_matrix,
        query_offset,
        key_offset,
        value_offset,
        first_gain,
        second_gain,
    ) = unpack_attention(stacked_again, row_parts, col_parts)
    gate_block, up_block, down_block = (
        lax.all_gather(gate_weight, "row", axis=0, tiled=True),
        lax.all_gather(up_weight, "row", axis=0, tiled=True),
        lax.all_gather(down_weight, "row", axis=1, tiled=True),
    )
    out_rows = lax.all_gather(out_grad, "col", axis=0, tiled=True)
    hidden_grad = contract_cols(out_rows, down_block)
    down_grad = contract_rows(hidden, out_rows)
    up_grad_act = (hidden_grad * silu_gate).astype(jnp.bfloat16)
    gate_grad_act = (
        hidden_grad * up_act * sigmoid_gate * (1.0 + gate_act * (1.0 - sigmoid_gate))
    ).astype(jnp.bfloat16)
    gate_grad = contract_rows(normed_rows, gate_grad_act)
    up_grad = contract_rows(normed_rows, up_grad_act)
    normed_grad = lax.psum_scatter(
        contract_cols(gate_grad_act, gate_block) + contract_cols(up_grad_act, up_block),
        "col",
        scatter_dimension=0,
        tiled=True,
    )
    second_gain_grad = jnp.sum(normed_grad * second_unit, axis=0)
    unit_grad = normed_grad * second_gain.astype(jnp.float32)
    residual_grad = out_grad.astype(jnp.float32) + second_rms * (
        unit_grad - second_unit * jnp.mean(unit_grad * second_unit, axis=-1, keepdims=True)
    )
    attended_grad = residual_grad.astype(jnp.bfloat16)
    mixed_grad = contract_cols(attended_grad, output_matrix).astype(jnp.bfloat16)
    grad_heads = mixed_grad.reshape(own_rows, KVH, group_size, HD)
    scores = masked_scores(query_heads, keys_window, visible, score_scale)
    probs = jnp.exp(scores - log_total)
    prob_grad = jnp.einsum(
        "tkgd,skd->kgts", grad_heads, values_window, preferred_element_type=jnp.float32
    )
    value_part = jnp.einsum(
        "kgts,tkgd->skd", probs.astype(jnp.bfloat16), grad_heads, preferred_element_type=jnp.float32
    )
    score_grad = (probs * (prob_grad - jnp.sum(probs * prob_grad, axis=-1, keepdims=True))).astype(
        jnp.bfloat16
    )
    query_grad = (
        jnp.einsum("kgts,skd->tkgd", score_grad, keys_window, preferred_element_type=jnp.float32)
        * score_scale
    )
    key_part = (
        jnp.einsum("kgts,tkgd->skd", score_grad, query_heads, preferred_element_type=jnp.float32)
        * score_scale
    )
    empty_rows = jnp.zeros((row_tokens, KVH * HD), jnp.float32)
    key_rows = lax.dynamic_update_slice_in_dim(
        empty_rows, key_part.reshape(window, KVH * HD), window_start, 0
    )
    value_rows = lax.dynamic_update_slice_in_dim(
        empty_rows, value_part.reshape(window, KVH * HD), window_start, 0
    )
    key_grad, value_grad = (
        lax.psum_scatter(key_rows, "col", scatter_dimension=0, tiled=True),
        lax.psum_scatter(value_rows, "col", scatter_dimension=0, tiled=True),
    )
    query_wide = rounded_wide(query_grad.reshape(own_rows, HQ, HD))
    query_base_grad = (
        rotate_back(query_wide, cosines, sines).reshape(own_rows, HQ * HD).astype(jnp.bfloat16)
    )
    key_wide = rounded_wide(key_grad.reshape(own_rows, KVH, HD))
    key_base_grad = (
        rotate_back(key_wide, cosines, sines).reshape(own_rows, KVH * HD).astype(jnp.bfloat16)
    )
    value_base_grad = value_grad.astype(jnp.bfloat16)
    query_b_grad = jnp.sum(query_base_grad.astype(jnp.float32), axis=0)
    key_b_grad = jnp.sum(key_base_grad.astype(jnp.float32), axis=0)
    value_b_grad = jnp.sum(value_base_grad.astype(jnp.float32), axis=0)
    first_normed_grad = (
        contract_cols(query_base_grad, query_matrix)
        + contract_cols(key_base_grad, key_matrix)
        + contract_cols(value_base_grad, value_matrix)
    )
    first_gain_grad = jnp.sum(first_normed_grad * first_unit, axis=0)
    first_unit_grad = first_normed_grad * first_gain.astype(jnp.float32)
    input_grad = residual_grad + first_rms * (
        first_unit_grad
        - first_unit * jnp.mean(first_unit_grad * first_unit, axis=-1, keepdims=True)
    )
    attn_grads = (
        lax.psum_scatter(
            split_blocks(contract_rows(first_normed, query_base_grad), row_parts, col_parts),
            ("row", "col"),
            scatter_dimension=0,
            tiled=True,
        ),
        lax.psum_scatter(
            split_blocks(contract_rows(first_normed, key_base_grad), row_parts, col_parts),
            ("row", "col"),
            scatter_dimension=0,
            tiled=True,
        ),
        lax.psum_scatter(
            split_blocks(contract_rows(first_normed, value_base_grad), row_parts, col_parts),
            ("row", "col"),
            scatter_dimension=0,
            tiled=True,
        ),
        lax.psum_scatter(
            split_blocks(contract_rows(mixed, attended_grad), row_parts, col_parts),
            ("row", "col"),
            scatter_dimension=0,
            tiled=True,
        ),
        lax.psum_scatter(query_b_grad, ("row", "col"), scatter_dimension=0, tiled=True),
        lax.psum_scatter(key_b_grad, ("row", "col"), scatter_dimension=0, tiled=True),
        lax.psum_scatter(value_b_grad, ("row", "col"), scatter_dimension=0, tiled=True),
        lax.psum_scatter(first_gain_grad, ("row", "col"), scatter_dimension=0, tiled=True),
        lax.psum_scatter(second_gain_grad, ("row", "col"), scatter_dimension=0, tiled=True),
    )
    query_w_out = attn_grads[0][0]
    key_w_out = attn_grads[1][0]
    value_w_out = attn_grads[2][0]
    output_w_out = attn_grads[3][0]
    small_out = attn_grads[4:9]
    mlp_grads = (
        lax.psum_scatter(gate_grad, "row", scatter_dimension=0, tiled=True),
        lax.psum_scatter(up_grad, "row", scatter_dimension=0, tiled=True),
        lax.psum_scatter(down_grad, "row", scatter_dimension=1, tiled=True),
    )
    return (
        layer_out,
        input_grad,
        small_out[3],
        query_w_out,
        small_out[0],
        key_w_out,
        small_out[1],
        value_w_out,
        small_out[2],
        output_w_out,
        small_out[4],
        mlp_grads[0],
        mlp_grads[1],
        mlp_grads[2],
    )


def solution(mesh):
    in_specs = (
        P(("row", "col"), None),
        P(("row", "col"), None),
        P("row", None),
        P(("row", "col")),
        P("row", "col"),
        P(("row", "col")),
        P("row", "col"),
        P(("row", "col")),
        P("row", "col"),
        P(("row", "col")),
        P("row", "col"),
        P(("row", "col")),
        P("row", "col"),
        P("row", "col"),
        P("col", "row"),
    )
    out_specs = (
        P(("row", "col"), None),
        P(("row", "col"), None),
        P(("row", "col")),
        P("row", "col"),
        P(("row", "col")),
        P("row", "col"),
        P(("row", "col")),
        P("row", "col"),
        P(("row", "col")),
        P("row", "col"),
        P(("row", "col")),
        P("row", "col"),
        P("row", "col"),
        P("col", "row"),
    )
    return jax.shard_map(shards, mesh=mesh, in_specs=in_specs, out_specs=out_specs, check_vma=False)
```

profile of v0, /device:TPU:8, one launch (start us, length us, event | category | flops | bytes accessed | tf_op | source)
XLA Modules:
  0.0 1828.1 jit_solution(13234642449965689146)
XLA Ops:
  11.6 40.7 %all-reduce.11 = (bf16[256]{0:T(256)(128)(2,1)S(1)}, bf16[1536]{0:T(1024)(128)(2,1)S(1)}, bf16[256]{0:T(256)(128)(2,1)S(1)}, bf16[1536]{0:T(1024)(128)(2,1)S(1)}, bf16[1536]{0:T(1024)(128)(2,1)S(1)}) all-reduce(bf16[256]{0:T(256)(128)(2,1)S(1)} %dynamic-update-slice.1, ...), channel_id=1, replica_groups=mesh['row'=4,'col'=8] {'row','col'}, use_global_device_ids=true, to_apply=%add.1 | all-reduce | flops 5120 | bytes 20480
  53.6 36.5 %all-gather = bf16[12288,32]{0,1:T(8,128)(2,1)S(1)} all-gather(bf16[384,32]{0,1:T(8,128)(2,1)} %param.23), channel_id=2, replica_groups=mesh['row'=4,'col'=8] {'row','col'}, dimensions={0}, use_global_device_ids=true | all-gather | bytes 811008 | tf_op jit(solution)/shard_map/all_gather | solution.py:118
  92.8 38.9 %all-gather.1 = bf16[12288,32]{0,1:T(8,128)(2,1)S(1)} all-gather(bf16[384,32]{0,1:T(8,128)(2,1)S(1)} %copy-done.32), channel_id=3, replica_groups=mesh['row'=4,'col'=8] {'row','col'}, dimensions={0}, use_global_device_ids=true | all-gather | bytes 811008 | tf_op jit(solution)/shard_map/all_gather | solution.py:117
  139.9 21.8 %all-gather.16.cloned.1.call-done = bf16[2048,256]{0,1:T(8,128)(2,1)} async-done(((bf16[256,256]{0,1:T(8,128)(2,1)}), bf16[2048,256]{0,1:T(8,128)(2,1)}) %all-gather.16.cloned.1.call-update) | async-done | bytes 1048592 | tf_op jit(solution)/shard_map/all_gather | solution.py:167
  163.1 63.9 %all-gather.28.cloned.1.call-done = bf16[12288,192]{0,1:T(8,128)(2,1)} async-done(((bf16[384,192]{0,1:T(8,128)(2,1)}), bf16[12288,192]{0,1:T(8,128)(2,1)}) %all-gather.28.cloned.1.call-update) | async-done | bytes 4718608 | tf_op jit(solution)/shard_map/all_gather | solution.py:116
  241.0 50.6 %all-gather.30.cloned.1.call-done = bf16[12288,192]{0,1:T(8,128)(2,1)} async-done(((bf16[384,192]{0,1:T(8,128)(2,1)}), bf16[12288,192]{0,1:T(8,128)(2,1)}) %all-gather.30.cloned.1.call-update) | async-done | bytes 4718608 | tf_op jit(solution)/shard_map/all_gather | solution.py:119
  325.8 32.9 %all-gather.20.cloned.1.call-done = bf16[1536,1120]{0,1:T(8,128)(2,1)} async-done(((bf16[384,1120]{0,1:T(8,128)(2,1)}), bf16[1536,1120]{0,1:T(8,128)(2,1)}) %all-gather.20.cloned.1.call-update) | async-done | bytes 3440656 | tf_op jit(solution)/shard_map/all_gather | solution.py:128
  358.7 48.0 %all-gather.18.cloned.1.call-done = bf16[2048,1536]{1,0:T(8,128)(2,1)} async-done(((bf16[256,1536]{1,0:T(8,128)(2,1)}), bf16[2048,1536]{1,0:T(8,128)(2,1)}) %all-gather.18.cloned.1.call-update) | async-done | bytes 6291472 | tf_op jit(solution)/shard_map/all_gather | solution.py:201
  406.7 12.9 fusion.47
  419.6 55.1 %all-gather.22.cloned.1.call-done = bf16[1536,1120]{0,1:T(8,128)(2,1)} async-done(((bf16[384,1120]{0,1:T(8,128)(2,1)}), bf16[1536,1120]{0,1:T(8,128)(2,1)}) %all-gather.22.cloned.1.call-update) | async-done | bytes 3440656 | tf_op jit(solution)/shard_map/all_gather | solution.py:129
  474.7 12.9 fusion.48
  487.5 55.4 %all-gather.24.cloned.1.call-done = bf16[1120,1536]{1,0:T(8,128)(2,1)} async-done(((bf16[1120,384]{1,0:T(8,128)(2,1)}), bf16[1120,1536]{1,0:T(8,128)(2,1)}) %all-gather.24.cloned.1.call-update) | async-done | bytes 3440656 | tf_op jit(solution)/shard_map/all_gather | solution.py:130
  543.0 47.6 %all-gather.26.cloned.1.call-done = bf16[2048,1536]{1,0:T(8,128)(2,1)} async-done(((bf16[256,1536]{1,0:T(8,128)(2,1)}), bf16[2048,1536]{1,0:T(8,128)(2,1)}) %all-gather.26.cloned.1.call-update) | async-done | bytes 6291472 | tf_op jit(solution)/shard_map/all_gather | solution.py:238
  590.5 20.8 %multiply_convert_fusion = (bf16[2048,1120]{0,1:T(8,128)(2,1)}, bf16[2048,1120]{0,1:T(8,128)(2,1)}, bf16[2048,1120]{0,1:T(8,128)(2,1)}) fusion(f32[2048,1120]{0,1:T(8,128)} %fusion.47, f32[2048,1120]{0,1:T(8,128)} %fusion.48, bf16[2048,1536]{1,0:T(8,128)(2,1)} %all-gather.26.cloned.1.call-done, bf16[1120,1536]{1,0:T(8,128)(2,1)} %all-gather.24.cloned.1.call-done), kind=kOutput, calls=%fused_computation.11 | convolution fusion | flops 7080837120 | bytes 41844736 | tf_op jit(solution)/shard_map/dot_general | solution.py:61
  611.3 13.5 fusion.50
  624.8 14.0 convolution_add_fusion
  638.9 15.2 fusion.49
  654.3 77.0 %reduce-scatter.14.cloned.1.call-done = f32[256,1536]{1,0:T(8,128)} async-done(((f32[2048,1536]{1,0:T(8,128)}), f32[256,1536]{1,0:T(8,128)}) %reduce-scatter.14.cloned.1.call-update) | async-done | bytes 1572880 | tf_op jit(solution)/shard_map/reduce_scatter | solution.py:247
  733.2 93.9 %reduce-scatter.12.cloned.1.call-done = f32[256,1536]{1,0:T(8,128)} async-done(((f32[2048,1536]{1,0:T(8,128)}), f32[256,1536]{1,0:T(8,128)}) %reduce-scatter.12.cloned.1.call-update) | async-done | bytes 1572880 | tf_op jit(solution)/shard_map/reduce_scatter | solution.py:207
  836.2 12.6 fusion
  881.5 10.8 dynamic_update_slice.7
  893.8 12.9 fusion.56
  907.0 12.6 fusion.57
  919.7 12.6 fusion.55
  991.6 48.9 %all-reduce.10 = (f32[1536]{0:T(1024)S(1)}, f32[1536]{0:T(1024)S(1)}, f32[256]{0:T(256)S(1)}, f32[256]{0:T(256)S(1)}, f32[1536]{0:T(1024)S(1)}) all-reduce(f32[1536]{0:T(1024)S(1)} %copy-done.31, f32[1536]{0:T(1024)S(1)} %bitcast.257, f32[256]{0:T(256)S(1)} %bitcast.261, ...), channel_id=10, replica_groups=mesh['row'=4,'col'=8] {'row','col'}, use_global_device_ids=true, to_apply=%region_15.16.clone | all-reduce | flops 5120 | bytes 40960
  1046.3 37.8 %reduce-scatter.28.cloned.1.call-done = f32[384,1120]{0,1:T(8,128)} async-done(((f32[1536,1120]{0,1:T(8,128)}), f32[384,1120]{0,1:T(8,128)}) %reduce-scatter.28.cloned.1.call-update) | async-done | bytes 1720336 | tf_op jit(solution)/shard_map/reduce_scatter | solution.py:351
  1084.2 123.6 %reduce-scatter.30.cloned.1.call-done = f32[384,1120]{0,1:T(8,128)} async-done(((f32[1536,1120]{0,1:T(8,128)}), f32[384,1120]{0,1:T(8,128)}) %reduce-scatter.30.cloned.1.call-update) | async-done | bytes 1720336 | tf_op jit(solution)/shard_map/reduce_scatter | solution.py:352
  1207.7 123.6 %reduce-scatter.32.cloned.1.call-done = f32[1120,384]{1,0:T(8,128)} async-done(((f32[1120,1536]{1,0:T(8,128)}), f32[1120,384]{1,0:T(8,128)}) %reduce-scatter.32.cloned.1.call-update) | async-done | bytes 1720336 | tf_op jit(solution)/shard_map/reduce_scatter | solution.py:353
  1331.4 104.0 %reduce-scatter.22.cloned.1.call-done = f32[1,384,32]{1,2,0:T(8,128)} async-done(((f32[32,384,32]{1,2,0:T(8,128)}), f32[1,384,32]{1,2,0:T(8,128)}) %reduce-scatter.22.cloned.1.call-update) | async-done | bytes 49168 | tf_op jit(solution)/shard_map/reduce_scatter | solution.py:321
  1435.4 102.7 %reduce-scatter.24.cloned.1.call-done = f32[1,384,32]{1,2,0:T(8,128)} async-done(((f32[32,384,32]{1,2,0:T(8,128)}), f32[1,384,32]{1,2,0:T(8,128)}) %reduce-scatter.24.cloned.1.call-update) | async-done | bytes 49168 | tf_op jit(solution)/shard_map/reduce_scatter | solution.py:327
  1538.1 141.5 %reduce-scatter.26.cloned.1.call-done = f32[1,384,192]{1,2,0:T(8,128)} async-done(((f32[32,384,192]{1,2,0:T(8,128)}), f32[1,384,192]{1,2,0:T(8,128)}) %reduce-scatter.26.cloned.1.call-update) | async-done | bytes 294928 | tf_op jit(solution)/shard_map/reduce_scatter | solution.py:333
  1679.6 141.4 %reduce-scatter.20.cloned.1.call-done = f32[1,384,192]{1,2,0:T(8,128)} async-done(((f32[32,384,192]{1,2,0:T(8,128)}), f32[1,384,192]{1,2,0:T(8,128)}) %reduce-scatter.20.cloned.1.call-update) | async-done | bytes 294928 | tf_op jit(solution)/shard_map/reduce_scatter | solution.py:315
  (236 shorter events, 176.2 us)
Async XLA Ops:
  7.2 84.4 %copy-start.1 = (bf16[256,1536]{1,0:T(8,128)(2,1)S(1)}, bf16[256,1536]{1,0:T(8,128)(2,1)}, u32[]{:S(2)}) copy-start(bf16[256,1536]{1,0:T(8,128)(2,1)} %param.15) | copy-start | bytes 2359300
  7.2 130.4 %all-gather.14.cloned.1.call-start = ((), (), s32[]{:S(2)}) async-start(), calls=%async_computation.11 | async-start | bytes 1179648 | tf_op jit(solution)/shard_map/all_gather | solution.py:168
  52.2 180.9 %copy-start.28 = (f32[1536]{0:T(1024)}, f32[1536]{0:T(1024)S(1)}, u32[]{:S(2)}) copy-start(f32[1536]{0:T(1024)S(1)} %convert_element_type.134) | copy-start | bytes 18436
  53.6 179.5 %copy-start.33 = (f32[256]{0:T(256)}, f32[256]{0:T(256)S(1)}, u32[]{:S(2)}) copy-start(f32[256]{0:T(256)S(1)} %add_rsqrt_fusion.1) | copy-start | bytes 3076
  92.7 39.5 %copy-start.36 = (s32[1,16]{1,0:T(1,128)S(1)}, s32[1,16]{1,0:T(1,128)}, u32[]{:S(2)}) copy-start(s32[1,16]{1,0:T(1,128)} %param.17) | copy-start | bytes 196
  92.7 69.0 %all-gather.16.cloned.1.call-start = ((), (), s32[]{:S(2)}) async-start(), calls=%async_computation.12 | async-start | bytes 1179648 | tf_op jit(solution)/shard_map/all_gather | solution.py:167
  133.1 164.5 %copy-start.12 = (f32[256,128]{0,1:T(8,128)}, f32[256,128]{0,1:T(8,128)S(1)}, u32[]{:S(2)}) copy-start(f32[256,128]{0,1:T(8,128)S(1)} %get-tuple-element.47) | copy-start | bytes 393220
  134.4 92.6 %all-gather.28.cloned.1.call-start = ((), (), s32[]{:S(2)}) async-start(), calls=%async_computation.29 | async-start | bytes 4866048 | tf_op jit(solution)/shard_map/all_gather | solution.py:116
  135.1 156.4 %all-gather.30.cloned.1.call-start = ((), (), s32[]{:S(2)}) async-start(), calls=%async_computation.30 | async-start | bytes 4866048 | tf_op jit(solution)/shard_map/all_gather | solution.py:119
  135.7 223.0 %all-gather.20.cloned.1.call-start = ((), (), s32[]{:S(2)}) async-start(), calls=%async_computation.14 | async-start | bytes 4300800 | tf_op jit(solution)/shard_map/all_gather | solution.py:128
  136.3 270.4 %all-gather.18.cloned.1.call-start = ((), (), s32[]{:S(2)}) async-start(), calls=%async_computation.13 | async-start | bytes 7077888 | tf_op jit(solution)/shard_map/all_gather | solution.py:201
  163.1 135.4 %copy-start.8 = (bf16[1280,256]{0,1:T(8,128)(2,1)}, bf16[1280,256]{0,1:T(8,128)(2,1)S(1)}, u32[]{:S(2)}) copy-start(bf16[1280,256]{0,1:T(8,128)(2,1)S(1)} %constant_dynamic-slice_fusion) | copy-start | bytes 1966084
  297.6 23.2 %copy-start.11 = (bf16[192,8,4,384]{3,1,2,0:T(8,128)(2,1)}, bf16[192,8,4,384]{3,1,2,0:T(8,128)(2,1)S(1)}, u32[]{:S(2)}) copy-start(bf16[192,8,4,384]{3,1,2,0:T(8,128)(2,1)S(1)} %copy.164) | copy-start | bytes 14155780
  323.5 151.2 %all-gather.22.cloned.1.call-start = ((), (), s32[]{:S(2)}) async-start(), calls=%async_computation.15 | async-start | bytes 4300800 | tf_op jit(solution)/shard_map/all_gather | solution.py:129
  324.2 218.7 %all-gather.24.cloned.1.call-start = ((), (), s32[]{:S(2)}) async-start(), calls=%async_computation.16 | async-start | bytes 4300800 | tf_op jit(solution)/shard_map/all_gather | solution.py:130
  325.0 265.5 %all-gather.26.cloned.1.call-start = ((), (), s32[]{:S(2)}) async-start(), calls=%async_computation.18 | async-start | bytes 7077888 | tf_op jit(solution)/shard_map/all_gather | solution.py:238
  325.7 405.6 %reduce-scatter.14.cloned.1.call-start = ((), (), s32[]{:S(2)}) async-start(), calls=%async_computation.19 | async-start | bytes 14155776 | tf_op jit(solution)/shard_map/reduce_scatter | solution.py:247
  590.5 20.8 %copy-start.39 = (bf16[1536,1120]{0,1:T(8,128)(2,1)S(1)}, bf16[1536,1120]{0,1:T(8,128)(2,1)}, u32[]{:S(2)}) copy-start(bf16[1536,1120]{0,1:T(8,128)(2,1)} %all-gather.20.cloned.1.call-done) | copy-start | bytes 10321924
  638.9 188.3 %reduce-scatter.12.cloned.1.call-start = ((), (), s32[]{:S(2)}) async-start(), calls=%async_computation.17 | async-start | bytes 14155776 | tf_op jit(solution)/shard_map/reduce_scatter | solution.py:207
  654.1 173.0 %copy-start.17 = (bf16[256,1536]{1,0:T(8,128)(2,1)S(1)}, bf16[256,1536]{1,0:T(8,128)(2,1)}, u32[]{:S(2)}) copy-start(bf16[256,1536]{1,0:T(8,128)(2,1)} %param.16) | copy-start | bytes 2359300
  654.1 291.5 %reduce-scatter.16.cloned.1.call-start = ((), (), s32[]{:S(2)}) async-start(), calls=%async_computation.20 | async-start | bytes 2359296 | tf_op jit(solution)/shard_map/reduce_scatter | solution.py:288
  836.1 15.5 slice-start.3
  874.3 85.7 %reduce-scatter.18.cloned.1.call-start = ((), (), s32[]{:S(2)}) async-start(), calls=%async_computation.21 | async-start | bytes 2359296 | tf_op jit(solution)/shard_map/reduce_scatter | solution.py:289
  893.7 190.4 %reduce-scatter.28.cloned.1.call-start = ((), (), s32[]{:S(2)}) async-start(), calls=%async_computation.26 | async-start | bytes 8601600 | tf_op jit(solution)/shard_map/reduce_scatter | solution.py:351
  906.7 301.0 %reduce-scatter.30.cloned.1.call-start = ((), (), s32[]{:S(2)}) async-start(), calls=%async_computation.27 | async-start | bytes 8601600 | tf_op jit(solution)/shard_map/reduce_scatter | solution.py:352
  919.6 411.7 %reduce-scatter.32.cloned.1.call-start = ((), (), s32[]{:S(2)}) async-start(), calls=%async_computation.28 | async-start | bytes 8601600 | tf_op jit(solution)/shard_map/reduce_scatter | solution.py:353
  932.3 503.1 %reduce-scatter.22.cloned.1.call-start = ((), (), s32[]{:S(2)}) async-start(), calls=%async_computation.23 | async-start | bytes 1622016 | tf_op jit(solution)/shard_map/reduce_scatter | solution.py:321
  967.3 570.8 %reduce-scatter.24.cloned.1.call-start = ((), (), s32[]{:S(2)}) async-start(), calls=%async_computation.24 | async-start | bytes 1622016 | tf_op jit(solution)/shard_map/reduce_scatter | solution.py:327
  975.5 704.1 %reduce-scatter.26.cloned.1.call-start = ((), (), s32[]{:S(2)}) async-start(), calls=%async_computation.25 | async-start | bytes 9732096 | tf_op jit(solution)/shard_map/reduce_scatter | solution.py:333
  984.6 836.4 %reduce-scatter.20.cloned.1.call-start = ((), (), s32[]{:S(2)}) async-start(), calls=%async_computation.22 | async-start | bytes 9732096 | tf_op jit(solution)/shard_map/reduce_scatter | solution.py:315
  990.8 52.5 %copy-start.37 = (f32[256]{0:T(256)S(1)}, f32[256]{0:T(256)}, u32[]{:S(2)}) copy-start(f32[256]{0:T(256)} %get-tuple-element.17) | copy-start | bytes 3076
  990.8 52.5 %copy-start.35 = (f32[256]{0:T(256)S(1)}, f32[256]{0:T(256)}, u32[]{:S(2)}) copy-start(f32[256]{0:T(256)} %copy-done.33) | copy-start | bytes 3076
  (34 other events, 195.4 us)
Sparse Core Ops, SparseCore 0:
  92.8 28.2 all-gather.13
  134.5 27.1 all-gather.15
  164.5 62.4 all-gather.27
  229.7 61.8 all-gather.29
  293.0 65.6 all-gather.19
  361.0 45.6 all-gather.17
  408.2 66.3 all-gather.21
  476.3 66.6 all-gather.23
  544.8 45.6 all-gather.25
  639.0 92.2 reduce-scatter.13
  734.8 92.2 reduce-scatter.11
  874.4 41.1 reduce-scatter.15
  918.8 41.1 reduce-scatter.17
  962.7 121.3 reduce-scatter.27
  1086.9 120.7 reduce-scatter.29
  1210.5 120.8 reduce-scatter.31
  1337.0 98.3 reduce-scatter.21
  1441.1 96.9 reduce-scatter.23
  1544.6 134.9 reduce-scatter.25
  1685.9 135.0 reduce-scatter.19
where the time goes:
time: 1840 us; the launch traced here: 1830 us
  waiting for transfers between devices  1330 us (72%)
  matrix products  206 us (11%)
  blocking collectives  165 us (9%)
  local copies, waits for them, and re-layouts  71.4 us (4%)
  other arithmetic  34.8 us (2%)
    reduce_scatter x1, waiting for transfers between devices, shards(): lax.psum_scatter(split_blocks(contract_rows(mixed, attended_grad), row_pa...  141 us
    reduce_scatter x1, waiting for transfers between devices, shards(): lax.psum_scatter(split_blocks(contract_rows(first_normed, query_base_grad...  141 us
    reduce_scatter x1, waiting for transfers between devices, shards(): lax.psum_scatter(down_grad, 'row', scatter_dimension=1, tiled=True)  124 us
    reduce_scatter x1, waiting for transfers between devices, shards(): lax.psum_scatter(up_grad, 'row', scatter_dimension=0, tiled=True)  124 us
    reduce_scatter x1, waiting for transfers between devices, shards(): lax.psum_scatter(split_blocks(contract_rows(first_normed, key_base_grad),...  104 us
    reduce_scatter x1, waiting for transfers between devices, shards(): lax.psum_scatter(split_blocks(contract_rows(first_normed, value_base_grad...  103 us
    reduce_scatter x1, waiting for transfers between devices, shards(): lax.psum_scatter(product(hidden, down_block), 'col', scatter_dimension=0,...  93.9 us
    unnamed x2, blocking collectives  89.5 us
  transfers between devices with their start and end apart: 20, of which 18 were waited for; matrix products, arithmetic and copies ran while one was open for 11% of the time, Pallas kernels for 0%

commit v1 on v0

v1 whole, which is shorter than its diff:
```python
import math

import jax
import jax.numpy as jnp
from jax import lax
from jax.sharding import PartitionSpec as P

HQ = 12
KVH = 2
HD = 128
MAXLEN = 1024

EPSILON = 1e-06
ROPE_BASE = 1000000.0
BF16 = jnp.bfloat16
F32 = jnp.float32


def seq_starts(slots, lengths):
    bounds = jnp.cumsum(lengths)
    picked = jnp.where(bounds[None, :] <= slots[:, None], lengths[None, :], 0)
    return jnp.sum(picked, axis=1)


def rope_tables(positions, head_dim):
    steps_up = jnp.arange(head_dim // 2, dtype=F32)
    freqs = jnp.exp(-math.log(ROPE_BASE) * (2.0 * steps_up / head_dim))
    angles = positions.astype(F32)[:, None] * freqs[None, :]
    angles = jnp.concatenate([angles, angles], axis=1)
    return (jnp.cos(angles)[:, None, :], jnp.sin(angles)[:, None, :])


def rotate_pairs(values, cosines, sines):
    half_dim = values.shape[-1] // 2
    turned = jnp.concatenate([-values[..., half_dim:], values[..., :half_dim]], axis=-1)
    return values * cosines + turned * sines


def rotate_back(grads_in, cosines, sines):
    half_dim = grads_in.shape[-1] // 2
    moved = grads_in * sines
    return grads_in * cosines + jnp.concatenate(
        [moved[..., half_dim:], -moved[..., :half_dim]], axis=-1
    )


def rms_scale(values):
    return lax.rsqrt(jnp.mean(values * values, axis=-1, keepdims=True) + EPSILON)


def dot_nn(left, right):
    return lax.dot_general(left, right, (((1,), (0,)), ((), ())), preferred_element_type=F32)


def dot_tn(left, right):
    return lax.dot_general(left, right, (((0,), (0,)), ((), ())), preferred_element_type=F32)


def dot_nt(left, right):
    return lax.dot_general(left, right, (((1,), (1,)), ((), ())), preferred_element_type=F32)


def rounded_wide(values):
    return lax.optimization_barrier(values.astype(BF16)).astype(F32)


def masked_scores(query_heads, keys_window, visible, score_scale):
    scores = jnp.einsum("tkgd,skd->kgts", query_heads, keys_window, preferred_element_type=F32)
    return jnp.where(visible, scores * score_scale, -jnp.inf)


def gather_row(block):
    return lax.all_gather(block, "row", axis=1, tiled=True)


def gather_col(block):
    return lax.all_gather(block, "col", axis=0, tiled=True)


def scatter_row(full):
    return lax.psum_scatter(full.astype(BF16), "row", scatter_dimension=1, tiled=True)


def scatter_col(full):
    return lax.psum_scatter(full.astype(BF16), "col", scatter_dimension=0, tiled=True)


def shards(
    hidden_in,
    out_grad,
    seq_lengths,
    norm1_gain,
    q_weight,
    q_bias,
    k_weight,
    k_bias,
    v_weight,
    v_bias,
    o_weight,
    norm2_gain,
    gate_weight,
    up_weight,
    down_weight,
):
    row_parts = lax.axis_size("row")
    col_parts = lax.axis_size("col")
    col_place = lax.axis_index("col")
    depth_own = q_weight.shape[0]
    depth = depth_own * row_parts
    q_own, k_own = q_weight.shape[1], k_weight.shape[1]
    smalls = (q_bias, k_bias, v_bias, norm1_gain, norm2_gain)
    small_sizes = [member.shape[0] for member in smalls]
    small_rows = 16
    packed_small = jnp.concatenate(smalls)
    packed_small = jnp.pad(packed_small, (0, small_rows * depth_own - packed_small.shape[0]))
    packed = jnp.concatenate(
        [
            q_weight.T,
            k_weight.T,
            v_weight.T,
            o_weight.T,
            packed_small.reshape(small_rows, depth_own),
        ],
        axis=0,
    )
    pack_rows = packed.shape[0]
    gathered = gather_col(gather_row(packed)).reshape(col_parts, pack_rows, depth)
    cuts = [0, q_own, q_own + k_own, q_own + 2 * k_own, 2 * q_own + 2 * k_own, pack_rows]
    query_t, key_t, value_t, output_t, small_t = (
        gathered[:, cuts[i] : cuts[i + 1], :] for i in range(5)
    )
    query_t = query_t.reshape(-1, depth)
    key_t = key_t.reshape(-1, depth)
    value_t = value_t.reshape(-1, depth)
    output_t = output_t.reshape(-1, depth)
    small_flat = small_t.reshape(col_parts, small_rows, row_parts, depth_own)
    small_flat = small_flat.transpose(2, 0, 1, 3).reshape(row_parts * col_parts, -1)
    small_full, offset = [], 0
    for size in small_sizes:
        small_full.append(small_flat[:, offset : offset + size].reshape(-1))
        offset += size
    query_offset, key_offset, value_offset, first_gain, second_gain = small_full

    gate_t = gather_row(gate_weight.T)
    up_t = gather_row(up_weight.T)
    down_block = gather_row(down_weight)

    own_rows = hidden_in.shape[0]
    row_tokens = own_rows * col_parts
    lengths = seq_lengths[0]
    query_slots = col_place * own_rows + jnp.arange(own_rows, dtype=jnp.int32)
    query_starts = seq_starts(query_slots, lengths)
    cosines, sines = rope_tables(query_slots - query_starts, HD)
    group_size = HQ // KVH
    score_scale = 1.0 / math.sqrt(HD)
    inputs_wide = hidden_in.astype(F32)
    first_rms = rms_scale(inputs_wide)
    first_unit = inputs_wide * first_rms
    first_normed = (first_unit * first_gain.astype(F32)).astype(BF16)
    query_base = dot_nt(first_normed, query_t) + query_offset.astype(F32)
    key_base = dot_nt(first_normed, key_t) + key_offset.astype(F32)
    value_own = (dot_nt(first_normed, value_t) + value_offset.astype(F32)).astype(BF16)
    queries = rotate_pairs(query_base.reshape(own_rows, HQ, HD), cosines, sines).astype(BF16)
    keys_own = rotate_pairs(key_base.reshape(own_rows, KVH, HD), cosines, sines).astype(BF16)
    both_all = gather_col(
        jnp.concatenate([keys_own.reshape(own_rows, KVH * HD), value_own], axis=1)
    )
    window = min(own_rows + MAXLEN, row_tokens)
    window_start = jnp.clip(col_place * own_rows - MAXLEN, 0, row_tokens - window)
    key_slots = window_start + jnp.arange(window, dtype=jnp.int32)
    key_starts = seq_starts(key_slots, lengths)
    visible = (query_starts[:, None] == key_starts[None, :]) & (
        key_slots[None, :] <= query_slots[:, None]
    )
    both_window = lax.dynamic_slice_in_dim(both_all, window_start, window, 0)
    keys_window = both_window[:, : KVH * HD].reshape(window, KVH, HD)
    values_window = both_window[:, KVH * HD :].reshape(window, KVH, HD)
    query_heads = queries.reshape(own_rows, KVH, group_size, HD)
    scores = masked_scores(query_heads, keys_window, visible, score_scale)
    peak = jnp.max(scores, axis=-1, keepdims=True)
    expanded = jnp.exp(scores - peak)
    totals = jnp.sum(expanded, axis=-1, keepdims=True)
    probs = expanded / totals
    log_total = peak + jnp.log(totals)
    mixed = jnp.einsum(
        "kgts,skd->tkgd", probs.astype(BF16), values_window, preferred_element_type=F32
    )
    mixed = mixed.reshape(own_rows, HQ * HD).astype(BF16)
    residual = inputs_wide + dot_nt(mixed, output_t)
    second_rms = rms_scale(residual)
    second_unit = residual * second_rms
    second_normed = (second_unit * second_gain.astype(F32)).astype(BF16)
    normed_rows = gather_col(second_normed)
    out_rows = gather_col(out_grad)
    gate_act = dot_nt(normed_rows, gate_t)
    up_act = dot_nt(normed_rows, up_t)
    sigmoid_gate = jax.nn.sigmoid(gate_act)
    silu_gate = gate_act * sigmoid_gate
    hidden = (silu_gate * up_act).astype(BF16)
    down_grad = dot_tn(hidden, out_rows)
    hidden_grad = dot_nt(out_rows, down_block)
    up_grad_act = (hidden_grad * silu_gate).astype(BF16)
    gate_grad_act = (
        hidden_grad * up_act * sigmoid_gate * (1.0 + gate_act * (1.0 - sigmoid_gate))
    ).astype(BF16)
    normed_grad = scatter_col(dot_nn(gate_grad_act, gate_t) + dot_nn(up_grad_act, up_t)).astype(
        F32
    )
    branch_out = scatter_col(dot_nn(hidden, down_block)).astype(F32)
    layer_out = residual + branch_out
    gate_grad_t = dot_tn(gate_grad_act, normed_rows)
    up_grad_t = dot_tn(up_grad_act, normed_rows)
    second_gain_grad = jnp.sum(normed_grad * second_unit, axis=0)
    unit_grad = normed_grad * second_gain.astype(F32)
    residual_grad = out_grad.astype(F32) + second_rms * (
        unit_grad - second_unit * jnp.mean(unit_grad * second_unit, axis=-1, keepdims=True)
    )
    attended_grad = residual_grad.astype(BF16)
    mixed_grad = dot_nn(attended_grad, output_t).astype(BF16)
    grad_heads = mixed_grad.reshape(own_rows, KVH, group_size, HD)
    scores = masked_scores(query_heads, keys_window, visible, score_scale)
    probs = jnp.exp(scores - log_total)
    prob_grad = jnp.einsum(
        "tkgd,skd->kgts", grad_heads, values_window, preferred_element_type=F32
    )
    value_part = jnp.einsum(
        "kgts,tkgd->skd", probs.astype(BF16), grad_heads, preferred_element_type=F32
    )
    score_grad = (
        probs * (prob_grad - jnp.sum(probs * prob_grad, axis=-1, keepdims=True))
    ).astype(BF16)
    query_grad = (
        jnp.einsum("kgts,skd->tkgd", score_grad, keys_window, preferred_element_type=F32)
        * score_scale
    )
    key_part = (
        jnp.einsum("kgts,tkgd->skd", score_grad, query_heads, preferred_element_type=F32)
        * score_scale
    )
    both_part = jnp.concatenate(
        [key_part.reshape(window, KVH * HD), value_part.reshape(window, KVH * HD)], axis=1
    ).astype(BF16)
    both_rows = lax.dynamic_update_slice_in_dim(
        jnp.zeros((row_tokens, 2 * KVH * HD), BF16), both_part, window_start, 0
    )
    both_grad = scatter_col(both_rows).astype(F32)
    key_grad, value_grad = both_grad[:, : KVH * HD], both_grad[:, KVH * HD :]
    query_wide = rounded_wide(query_grad.reshape(own_rows, HQ, HD))
    query_base_grad = (
        rotate_back(query_wide, cosines, sines).reshape(own_rows, HQ * HD).astype(BF16)
    )
    key_wide = rounded_wide(key_grad.reshape(own_rows, KVH, HD))
    key_base_grad = (
        rotate_back(key_wide, cosines, sines).reshape(own_rows, KVH * HD).astype(BF16)
    )
    value_base_grad = value_grad.astype(BF16)
    query_b_grad = jnp.sum(query_base_grad.astype(F32), axis=0)
    key_b_grad = jnp.sum(key_base_grad.astype(F32), axis=0)
    value_b_grad = jnp.sum(value_base_grad.astype(F32), axis=0)
    first_normed_grad = (
        dot_nn(query_base_grad, query_t)
        + dot_nn(key_base_grad, key_t)
        + dot_nn(value_base_grad, value_t)
    )
    first_gain_grad = jnp.sum(first_normed_grad * first_unit, axis=0)
    first_unit_grad = first_normed_grad * first_gain.astype(F32)
    input_grad = residual_grad + first_rms * (
        first_unit_grad
        - first_unit * jnp.mean(first_unit_grad * first_unit, axis=-1, keepdims=True)
    )
    small_grads = (query_b_grad, key_b_grad, value_b_grad, first_gain_grad, second_gain_grad)
    small_flat = jnp.concatenate(
        [member.reshape(row_parts * col_parts, -1) for member in small_grads], axis=1
    )
    small_flat = jnp.pad(
        small_flat, ((0, 0), (0, small_rows * depth_own - small_flat.shape[1]))
    ).reshape(row_parts, col_parts, small_rows, depth_own)
    small_flat = small_flat.transpose(1, 2, 0, 3).reshape(col_parts, small_rows, depth)
    packed_grads = jnp.concatenate(
        [
            dot_tn(query_base_grad, first_normed).astype(BF16).reshape(col_parts, q_own, depth),
            dot_tn(key_base_grad, first_normed).astype(BF16).reshape(col_parts, k_own, depth),
            dot_tn(value_base_grad, first_normed).astype(BF16).reshape(col_parts, k_own, depth),
            dot_tn(attended_grad, mixed).astype(BF16).reshape(col_parts, q_own, depth),
            small_flat.astype(BF16),
        ],
        axis=1,
    ).reshape(col_parts * pack_rows, depth)
    packed_out = scatter_row(scatter_col(packed_grads)).astype(F32)
    query_w_out, key_w_out, value_w_out, output_w_out, small_out = (
        packed_out[cuts[i] : cuts[i + 1]] for i in range(5)
    )
    small_out = small_out.reshape(-1)
    small_list, offset = [], 0
    for size in small_sizes:
        small_list.append(small_out[offset : offset + size])
        offset += size
    return (
        layer_out,
        input_grad,
        small_list[3],
        query_w_out.T,
        small_list[0],
        key_w_out.T,
        small_list[1],
        value_w_out.T,
        small_list[2],
        output_w_out.T,
        small_list[4],
        scatter_row(gate_grad_t).astype(F32).T,
        scatter_row(up_grad_t).astype(F32).T,
        scatter_row(down_grad).astype(F32),
    )


def solution(mesh):
    in_specs = (
        P(("row", "col"), None),
        P(("row", "col"), None),
        P("row", None),
        P(("row", "col")),
        P("row", "col"),
        P(("row", "col")),
        P("row", "col"),
        P(("row", "col")),
        P("row", "col"),
        P(("row", "col")),
        P("row", "col"),
        P(("row", "col")),
        P("row", "col"),
        P("row", "col"),
        P("col", "row"),
    )
    out_specs = (
        P(("row", "col"), None),
        P(("row", "col"), None),
        P(("row", "col")),
        P("row", "col"),
        P(("row", "col")),
        P("row", "col"),
        P(("row", "col")),
        P("row", "col"),
        P(("row", "col")),
        P("row", "col"),
        P(("row", "col")),
        P("row", "col"),
        P("row", "col"),
        P("col", "row"),
    )
    return jax.shard_map(shards, mesh=mesh, in_specs=in_specs, out_specs=out_specs, check_vma=False)
```

time: 1840 us -> 1090 us (0.59)
  waiting for transfers between devices: 1330 us -> 752 us
  blocking collectives: 165 us -> 0 us
  matrix products: 206 us -> 186 us
    reduce_scatter x11 -> x4, waiting for transfers between devices: 955 us -> 167 us  [scatter_col(): lax.psum_scatter(full.astype(BF16), 'col', scatter_dimension=0, tiled=True)]
    unnamed x20, waiting for transfers between devices: 4.04 us -> 230 us
    unnamed x2 -> x0, blocking collectives: 89.5 us -> none
    all_gather x2 -> x0, blocking collectives: 75.4 us -> none  [the longest x1 38.9 us: shards(): lax.all_gather(k_weight[None], ('row', 'col'), axis=0, tiled=True)]
    all_gather x9 -> x8, waiting for transfers between devices: 375 us -> 355 us  [the longest x4 184 us: gather_row(): return lax.all_gather(block, 'row', axis=1, tiled=True)]
    dot_general x23, matrix products: 178 us -> 158 us  [the longest x7 54 us: dot_nt(): lax.dot_general(left, right, (((1,), (1,)), ((), ())), preferred_element_...]
    unnamed x115 -> x116, local copies, waits for them, and re-layouts: 29.3 us -> 46.4 us
  transfers between devices with their start and end apart: 20 -> 16, of which waited for: 18 -> 16; matrix products, arithmetic and copies ran while one was open for 11% -> 16% of each run, Pallas kernels for 0% -> 0%
where the time goes in v1:
time: 1090 us; the launch traced here: 1080 us
  waiting for transfers between devices  752 us (69%)
  matrix products  186 us (17%)
  local copies, waits for them, and re-layouts  88.3 us (8%)
  other arithmetic  37.7 us (3%)
  between operations  15.1 us (1%)
    unnamed x20, waiting for transfers between devices  230 us
    all_gather x4, waiting for transfers between devices, gather_row(): return lax.all_gather(block, 'row', axis=1, tiled=True)  184 us
    all_gather x4, waiting for transfers between devices, gather_col(): return lax.all_gather(block, 'col', axis=0, tiled=True)  171 us
    reduce_scatter x4, waiting for transfers between devices, scatter_col(): lax.psum_scatter(full.astype(BF16), 'col', scatter_dimension=0, tiled=True)  167 us
    dot_general x7, matrix products, dot_nt(): lax.dot_general(left, right, (((1,), (1,)), ((), ())), preferred_element_...  54 us
    dot_general x7, matrix products, dot_nn(): lax.dot_general(left, right, (((1,), (0,)), ((), ())), preferred_element_...  49.1 us
    unnamed x116, local copies, waits for them, and re-layouts  46.4 us
    dot_general x7, matrix products, dot_tn(): lax.dot_general(left, right, (((0,), (0,)), ((), ())), preferred_element_...  44.3 us
  transfers between devices with their start and end apart: 16, of which 16 were waited for; matrix products, arithmetic and copies ran while one was open for 16% of the time, Pallas kernels for 0%

profile of v1, /device:TPU:8, one launch (start us, length us, event | category | flops | bytes accessed | tf_op | source)
XLA Modules:
  0.0 1080.9 jit_solution(11490301202018568363)
XLA Ops:
  14.9 35.4 %all-gather.9.cloned.1.call-done = bf16[464,1536]{1,0:T(8,128)(2,1)} async-done(((bf16[464,384]{1,0:T(8,128)(2,1)}), bf16[464,1536]{1,0:T(8,128)(2,1)}) %all-gather.9.cloned.1.call-update) | async-done | bytes 1425424 | tf_op jit(solution)/shard_map/all_gather | solution.py:73
  52.9 65.7 %all-gather.11.cloned.1.call-done = bf16[3712,1536]{1,0:T(8,128)(2,1)} async-done(((bf16[464,1536]{1,0:T(8,128)(2,1)}), bf16[3712,1536]{1,0:T(8,128)(2,1)}) %all-gather.11.cloned.1.call-update) | async-done | bytes 11403280 | tf_op jit(solution)/shard_map/all_gather | solution.py:77
  125.6 8.3 fusion.60
  142.3 9.7 all-gather.13.cloned.1.call-done
  154.0 7.1 fusion.66
  161.1 8.0 fusion.3
  169.2 7.5 fusion.39
  181.7 38.2 %all-gather.17.cloned.1.call-done = bf16[1120,1536]{1,0:T(8,128)(2,1)} async-done(((bf16[1120,384]{1,0:T(8,128)(2,1)}), bf16[1120,1536]{1,0:T(8,128)(2,1)}) %all-gather.17.cloned.1.call-update) | async-done | bytes 3440656 | tf_op jit(solution)/shard_map/all_gather | solution.py:73
  219.9 48.0 %all-gather.15.cloned.1.call-done = bf16[2048,1536]{1,0:T(8,128)(2,1)} async-done(((bf16[256,1536]{1,0:T(8,128)(2,1)}), bf16[2048,1536]{1,0:T(8,128)(2,1)}) %all-gather.15.cloned.1.call-update) | async-done | bytes 6291472 | tf_op jit(solution)/shard_map/all_gather | solution.py:77
  267.9 12.9 %fusion.67 = f32[2048,1120]{0,1:T(8,128)} fusion(bf16[2048,1536]{1,0:T(8,128)(2,1)} %all-gather.15.cloned.1.call-done, bf16[1120,1536]{1,0:T(8,128)(2,1)} %all-gather.17.cloned.1.call-done), kind=kOutput, calls=%fused_computation.142 | convolution fusion | flops 7046430720 | bytes 18907136 | tf_op jit(solution)/shard_map/dot_general | solution.py:60
  280.8 55.0 %all-gather.19.cloned.1.call-done = bf16[1120,1536]{1,0:T(8,128)(2,1)} async-done(((bf16[1120,384]{1,0:T(8,128)(2,1)}), bf16[1120,1536]{1,0:T(8,128)(2,1)}) %all-gather.19.cloned.1.call-update) | async-done | bytes 3440656 | tf_op jit(solution)/shard_map/all_gather | solution.py:73
  335.7 12.9 %fusion.68 = f32[2048,1120]{0,1:T(8,128)} fusion(bf16[2048,1536]{1,0:T(8,128)(2,1)} %all-gather.15.cloned.1.call-done, bf16[1120,1536]{1,0:T(8,128)(2,1)} %all-gather.19.cloned.1.call-done), kind=kOutput, calls=%fused_computation.143 | convolution fusion | flops 7046430720 | bytes 18907136 | tf_op jit(solution)/shard_map/dot_general | solution.py:60
  348.7 55.3 %all-gather.21.cloned.1.call-done = bf16[1120,1536]{1,0:T(8,128)(2,1)} async-done(((bf16[1120,384]{1,0:T(8,128)(2,1)}), bf16[1120,1536]{1,0:T(8,128)(2,1)}) %all-gather.21.cloned.1.call-update) | async-done | bytes 3440656 | tf_op jit(solution)/shard_map/all_gather | solution.py:73
  404.0 47.5 %all-gather.23.cloned.1.call-done = bf16[2048,1536]{1,0:T(8,128)(2,1)} async-done(((bf16[256,1536]{1,0:T(8,128)(2,1)}), bf16[2048,1536]{1,0:T(8,128)(2,1)}) %all-gather.23.cloned.1.call-update) | async-done | bytes 6291472 | tf_op jit(solution)/shard_map/all_gather | solution.py:77
  451.6 20.7 %multiply_convert_fusion = (bf16[2048,1120]{0,1:T(8,128)(2,1)}, bf16[2048,1120]{0,1:T(8,128)(2,1)}, bf16[2048,1120]{0,1:T(8,128)(2,1)}) fusion(f32[2048,1120]{0,1:T(8,128)} %fusion.67, f32[2048,1120]{0,1:T(8,128)} %fusion.68, bf16[2048,1536]{1,0:T(8,128)(2,1)} %all-gather.23.cloned.1.call-done, bf16[1120,1536]{1,0:T(8,128)(2,1)} %all-gather.21.cloned.1.call-done), kind=kOutput, calls=%fused_computation.12 | convolution fusion | flops 7080837120 | bytes 41844736 | tf_op jit(solution)/shard_map/dot_general | solution.py:60
  472.3 13.6 %fusion.69 = f32[2048,1536]{1,0:T(8,128)} fusion(bf16[2048,1120]{0,1:T(8,128)(2,1)} %get-tuple-element.23, bf16[1120,1536]{1,0:T(8,128)(2,1)S(1)} %copy-done.38), kind=kOutput, calls=%fused_computation.144 | convolution fusion | flops 7046430720 | bytes 20611072 | tf_op jit(solution)/shard_map/dot_general | solution.py:52
  485.9 12.6 %add_convert_fusion = bf16[2048,1536]{1,0:T(8,128)(2,1)} fusion(f32[2048,1536]{1,0:T(8,128)} %fusion.69, bf16[2048,1120]{0,1:T(8,128)(2,1)S(1)} %copy-done.40, bf16[1120,1536]{1,0:T(8,128)(2,1)S(1)} %copy-done.39), kind=kOutput, calls=%fused_computation.10 | convolution fusion | flops 7052722176 | bytes 26902528 | tf_op jit(solution)/shard_map/dot_general | solution.py:52
  498.6 13.3 %convolution_convert_fusion = bf16[2048,1536]{1,0:T(8,128)(2,1)} fusion(bf16[2048,1120]{0,1:T(8,128)(2,1)} %get-tuple-element.24, bf16[1120,1536]{1,0:T(8,128)(2,1)} %all-gather.21.cloned.1.call-done), kind=kOutput, calls=%fused_computation.20 | convolution fusion | flops 7049576448 | bytes 14319616 | tf_op jit(solution)/shard_map/dot_general | solution.py:52
  512.2 48.2 %reduce-scatter.19.cloned.1.call-done = bf16[256,1536]{1,0:T(8,128)(2,1)} async-done(((bf16[2048,1536]{1,0:T(8,128)(2,1)}), bf16[256,1536]{1,0:T(8,128)(2,1)}) %reduce-scatter.19.cloned.1.call-update) | async-done | bytes 786448 | tf_op jit(solution)/shard_map/reduce_scatter | solution.py:85
  562.2 63.3 %reduce-scatter.17.cloned.1.call-done = bf16[256,1536]{1,0:T(8,128)(2,1)} async-done(((bf16[2048,1536]{1,0:T(8,128)(2,1)}), bf16[256,1536]{1,0:T(8,128)(2,1)}) %reduce-scatter.17.cloned.1.call-update) | async-done | bytes 786448 | tf_op jit(solution)/shard_map/reduce_scatter | solution.py:85
  636.8 14.3 %fusion = (f32[2,6,256]{2,1,0:T(8,128)S(1)}, f32[2,1280,256,6]{2,1,3,0:T(8,128)}) fusion(f32[2,6,256,1280]{2,3,1,0:T(8,128)} %get-tuple-element.60, f32[2,6,256]{2,1,0:T(8,128)S(1)} %log_add_fusion, bf16[1280,2,128,1]{0,2,3,1:T(8,128)(2,1)} %bitcast.207, bf16[256,2,6,128]{0,3,2,1:T(8,128)(2,1)} %bitcast.181), kind=kOutput, calls=%fused_computation.2 | convolution fusion | flops 1018426368 | bytes 32923648 | tf_op jit(solution)/shard_map/tkgd,skd->kgts/dot_general | solution.py:223
  654.2 7.5 fusion.2
  666.2 15.3 %dynamic_update_slice.3 = bf16[2048,512]{0,1:T(8,128)(2,1)S(1)} dynamic-update-slice(bf16[2048,512]{0,1:T(8,128)(2,1)S(1)} %broadcast_in_dim.45, bf16[1280,512]{0,1:T(8,128)(2,1)} %pad_maximum_fusion, s32[]{:T(128)S(6)} %min.4, s32[]{:T(128)} %constant.42.clone.1) | dynamic-update-slice | bytes 2621444 | tf_op jit(solution)/shard_map/dynamic_update_slice | solution.py:243
  700.0 24.2 %reduce-scatter.21.cloned.1.call-done = bf16[256,512]{0,1:T(8,128)(2,1)} async-done(((bf16[2048,512]{0,1:T(8,128)(2,1)}), bf16[256,512]{0,1:T(8,128)(2,1)}) %reduce-scatter.21.cloned.1.call-update) | async-done | bytes 262160 | tf_op jit(solution)/shard_map/reduce_scatter | solution.py:85
  740.6 12.0 %convolution_convert_fusion.2 = bf16[1120,1536]{1,0:T(8,128)(2,1)} fusion(bf16[2048,1120]{0,1:T(8,128)(2,1)} %get-tuple-element.22, bf16[2048,1536]{1,0:T(8,128)(2,1)} %all-gather.15.cloned.1.call-done), kind=kOutput, calls=%fused_computation.22 | convolution fusion | flops 7048151040 | bytes 14319616 | tf_op jit(solution)/shard_map/dot_general | solution.py:56
  759.1 12.4 %convolution_convert_fusion.3 = bf16[1120,1536]{1,0:T(8,128)(2,1)} fusion(bf16[2048,1120]{0,1:T(8,128)(2,1)} %get-tuple-element.23, bf16[2048,1536]{1,0:T(8,128)(2,1)} %all-gather.15.cloned.1.call-done), kind=kOutput, calls=%fused_computation.23 | convolution fusion | flops 7048151040 | bytes 14319616 | tf_op jit(solution)/shard_map/dot_general | solution.py:56
  777.3 12.3 %convolution_convert_fusion.1 = bf16[1120,1536]{1,0:T(8,128)(2,1)} fusion(bf16[2048,1120]{0,1:T(8,128)(2,1)} %get-tuple-element.24, bf16[2048,1536]{1,0:T(8,128)(2,1)} %all-gather.23.cloned.1.call-done), kind=kOutput, calls=%fused_computation.21 | convolution fusion | flops 7048151040 | bytes 14319616 | tf_op jit(solution)/shard_map/dot_general | solution.py:56
  795.3 31.8 %reduce-scatter.23.cloned.1.call-done = bf16[464,1536]{1,0:T(8,128)(2,1)} async-done(((bf16[3712,1536]{1,0:T(8,128)(2,1)}), bf16[464,1536]{1,0:T(8,128)(2,1)}) %reduce-scatter.23.cloned.1.call-update) | async-done | bytes 1425424 | tf_op jit(solution)/shard_map/reduce_scatter | solution.py:85
  829.6 65.9 %reduce-scatter.29.cloned.1.call-done = bf16[384,1120]{1,0:T(8,128)(2,1)} async-done(((bf16[1536,1120]{1,0:T(8,128)(2,1)}), bf16[384,1120]{1,0:T(8,128)(2,1)}) %reduce-scatter.29.cloned.1.call-update) | async-done | bytes 860176
  897.9 66.5 %reduce-scatter.27.cloned.1.call-done = bf16[384,1120]{1,0:T(8,128)(2,1)} async-done(((bf16[1536,1120]{1,0:T(8,128)(2,1)}), bf16[384,1120]{1,0:T(8,128)(2,1)}) %reduce-scatter.27.cloned.1.call-update) | async-done | bytes 860176
  966.6 66.7 %reduce-scatter.31.cloned.1.call-done = bf16[384,1120]{1,0:T(8,128)(2,1)} async-done(((bf16[1536,1120]{1,0:T(8,128)(2,1)}), bf16[384,1120]{1,0:T(8,128)(2,1)}) %reduce-scatter.31.cloned.1.call-update) | async-done | bytes 860176
  1042.3 27.8 %reduce-scatter.25.cloned.1.call-done = bf16[384,464]{1,0:T(8,128)(2,1)} async-done(((bf16[1536,464]{1,0:T(8,128)(2,1)}), bf16[384,464]{1,0:T(8,128)(2,1)}) %reduce-scatter.25.cloned.1.call-update) | async-done | bytes 356368
  (240 shorter events, 125.7 us)
Async XLA Ops:
  7.2 45.5 %copy-start.3 = (bf16[256,1536]{1,0:T(8,128)(2,1)S(1)}, bf16[256,1536]{1,0:T(8,128)(2,1)}, u32[]{:S(2)}) copy-start(bf16[256,1536]{1,0:T(8,128)(2,1)} %param.15) | copy-start | bytes 2359300
  7.2 43.2 %all-gather.9.cloned.1.call-start = ((), (), s32[]{:S(2)}) async-start(), calls=%async_computation.8 | async-start | bytes 1781760 | tf_op jit(solution)/shard_map/all_gather | solution.py:73
  14.9 103.7 %all-gather.11.cloned.1.call-start = ((), (), s32[]{:S(2)}) async-start(), calls=%async_computation.9 | async-start | bytes 12828672 | tf_op jit(solution)/shard_map/all_gather | solution.py:77
  50.4 101.6 %all-gather.13.cloned.1.call-start = ((), (), s32[]{:S(2)}) async-start(), calls=%async_computation.10 | async-start | bytes 2359296 | tf_op jit(solution)/shard_map/all_gather | solution.py:77
  52.6 69.7 %copy-start.15 = (f32[256,128]{0,1:T(8,128)}, f32[256,128]{0,1:T(8,128)S(1)}, u32[]{:S(2)}) copy-start(f32[256,128]{0,1:T(8,128)S(1)} %get-tuple-element.53) | copy-start | bytes 393220
  52.7 69.8 %copy-start.13 = (f32[256,128]{0,1:T(8,128)}, f32[256,128]{0,1:T(8,128)S(1)}, u32[]{:S(2)}) copy-start(f32[256,128]{0,1:T(8,128)S(1)} %get-tuple-element.52) | copy-start | bytes 393220
  52.9 81.0 %copy-start.31 = (f32[256]{0:T(256)}, f32[256]{0:T(256)S(1)}, u32[]{:S(2)}) copy-start(f32[256]{0:T(256)S(1)} %add_rsqrt_fusion.1) | copy-start | bytes 3076
  123.8 96.1 %all-gather.17.cloned.1.call-start = ((), (), s32[]{:S(2)}) async-start(), calls=%async_computation.12 | async-start | bytes 4300800 | tf_op jit(solution)/shard_map/all_gather | solution.py:73
  124.3 143.5 %all-gather.15.cloned.1.call-start = ((), (), s32[]{:S(2)}) async-start(), calls=%async_computation.11 | async-start | bytes 7077888 | tf_op jit(solution)/shard_map/all_gather | solution.py:77
  142.2 18.9 %copy-start.5 = (bf16[256,2,6,128]{0,3,2,1:T(8,128)(2,1)}, bf16[256,2,6,128]{0,3,2,1:T(8,128)(2,1)S(1)}, u32[]{:S(2)}) copy-start(bf16[256,2,6,128]{0,3,2,1:T(8,128)(2,1)S(1)} %fusion.38) | copy-start | bytes 2359300
  154.0 15.2 %copy-start.22 = (bf16[1280,256]{0,1:T(8,128)(2,1)}, bf16[1280,256]{0,1:T(8,128)(2,1)S(1)}, u32[]{:S(2)}) copy-start(bf16[1280,256]{0,1:T(8,128)(2,1)S(1)} %get-tuple-element.30) | copy-start | bytes 1966084
  161.1 15.5 %slice-start.6 = ((s8[4718592]{0:T(1024)(128)(4,1)}), s8[524288]{0:T(1024)(128)(4,1)S(1)}, s32[]{:S(2)}) async-start(s8[4718592]{0:T(1024)(128)(4,1)} %bitcast.195), calls=%async_computation.30 | async-start | bytes 1048576
  179.3 156.4 %all-gather.19.cloned.1.call-start = ((), (), s32[]{:S(2)}) async-start(), calls=%async_computation.13 | async-start | bytes 4300800 | tf_op jit(solution)/shard_map/all_gather | solution.py:73
  179.9 224.1 %all-gather.21.cloned.1.call-start = ((), (), s32[]{:S(2)}) async-start(), calls=%async_computation.14 | async-start | bytes 4300800 | tf_op jit(solution)/shard_map/all_gather | solution.py:73
  180.7 270.9 %all-gather.23.cloned.1.call-start = ((), (), s32[]{:S(2)}) async-start(), calls=%async_computation.16 | async-start | bytes 7077888 | tf_op jit(solution)/shard_map/all_gather | solution.py:77
  181.4 379.1 %reduce-scatter.19.cloned.1.call-start = ((), (), s32[]{:S(2)}) async-start(), calls=%async_computation.17 | async-start | bytes 7077888 | tf_op jit(solution)/shard_map/reduce_scatter | solution.py:85
  451.6 20.7 %copy-start.38 = (bf16[1120,1536]{1,0:T(8,128)(2,1)S(1)}, bf16[1120,1536]{1,0:T(8,128)(2,1)}, u32[]{:S(2)}) copy-start(bf16[1120,1536]{1,0:T(8,128)(2,1)} %all-gather.17.cloned.1.call-done) | copy-start | bytes 10321924
  472.3 13.6 %copy-start.39 = (bf16[1120,1536]{1,0:T(8,128)(2,1)S(1)}, bf16[1120,1536]{1,0:T(8,128)(2,1)}, u32[]{:S(2)}) copy-start(bf16[1120,1536]{1,0:T(8,128)(2,1)} %all-gather.19.cloned.1.call-done) | copy-start | bytes 10321924
  498.6 126.9 %reduce-scatter.17.cloned.1.call-start = ((), (), s32[]{:S(2)}) async-start(), calls=%async_computation.15 | async-start | bytes 7077888 | tf_op jit(solution)/shard_map/reduce_scatter | solution.py:85
  512.0 113.5 %copy-start.17 = (bf16[256,1536]{1,0:T(8,128)(2,1)S(1)}, bf16[256,1536]{1,0:T(8,128)(2,1)}, u32[]{:S(2)}) copy-start(bf16[256,1536]{1,0:T(8,128)(2,1)} %param.16) | copy-start | bytes 2359300
  512.0 212.2 %reduce-scatter.21.cloned.1.call-start = ((), (), s32[]{:S(2)}) async-start(), calls=%async_computation.18 | async-start | bytes 2359296 | tf_op jit(solution)/shard_map/reduce_scatter | solution.py:85
  629.7 21.4 %slice-start = ((s8[15728640]{0:T(1024)(128)(4,1)}), s8[3145728]{0:T(1024)(128)(4,1)S(1)}, s32[]{:S(2)}) async-start(s8[15728640]{0:T(1024)(128)(4,1)} %bitcast.168), calls=%async_computation.24 | async-start | bytes 6291456
  636.8 14.3 %slice-start.1 = ((s8[15728640]{0:T(1024)(128)(4,1)}), s8[4194304]{0:T(1024)(128)(4,1)S(1)}, s32[]{:S(2)}) async-start(s8[15728640]{0:T(1024)(128)(4,1)} %bitcast.168), calls=%async_computation.25 | async-start | bytes 8388608
  636.8 14.3 %slice-start.2 = ((s8[15728640]{0:T(1024)(128)(4,1)}), s8[4194304]{0:T(1024)(128)(4,1)S(1)}, s32[]{:S(2)}) async-start(s8[15728640]{0:T(1024)(128)(4,1)} %bitcast.168), calls=%async_computation.26 | async-start | bytes 8388608
  636.8 14.3 %slice-start.3 = ((s8[15728640]{0:T(1024)(128)(4,1)}), s8[4194304]{0:T(1024)(128)(4,1)S(1)}, s32[]{:S(2)}) async-start(s8[15728640]{0:T(1024)(128)(4,1)} %bitcast.168), calls=%async_computation.27 | async-start | bytes 8388608
  636.8 14.3 %copy-start.8 = (bf16[256,1536]{0,1:T(8,128)(2,1)S(1)}, bf16[256,1536]{0,1:T(8,128)(2,1)}, u32[]{:S(2)}) copy-start(bf16[256,1536]{0,1:T(8,128)(2,1)} %copy.89) | copy-start | bytes 2359300
  666.0 17.2 %copy-start.11 = (bf16[1280,256]{0,1:T(8,128)(2,1)S(1)}, bf16[1280,256]{0,1:T(8,128)(2,1)}, u32[]{:S(2)}) copy-start(bf16[1280,256]{0,1:T(8,128)(2,1)} %copy-done.10) | copy-start | bytes 1966084
  682.9 144.2 %reduce-scatter.23.cloned.1.call-start = ((), (), s32[]{:S(2)}) async-start(), calls=%async_computation.19 | async-start | bytes 12828672 | tf_op jit(solution)/shard_map/reduce_scatter | solution.py:85
  740.6 155.0 %reduce-scatter.29.cloned.1.call-start = ((), (), s32[]{:S(2)}) async-start(), calls=%async_computation.22 | async-start | bytes 4423680
  758.8 205.6 %reduce-scatter.27.cloned.1.call-start = ((), (), s32[]{:S(2)}) async-start(), calls=%async_computation.21 | async-start | bytes 4423680
  777.2 256.1 %reduce-scatter.31.cloned.1.call-start = ((), (), s32[]{:S(2)}) async-start(), calls=%async_computation.23 | async-start | bytes 4423680
  795.3 274.9 %reduce-scatter.25.cloned.1.call-start = ((), (), s32[]{:S(2)}) async-start(), calls=%async_computation.20 | async-start | bytes 1966080
  (33 other events, 125.4 us)
Sparse Core Ops, SparseCore 0:
  15.0 35.2 all-gather.8
  52.2 66.3 all-gather.10
  123.9 28.0 all-gather.12
  153.5 66.3 all-gather.16
  222.2 45.6 all-gather.14
  269.3 66.3 all-gather.18
  337.3 66.6 all-gather.20
  405.9 45.6 all-gather.22
  498.7 61.7 reduce-scatter.18
  563.7 61.7 reduce-scatter.16
  683.0 41.1 reduce-scatter.20
  740.7 86.2 reduce-scatter.22
  829.4 66.1 reduce-scatter.28
  897.7 66.6 reduce-scatter.26
  966.6 66.6 reduce-scatter.30
  1035.5 34.6 reduce-scatter.24

commit v2 on v1

--- a/solution.py
+++ b/solution.py
@@ -1,8 +1,11 @@
+import functools
 import math
 
 import jax
 import jax.numpy as jnp
 from jax import lax
+from jax.experimental import pallas as pl
+from jax.experimental.pallas import tpu as pltpu
 from jax.sharding import PartitionSpec as P
 
 HQ = 12
@@ -14,6 +17,7 @@
 ROPE_BASE = 1000000.0
 BF16 = jnp.bfloat16
 F32 = jnp.float32
+MESH = pl.DeviceIdType.MESH
 
 
 def seq_starts(slots, lengths):
@@ -69,20 +73,301 @@
     return jnp.where(visible, scores * score_scale, -jnp.inf)
 
 
+def plane_places():
+    me = lax.axis_index("col")
+    chip, core = me // 2, me % 2
+    low, high = chip % 2, chip // 2
+    beside = high * 2 + (1 - low)
+    above = (1 - high) * 2 + low
+    across = (1 - high) * 2 + (1 - low)
+    return chip, beside, above, across, core
+
+
+def greet(peers):
+    barrier = pltpu.get_barrier_semaphore()
+    for peer in peers:
+        pl.semaphore_signal(barrier, inc=1, device_id={"col": peer}, device_id_type=MESH)
+    pl.semaphore_wait(barrier, len(peers))
+
+
+def plane_gather_kernel(count, *refs):
+    ins, outs = refs[:count], refs[count : 2 * count]
+    send_sem, recv_sem, own_sem = refs[2 * count :]
+    chip, beside, above, across, core = plane_places()
+    mine = chip * 2 + core
+    partner = chip * 2 + 1 - core
+    to_x, to_y = beside * 2 + core, above * 2 + core
+    greet((partner, to_x, to_y))
+
+    def view(i, slot, part):
+        size = ins[i].shape[1]
+        half = size // 2
+        if part is None:
+            return outs[i].at[:, pl.ds(pl.multiple_of(slot * size, size), size), :]
+        return outs[i].at[:, pl.ds(pl.multiple_of(slot * size + part * half, half), half), :]
+
+    def copies(k, slot, part, peer, own=False):
+        return [
+            pltpu.make_async_remote_copy(
+                src_ref=ins[i] if own else view(i, slot, part),
+                dst_ref=view(i, slot, part),
+                send_sem=send_sem.at[i, k],
+                recv_sem=recv_sem.at[i, k],
+                device_id={"col": peer},
+                device_id_type=MESH,
+            )
+            for i in range(count)
+        ]
+
+    def start(cs):
+        for c in cs:
+            c.start()
+
+    def wait_recv(cs):
+        for c in cs:
+            c.wait_recv()
+
+    sent = [
+        copies(1, mine, None, to_x, True),
+        copies(2, mine, None, to_y, True),
+        copies(0, mine, None, partner, True),
+    ]
+    for c in sent:
+        start(c)
+    own = [
+        pltpu.make_async_copy(ins[i], view(i, mine, None), own_sem.at[i]) for i in range(count)
+    ]
+    start(own)
+    other = 1 - core
+    wait_recv(copies(1, to_x, None, to_x))
+    more = [copies(3, to_x, 0, to_y), copies(5, to_x, None, partner)]
+    for c in more:
+        start(c)
+    sent += more
+    wait_recv(copies(2, to_y, None, to_y))
+    more = [copies(4, to_y, 1, to_x), copies(6, to_y, None, partner)]
+    for c in more:
+        start(c)
+    sent += more
+    far = across * 2 + core
+    wait_recv(copies(3, far, 0, to_y))
+    more = [copies(7, far, 0, partner)]
+    start(more[0])
+    sent += more
+    wait_recv(copies(4, far, 1, to_x))
+    more = [copies(8, far, 1, partner)]
+    start(more[0])
+    sent += more
+    wait_recv(copies(0, partner, None, partner))
+    wait_recv(copies(5, beside * 2 + other, None, partner))
+    wait_recv(copies(6, above * 2 + other, None, partner))
+    wait_recv(copies(7, across * 2 + other, 0, partner))
+    wait_recv(copies(8, across * 2 + other, 1, partner))
+    for cs in sent:
+        for c in cs:
+            c.wait_send()
+    for c in own:
+        c.wait()
+
+
+def plane_gather(shards, ident):
+    count = len(shards)
+    parts = lax.axis_size("col")
+    outs = [
+        jax.ShapeDtypeStruct((s.shape[0], s.shape[1] * parts, s.shape[2]), s.dtype)
+        for s in shards
+    ]
+    return pl.pallas_call(
+        functools.partial(plane_gather_kernel, count),
+        out_shape=outs,
+        in_specs=[pl.BlockSpec(memory_space=pl.ANY)] * count,
+        out_specs=[pl.BlockSpec(memory_space=pl.ANY)] * count,
+        scratch_shapes=[
+            pltpu.SemaphoreType.DMA((count, 9)),
+            pltpu.SemaphoreType.DMA((count, 9)),
+            pltpu.SemaphoreType.DMA((count,)),
+        ],
+        compiler_params=pltpu.CompilerParams(collective_id=ident, has_side_effects=True),
+        name="plane_gather",
+    )(*shards)
+
+
+def plane_scatter_kernel(count, *refs):
+    ins, outs = refs[:count], refs[count : 2 * count]
+    scratch = refs[2 * count :]
+    near, made, side, land = (scratch[i * count : (i + 1) * count] for i in range(4))
+    send_sem, recv_sem = scratch[4 * count :]
+    chip, beside, above, across, core = plane_places()
+    partner = chip * 2 + 1 - core
+    to_x, to_y = beside * 2 + core, above * 2 + core
+    greet((partner, to_x, to_y))
+    order = (across, beside, above, chip)
+
+    def rows(i, slot):
+        size = outs[i].shape[1]
+        return pl.ds(pl.multiple_of(slot * size, size), size)
+
+    def half(i, part):
+        size = outs[i].shape[1] // 2
+        return pl.ds(part * size, size)
+
+    def remote(i, k, src, dst, peer):
+        return pltpu.make_async_remote_copy(
+            src_ref=src,
+            dst_ref=dst,
+            send_sem=send_sem.at[i, k],
+            recv_sem=recv_sem.at[i, k],
+            device_id={"col": peer},
+            device_id_type=MESH,
+        )
+
+    def near_copy(i, j):
+        return remote(
+            i, j, ins[i].at[:, rows(i, order[j] * 2 + 1 - core), :], near[i].at[j], partner
+        )
+
+    def side_copy(i, part):
+        return remote(
+            i, 4 + part, made[i].at[0, :, half(i, part), :], side[i].at[part],
+            to_x if part == 0 else to_y,
+        )
+
+    def land_copy(i, which, part):
+        return remote(
+            i, 6 + which * 2 + part, made[i].at[1 + which, :, half(i, part), :],
+            land[i].at[which, :, half(i, part), :], to_x if which == 0 else to_y,
+        )
+
+    step = 16
+
+    def each(i, size, body):
+        def tile(t, _):
+            body(pl.multiple_of(t * step, step))
+            return 0
+
+        lax.fori_loop(0, size // step, tile, 0)
+
+    def combine(i, j):
+        size = outs[i].shape[1]
+        first = (order[j] * 2 + core) * size
+
+        def body(at):
+            for a in range(outs[i].shape[0]):
+                left = ins[i][a, pl.ds(pl.multiple_of(first + at, step), step), :].astype(F32)
+                right = near[i][j, a, pl.ds(at, step), :].astype(F32)
+                made[i][j, a, pl.ds(at, step), :] = (left + right).astype(BF16)
+
+        each(i, size, body)
+
+    def fold(i, which, part):
+        size = outs[i].shape[1] // 2
+
+        def body(at):
+            at2 = pl.multiple_of(part * size + at, step)
+            for a in range(outs[i].shape[0]):
+                left = made[i][1 + which, a, pl.ds(at2, step), :].astype(F32)
+                right = side[i][1 - which, a, pl.ds(at, step), :].astype(F32)
+                made[i][1 + which, a, pl.ds(at2, step), :] = (left + right).astype(BF16)
+
+        each(i, size, body)
+
+    every = range(count)
+    for j in range(4):
+        for i in every:
+            near_copy(i, j).start()
+    for i in every:
+        near_copy(i, 0).wait_recv()
+        combine(i, 0)
+        side_copy(i, 0).start()
+        side_copy(i, 1).start()
+    for i in every:
+        near_copy(i, 1).wait_recv()
+        combine(i, 1)
+        land_copy(i, 0, 0).start()
+    for i in every:
+        near_copy(i, 2).wait_recv()
+        combine(i, 2)
+        land_copy(i, 1, 1).start()
+    for i in every:
+        side_copy(i, 0).wait_recv()
+        fold(i, 1, 0)
+        land_copy(i, 1, 0).start()
+        side_copy(i, 1).wait_recv()
+        fold(i, 0, 1)
+        land_copy(i, 0, 1).start()
+    for i in every:
+        near_copy(i, 3).wait_recv()
+    for i in every:
+        for which in range(2):
+            for part in range(2):
+                land_copy(i, which, part).wait_recv()
+        size = outs[i].shape[1]
+        first = (chip * 2 + core) * size
+
+        def body(at, i=i, first=first):
+            for a in range(outs[i].shape[0]):
+                spot = pl.ds(at, step)
+                total = ins[i][a, pl.ds(pl.multiple_of(first + at, step), step), :].astype(F32)
+                total += near[i][3, a, spot, :].astype(F32)
+                total += land[i][0, a, spot, :].astype(F32)
+                total += land[i][1, a, spot, :].astype(F32)
+                outs[i][a, spot, :] = total.astype(outs[i].dtype)
+
+        each(i, size, body)
+    for i in every:
+        for j in range(4):
+            near_copy(i, j).wait_send()
+        for part in range(2):
+            side_copy(i, part).wait_send()
+            for which in range(2):
+                land_copy(i, which, part).wait_send()
+
+
+def plane_scatter(fulls, ident, out_dtype=F32):
+    count = len(fulls)
+    parts = lax.axis_size("col")
+    shapes = [(f.shape[0], f.shape[1] // parts, f.shape[2]) for f in fulls]
+    scratch = []
+    scratch += [pltpu.VMEM((4,) + s, BF16) for s in shapes]
+    scratch += [pltpu.VMEM((3,) + s, BF16) for s in shapes]
+    scratch += [pltpu.VMEM((2, s[0], s[1] // 2, s[2]), BF16) for s in shapes]
+    scratch += [pltpu.VMEM((2,) + s, BF16) for s in shapes]
+    return pl.pallas_call(
+        functools.partial(plane_scatter_kernel, count),
+        out_shape=[jax.ShapeDtypeStruct(s, out_dtype) for s in shapes],
+        in_specs=[pl.BlockSpec(memory_space=pltpu.VMEM)] * count,
+        out_specs=[pl.BlockSpec(memory_space=pltpu.VMEM)] * count,
+        scratch_shapes=scratch
+        + [pltpu.SemaphoreType.DMA((count, 10)), pltpu.SemaphoreType.DMA((count, 10))],
+        compiler_params=pltpu.CompilerParams(collective_id=ident, has_side_effects=True),
+        name="plane_scatter",
+    )(*fulls)
+
+
 def gather_row(block):
-    return lax.all_gather(block, "row", axis=1, tiled=True)
-
-
-def gather_col(block):
-    return lax.all_gather(block, "col", axis=0, tiled=True)
+    return lax.all_gather(block, "row", axis=block.ndim - 1, tiled=True)
 
 
 def scatter_row(full):
-    return lax.psum_scatter(full.astype(BF16), "row", scatter_dimension=1, tiled=True)
-
-
-def scatter_col(full):
-    return lax.psum_scatter(full.astype(BF16), "col", scatter_dimension=0, tiled=True)
+    return lax.psum_scatter(
+        full.astype(BF16), "row", scatter_dimension=full.ndim - 1, tiled=True
+    )
+
+
+def gather_col(blocks, ident):
+    if lax.axis_size("col") == 8:
+        return plane_gather(blocks, ident)
+    return [lax.all_gather(block, "col", axis=1, tiled=True) for block in blocks]
+
+
+def scatter_col(fulls, ident):
+    fulls = [full.astype(BF16) for full in fulls]
+    if lax.axis_size("col") == 8:
+        return plane_scatter(fulls, ident)
+    return [
+        lax.psum_scatter(full, "col", scatter_dimension=1, tiled=True).astype(F32)
+        for full in fulls
+    ]
 
 
 def shards(
@@ -110,30 +395,16 @@
     q_own, k_own = q_weight.shape[1], k_weight.shape[1]
     smalls = (q_bias, k_bias, v_bias, norm1_gain, norm2_gain)
     small_sizes = [member.shape[0] for member in smalls]
-    small_rows = 16
     packed_small = jnp.concatenate(smalls)
-    packed_small = jnp.pad(packed_small, (0, small_rows * depth_own - packed_small.shape[0]))
-    packed = jnp.concatenate(
-        [
-            q_weight.T,
-            k_weight.T,
-            v_weight.T,
-            o_weight.T,
-            packed_small.reshape(small_rows, depth_own),
-        ],
-        axis=0,
-    )
-    pack_rows = packed.shape[0]
-    gathered = gather_col(gather_row(packed)).reshape(col_parts, pack_rows, depth)
-    cuts = [0, q_own, q_own + k_own, q_own + 2 * k_own, 2 * q_own + 2 * k_own, pack_rows]
-    query_t, key_t, value_t, output_t, small_t = (
-        gathered[:, cuts[i] : cuts[i + 1], :] for i in range(5)
-    )
-    query_t = query_t.reshape(-1, depth)
-    key_t = key_t.reshape(-1, depth)
-    value_t = value_t.reshape(-1, depth)
-    output_t = output_t.reshape(-1, depth)
-    small_flat = small_t.reshape(col_parts, small_rows, row_parts, depth_own)
+    packed_small = jnp.pad(packed_small, (0, k_own * depth_own - packed_small.shape[0]))
+    wide_own = gather_row(jnp.stack([q_weight.T, o_weight.T]))
+    thin_own = gather_row(
+        jnp.stack([k_weight.T, v_weight.T, packed_small.reshape(k_own, depth_own)])
+    )
+    wide_full, thin_full = gather_col([wide_own, thin_own], 1)
+    query_t, output_t = wide_full[0], wide_full[1]
+    key_t, value_t = thin_full[0], thin_full[1]
+    small_flat = thin_full[2].reshape(col_parts, k_own, row_parts, depth_own)
     small_flat = small_flat.transpose(2, 0, 1, 3).reshape(row_parts * col_parts, -1)
     small_full, offset = [], 0
     for size in small_sizes:
@@ -162,9 +433,8 @@
     value_own = (dot_nt(first_normed, value_t) + value_offset.astype(F32)).astype(BF16)
     queries = rotate_pairs(query_base.reshape(own_rows, HQ, HD), cosines, sines).astype(BF16)
     keys_own = rotate_pairs(key_base.reshape(own_rows, KVH, HD), cosines, sines).astype(BF16)
-    both_all = gather_col(
-        jnp.concatenate([keys_own.reshape(own_rows, KVH * HD), value_own], axis=1)
-    )
+    both_own = jnp.concatenate([keys_own.reshape(own_rows, KVH * HD), value_own], axis=1)
+    both_all = gather_col([both_own[None]], 2)[0][0]
     window = min(own_rows + MAXLEN, row_tokens)
     window_start = jnp.clip(col_place * own_rows - MAXLEN, 0, row_tokens - window)
     key_slots = window_start + jnp.arange(window, dtype=jnp.int32)
@@ -190,26 +460,35 @@
     second_rms = rms_scale(residual)
     second_unit = residual * second_rms
     second_normed = (second_unit * second_gain.astype(F32)).astype(BF16)
-    normed_rows = gather_col(second_normed)
-    out_rows = gather_col(out_grad)
+    normed_rows, out_rows = (
+        member[0] for member in gather_col([second_normed[None], out_grad[None]], 3)
+    )
     gate_act = dot_nt(normed_rows, gate_t)
     up_act = dot_nt(normed_rows, up_t)
     sigmoid_gate = jax.nn.sigmoid(gate_act)
     silu_gate = gate_act * sigmoid_gate
     hidden = (silu_gate * up_act).astype(BF16)
-    down_grad = dot_tn(hidden, out_rows)
+    down_grad = dot_tn(hidden, out_rows).astype(BF16)
+    down_grad, out_rows = lax.optimization_barrier((down_grad, out_rows))
+    down_grad_own = scatter_row(down_grad)
     hidden_grad = dot_nt(out_rows, down_block)
     up_grad_act = (hidden_grad * silu_gate).astype(BF16)
     gate_grad_act = (
         hidden_grad * up_act * sigmoid_gate * (1.0 + gate_act * (1.0 - sigmoid_gate))
     ).astype(BF16)
-    normed_grad = scatter_col(dot_nn(gate_grad_act, gate_t) + dot_nn(up_grad_act, up_t)).astype(
-        F32
-    )
-    branch_out = scatter_col(dot_nn(hidden, down_block)).astype(F32)
+    normed_part = (dot_nn(gate_grad_act, gate_t) + dot_nn(up_grad_act, up_t)).astype(BF16)
+    branch_part = dot_nn(hidden, down_block).astype(BF16)
+    gate_grad_t = dot_tn(gate_grad_act, normed_rows).astype(BF16)
+    up_grad_t = dot_tn(up_grad_act, normed_rows).astype(BF16)
+    gate_grad_t, up_grad_t, normed_part = lax.optimization_barrier(
+        (gate_grad_t, up_grad_t, normed_part)
+    )
+    gate_grad_own = scatter_row(gate_grad_t)
+    up_grad_own = scatter_row(up_grad_t)
+    normed_grad, branch_out = (
+        member[0] for member in scatter_col([normed_part[None], branch_part[None]], 4)
+    )
     layer_out = residual + branch_out
-    gate_grad_t = dot_tn(gate_grad_act, normed_rows)
-    up_grad_t = dot_tn(up_grad_act, normed_rows)
     second_gain_grad = jnp.sum(normed_grad * second_unit, axis=0)
     unit_grad = normed_grad * second_gain.astype(F32)
     residual_grad = out_grad.astype(F32) + second_rms * (
@@ -243,7 +522,7 @@
     both_rows = lax.dynamic_update_slice_in_dim(
         jnp.zeros((row_tokens, 2 * KVH * HD), BF16), both_part, window_start, 0
     )
-    both_grad = scatter_col(both_rows).astype(F32)
+    both_grad = scatter_col([both_rows[None]], 5)[0][0]
     key_grad, value_grad = both_grad[:, : KVH * HD], both_grad[:, KVH * HD :]
     query_wide = rounded_wide(query_grad.reshape(own_rows, HQ, HD))
     query_base_grad = (
@@ -273,23 +552,27 @@
         [member.reshape(row_parts * col_parts, -1) for member in small_grads], axis=1
     )
     small_flat = jnp.pad(
-        small_flat, ((0, 0), (0, small_rows * depth_own - small_flat.shape[1]))
-    ).reshape(row_parts, col_parts, small_rows, depth_own)
-    small_flat = small_flat.transpose(1, 2, 0, 3).reshape(col_parts, small_rows, depth)
-    packed_grads = jnp.concatenate(
+        small_flat, ((0, 0), (0, k_own * depth_own - small_flat.shape[1]))
+    ).reshape(row_parts, col_parts, k_own, depth_own)
+    small_flat = small_flat.transpose(1, 2, 0, 3).reshape(col_parts * k_own, depth)
+    wide_grads = jnp.stack(
         [
-            dot_tn(query_base_grad, first_normed).astype(BF16).reshape(col_parts, q_own, depth),
-            dot_tn(key_base_grad, first_normed).astype(BF16).reshape(col_parts, k_own, depth),
-            dot_tn(value_base_grad, first_normed).astype(BF16).reshape(col_parts, k_own, depth),
-            dot_tn(attended_grad, mixed).astype(BF16).reshape(col_parts, q_own, depth),
+            dot_tn(query_base_grad, first_normed).astype(BF16),
+            dot_tn(attended_grad, mixed).astype(BF16),
+        ]
+    )
+    thin_grads = jnp.stack(
+        [
+            dot_tn(key_base_grad, first_normed).astype(BF16),
+            dot_tn(value_base_grad, first_normed).astype(BF16),
             small_flat.astype(BF16),
-        ],
-        axis=1,
-    ).reshape(col_parts * pack_rows, depth)
-    packed_out = scatter_row(scatter_col(packed_grads)).astype(F32)
-    query_w_out, key_w_out, value_w_out, output_w_out, small_out = (
-        packed_out[cuts[i] : cuts[i + 1]] for i in range(5)
-    )
+        ]
+    )
+    wide_part, thin_part = scatter_col([wide_grads, thin_grads], 6)
+    wide_out = scatter_row(wide_part).astype(F32)
+    thin_out = scatter_row(thin_part).astype(F32)
+    query_w_out, output_w_out = wide_out[0], wide_out[1]
+    key_w_out, value_w_out, small_out = thin_out[0], thin_out[1], thin_out[2]
     small_out = small_out.reshape(-1)
     small_list, offset = [], 0
     for size in small_sizes:
@@ -307,9 +590,9 @@
         small_list[2],
         output_w_out.T,
         small_list[4],
-        scatter_row(gate_grad_t).astype(F32).T,
-        scatter_row(up_grad_t).astype(F32).T,
-        scatter_row(down_grad).astype(F32),
+        gate_grad_own.astype(F32).T,
+        up_grad_own.astype(F32).T,
+        down_grad_own.astype(F32),
     )
 
 

time: 1090 us -> 852 us (0.78)
  waiting for transfers between devices: 752 us -> 226 us
  Pallas kernels: 0 us -> 270 us
  other arithmetic: 37.7 us -> 56.2 us
  blocking collectives: 0 us -> 17 us
  local copies, waits for them, and re-layouts: 88.3 us -> 71.7 us
    all_gather x8 -> x4, waiting for transfers between devices: 355 us -> 12.5 us  [gather_row(): return lax.all_gather(block, 'row', axis=block.ndim - 1, tiled=True)]
    pallas_call x0 -> x6, Pallas kernels: none -> 270 us  [the longest x3 139 us: plane_scatter(): pl.pallas_call(functools.partial(plane_scatter_kernel, count), out_shape=...]
    reduce_scatter x4 -> x0, waiting for transfers between devices: 167 us -> none  [scatter_col(): lax.psum_scatter(full.astype(BF16), 'col', scatter_dimension=0, tiled=True)]
    all_gather x0 -> x1, blocking collectives: none -> 17 us  [gather_row(): return lax.all_gather(block, 'row', axis=block.ndim - 1, tiled=True)]
    unnamed x20 -> x14, waiting for transfers between devices: 230 us -> 213 us
    another operation x2 -> x7, other arithmetic: 0.15 us -> 14.4 us  [the longest x1 8.29 us: shards(): jnp.stack([dot_tn(query_base_grad, first_normed).astype(BF16), dot_tn(att...]
    unnamed x116 -> x136, local copies, waits for them, and re-layouts: 46.4 us -> 43.7 us
  transfers between devices with their start and end apart: 16 -> 9, of which waited for: 16 -> 5; matrix products, arithmetic and copies ran while one was open for 16% -> 16% of each run, Pallas kernels for 0% -> 16%
where the time goes in v2:
time: 852 us; the launch traced here: 840 us
  Pallas kernels  270 us (32%)
  waiting for transfers between devices  226 us (27%)
  matrix products  184 us (22%)
  local copies, waits for them, and re-layouts  71.7 us (8%)
  other arithmetic  56.2 us (7%)
  blocking collectives  17 us (2%)
  between operations  15.3 us (2%)
    unnamed x14, waiting for transfers between devices  213 us
    pallas_call x3, Pallas kernels, plane_scatter(): pl.pallas_call(functools.partial(plane_scatter_kernel, count), out_shape=...  139 us
    pallas_call x3, Pallas kernels, plane_gather(): pl.pallas_call(functools.partial(plane_gather_kernel, count), out_shape=o...  131 us
    dot_general x7, matrix products, dot_nt(): lax.dot_general(left, right, (((1,), (1,)), ((), ())), preferred_element_...  58.9 us
    dot_general x7, matrix products, dot_nn(): lax.dot_general(left, right, (((1,), (0,)), ((), ())), preferred_element_...  49 us
    unnamed x136, local copies, waits for them, and re-layouts  43.7 us
    dot_general x7, matrix products, dot_tn(): lax.dot_general(left, right, (((0,), (0,)), ((), ())), preferred_element_...  39.7 us
  transfers between devices with their start and end apart: 9, of which 5 were waited for; matrix products, arithmetic and copies ran while one was open for 16% of the time, Pallas kernels for 16%

profile of v2, /device:TPU:8, one launch (start us, length us, event | category | flops | bytes accessed | tf_op | source)
XLA Modules:
  0.0 839.6 jit_solution(4755194721474389462)
XLA Ops:
  11.5 17.0 %all_gather.16.refs_1_ = bf16[3,32,1536]{2,1,0:T(8,128)(2,1)} all-gather(bf16[3,32,384]{2,1,0:T(8,128)(2,1)S(1)} %pad_maximum_fusion.5), channel_id=1, replica_groups=mesh['row'=4,'col'=8] {'row'}, dimensions={2}, use_global_device_ids=true | all-gather | bytes 368640 | tf_op jit(solution)/shard_map/all_gather | solution.py:348
  30.9 12.5 %all-gather.5.cloned.1.call-done.refs_0_ = bf16[2,192,1536]{2,1,0:T(8,128)(2,1)} async-done(((bf16[2,192,384]{2,1,0:T(8,128)(2,1)}), bf16[2,192,1536]{2,1,0:T(8,128)(2,1)}) %all-gather.5.cloned.1.call-update) | async-done | bytes 1179664 | tf_op jit(solution)/shard_map/all_gather | solution.py:348
  43.4 56.2 %plane_gather.3 = (bf16[2,1536,1536]{2,1,0:T(8,128)(2,1)}, bf16[3,256,1536]{2,1,0:T(8,128)(2,1)}) custom-call(bf16[2,192,1536]{2,1,0:T(8,128)(2,1)} %all-gather.5.cloned.1.call-done.refs_0_, bf16[3,32,1536]{2,1,0:T(8,128)(2,1)} %all_gather.16.refs_1_), custom_call_target="tpu_custom_call" | custom-call | tf_op jit(solution)/shard_map/plane_gather/pallas_call | solution.py:180
  106.7 14.9 %plane_gather.4 = bf16[1,2048,512]{2,1,0:T(8,128)(2,1)} custom-call(bf16[1,256,512]{2,1,0:T(8,128)(2,1)} %maximum_bitcast_fusion.refs_0_), custom_call_target="tpu_custom_call" | custom-call | tf_op jit(solution)/shard_map/plane_gather/pallas_call | solution.py:180
  124.6 5.1 fusion.31
  136.7 6.9 fusion.106
  143.6 7.6 fusion.3
  151.8 7.5 fusion.66
  164.9 59.6 %plane_gather.5 = (bf16[1,2048,1536]{2,1,0:T(8,128)(2,1)}, bf16[1,2048,1536]{2,1,0:T(8,128)(2,1)}) custom-call(bf16[1,256,1536]{2,1,0:T(8,128)(2,1)} %fusion.68.refs_0_, bf16[1,256,1536]{2,1,0:T(8,128)(2,1)} %bitcast.256), custom_call_target="tpu_custom_call" | custom-call | tf_op jit(solution)/shard_map/plane_gather/pallas_call | solution.py:180
  224.6 13.0 %fusion.17 = f32[2048,1120]{0,1:T(8,128)} fusion(bf16[1120,1536]{1,0:T(8,128)(2,1)} %all-gather.7.cloned.1.call-done, bf16[1,2048,1536]{2,1,0:T(8,128)(2,1)} %get-tuple-element.29), kind=kOutput, calls=%fused_computation.34 | convolution fusion | flops 7046430720 | bytes 18907136 | tf_op jit(solution)/shard_map/dot_general | solution.py:64
  237.7 14.7 %multiply_convert_fusion.2 = (bf16[2048,1120]{0,1:T(8,128)(2,1)S(1)}, f32[2048,1120]{0,1:T(8,128)}) fusion(f32[2048,1120]{0,1:T(8,128)} %fusion.17, bf16[1120,1536]{1,0:T(8,128)(2,1)} %all-gather.9.cloned.1.call-done, bf16[1,2048,1536]{2,1,0:T(8,128)(2,1)} %get-tuple-element.29), kind=kOutput, calls=%fused_computation.15 | convolution fusion | flops 7060193280 | bytes 32669696 | tf_op jit(solution)/shard_map/dot_general | solution.py:64
  252.4 8.8 %convolution_convert_fusion.5 = bf16[1120,1536]{1,0:T(8,128)(2,1)} fusion(bf16[2048,1120]{0,1:T(8,128)(2,1)S(1)} %get-tuple-element.84, bf16[1,2048,1536]{2,1,0:T(8,128)(2,1)S(1)} %copy-done.48), kind=kOutput, calls=%fused_computation.26 | convolution fusion | flops 7048151040 | bytes 14319616 | tf_op jit(solution)/shard_map/dot_general | solution.py:60
  261.2 18.8 %multiply_convert_fusion = (bf16[2048,1120]{0,1:T(8,128)(2,1)}, bf16[2048,1120]{0,1:T(8,128)(2,1)S(1)}) fusion(f32[2048,1120]{0,1:T(8,128)} %fusion.17, f32[2048,1120]{0,1:T(8,128)} %get-tuple-element.85, bf16[2048,1536]{1,0:T(8,128)(2,1)} %bitcast.287, bf16[1120,1536]{1,0:T(8,128)(2,1)} %all-gather.11.cloned.1.call-done), kind=kOutput, calls=%fused_computation.13 | convolution fusion | flops 7076249600 | bytes 37257216 | tf_op jit(solution)/shard_map/dot_general | solution.py:64
  280.1 12.0 %convolution_convert_fusion.3 = bf16[1120,1536]{1,0:T(8,128)(2,1)} fusion(bf16[2048,1120]{0,1:T(8,128)(2,1)} %get-tuple-element.48, bf16[1,2048,1536]{2,1,0:T(8,128)(2,1)S(1)} %bitcast.286), kind=kOutput, calls=%fused_computation.24 | convolution fusion | flops 7048151040 | bytes 14319616 | tf_op jit(solution)/shard_map/dot_general | solution.py:60
  292.0 8.8 %convolution_convert_fusion.4 = bf16[1120,1536]{1,0:T(8,128)(2,1)} fusion(bf16[2048,1120]{0,1:T(8,128)(2,1)S(1)} %get-tuple-element.49, bf16[1,2048,1536]{2,1,0:T(8,128)(2,1)S(1)} %bitcast.286), kind=kOutput, calls=%fused_computation.25 | convolution fusion | flops 7048151040 | bytes 14319616 | tf_op jit(solution)/shard_map/dot_general | solution.py:60
  300.8 11.0 %fusion.107 = f32[2048,1536]{1,0:T(8,128)S(1)} fusion(bf16[2048,1120]{0,1:T(8,128)(2,1)} %copy-done.52, bf16[1120,1536]{1,0:T(8,128)(2,1)S(1)} %copy-done.49), kind=kOutput, calls=%fused_computation.170 | convolution fusion | flops 7046430720 | bytes 20611072 | tf_op jit(solution)/shard_map/dot_general | solution.py:56
  311.9 13.1 %add_convert_fusion = bf16[2048,1536]{1,0:T(8,128)(2,1)} fusion(f32[2048,1536]{1,0:T(8,128)S(1)} %fusion.107, bf16[2048,1120]{0,1:T(8,128)(2,1)} %get-tuple-element.48, bf16[1120,1536]{1,0:T(8,128)(2,1)S(1)} %copy-done.50), kind=kOutput, calls=%fused_computation.10 | convolution fusion | flops 7052722176 | bytes 26902528 | tf_op jit(solution)/shard_map/dot_general | solution.py:56
  325.0 12.6 %fusion.12.refs_1_ = bf16[1,2048,1536]{2,1,0:T(8,128)(2,1)} fusion(bf16[2048,1120]{0,1:T(8,128)(2,1)} %copy-done.53, bf16[1120,1536]{1,0:T(8,128)(2,1)S(1)} %copy-done.51), kind=kOutput, calls=%fused_computation.29 | convolution fusion | flops 7049576448 | bytes 14319616 | tf_op jit(solution)/shard_map/dot_general | solution.py:56
  337.6 63.4 %plane_scatter.3 = (f32[1,256,1536]{2,1,0:T(8,128)}, f32[1,256,1536]{2,1,0:T(8,128)}) custom-call(bf16[1,2048,1536]{2,1,0:T(8,128)(2,1)} %bitcast.246, bf16[1,2048,1536]{2,1,0:T(8,128)(2,1)} %fusion.12.refs_1_), custom_call_target="tpu_custom_call" | custom-call | tf_op jit(solution)/shard_map/plane_scatter/pallas_call | solution.py:335
  414.3 14.4 %fusion = (f32[2,6,256]{2,1,0:T(8,128)S(1)}, f32[2,1280,256,6]{2,1,3,0:T(8,128)}) fusion(f32[2,6,256,1280]{2,3,1,0:T(8,128)} %get-tuple-element.81, f32[2,6,256]{2,1,0:T(8,128)S(1)} %copy-done.27, bf16[1280,2,128,1]{0,2,3,1:T(8,128)(2,1)} %bitcast.259, bf16[256,2,6,128]{0,3,2,1:T(8,128)(2,1)} %bitcast.242), kind=kOutput, calls=%fused_computation.2 | convolution fusion | flops 1018426368 | bytes 32923648 | tf_op jit(solution)/shard_map/tkgd,skd->kgts/dot_general | solution.py:502
  432.5 7.5 fusion.2
  447.1 7.8 dynamic_update_slice.4.refs_0_
  454.9 15.5 %plane_scatter.4 = f32[1,256,512]{2,1,0:T(8,128)} custom-call(bf16[1,2048,512]{2,1,0:T(8,128)(2,1)} %dynamic_update_slice.4.refs_0_), custom_call_target="tpu_custom_call" | custom-call | tf_op jit(solution)/shard_map/plane_scatter/pallas_call | solution.py:335
  496.0 8.3 pad_maximum_fusion.refs_0_
  507.3 60.0 %plane_scatter.5 = (f32[2,192,1536]{2,1,0:T(8,128)}, f32[3,32,1536]{2,1,0:T(8,128)}) custom-call(bf16[2,1536,1536]{2,1,0:T(8,128)(2,1)} %pad_maximum_fusion.refs_0_, bf16[3,256,1536]{2,1,0:T(8,128)(2,1)} %pad_maximum_fusion.1.refs_1_), custom_call_target="tpu_custom_call" | custom-call | tf_op jit(solution)/shard_map/plane_scatter/pallas_call | solution.py:335
  583.8 5.7 copy.141
  589.5 5.7 copy.139
  595.3 5.7 copy.143
  607.8 14.1 %reduce-scatter.18.cloned.1.call-done = bf16[384,384]{1,0:T(8,128)(2,1)} async-done(((bf16[1536,384]{1,0:T(8,128)(2,1)}), bf16[384,384]{1,0:T(8,128)(2,1)}) %reduce-scatter.18.cloned.1.call-update) | async-done | bytes 294928
  624.7 66.2 %reduce-scatter.22.cloned.1.call-done = bf16[384,1120]{1,0:T(8,128)(2,1)} async-done(((bf16[1536,1120]{1,0:T(8,128)(2,1)}), bf16[384,1120]{1,0:T(8,128)(2,1)}) %reduce-scatter.22.cloned.1.call-update) | async-done | bytes 860176
  693.3 66.7 %reduce-scatter.20.cloned.1.call-done = bf16[384,1120]{1,0:T(8,128)(2,1)} async-done(((bf16[1536,1120]{1,0:T(8,128)(2,1)}), bf16[384,1120]{1,0:T(8,128)(2,1)}) %reduce-scatter.20.cloned.1.call-update) | async-done | bytes 860176
  764.9 64.1 %reduce-scatter.24.cloned.1.call-done = bf16[384,1120]{1,0:T(8,128)(2,1)} async-done(((bf16[1536,1120]{1,0:T(8,128)(2,1)}), bf16[384,1120]{1,0:T(8,128)(2,1)}) %reduce-scatter.24.cloned.1.call-update) | async-done | bytes 860176
  (260 shorter events, 119.2 us)
Async XLA Ops:
  7.3 21.2 %copy-start.6 = (bf16[256,1536]{1,0:T(8,128)(2,1)S(1)}, bf16[256,1536]{1,0:T(8,128)(2,1)}, u32[]{:S(2)}) copy-start(bf16[256,1536]{1,0:T(8,128)(2,1)} %param.15) | copy-start | bytes 2359300
  7.3 21.5 %copy-start.40 = (s32[1,16]{1,0:T(1,128)S(1)}, s32[1,16]{1,0:T(1,128)}, u32[]{:S(2)}) copy-start(s32[1,16]{1,0:T(1,128)} %param.17) | copy-start | bytes 196
  7.3 36.1 %all-gather.5.cloned.1.call-start = ((), (), s32[]{:S(2)}) async-start(), calls=%async_computation.5 | async-start | bytes 1474560 | tf_op jit(solution)/shard_map/all_gather | solution.py:348
  9.1 215.5 %all-gather.7.cloned.1.call-start = ((), (), s32[]{:S(2)}) async-start(), calls=%async_computation.6 | async-start | bytes 4300800 | tf_op jit(solution)/shard_map/all_gather | solution.py:348
  9.9 227.8 %all-gather.9.cloned.1.call-start = ((), (), s32[]{:S(2)}) async-start(), calls=%async_computation.7 | async-start | bytes 4300800 | tf_op jit(solution)/shard_map/all_gather | solution.py:348
  10.6 250.6 %all-gather.11.cloned.1.call-start = ((), (), s32[]{:S(2)}) async-start(), calls=%async_computation.8 | async-start | bytes 4300800 | tf_op jit(solution)/shard_map/all_gather | solution.py:348
  11.2 593.4 %reduce-scatter.16.cloned.1.call-start = ((), (), s32[]{:S(2)}) async-start(), calls=%async_computation.9 | async-start | bytes 491520
  28.7 95.9 %copy-start.36 = (f32[256]{0:T(256)}, f32[256]{0:T(256)S(1)}, u32[]{:S(2)}) copy-start(f32[256]{0:T(256)S(1)} %add_rsqrt_fusion.1) | copy-start | bytes 3076
  29.6 71.5 %copy-start.18 = (f32[256,128]{0,1:T(8,128)}, f32[256,128]{0,1:T(8,128)S(1)}, u32[]{:S(2)}) copy-start(f32[256,128]{0,1:T(8,128)S(1)} %get-tuple-element.74) | copy-start | bytes 393220
  29.7 105.4 %copy-start.16 = (f32[256,128]{0,1:T(8,128)}, f32[256,128]{0,1:T(8,128)S(1)}, u32[]{:S(2)}) copy-start(f32[256,128]{0,1:T(8,128)S(1)} %get-tuple-element.73) | copy-start | bytes 393220
  29.8 75.6 %copy-start.23 = (f32[256,128]{1,0:T(8,128)}, f32[256,128]{1,0:T(8,128)S(1)}, u32[]{:S(2)}) copy-start(f32[256,128]{1,0:T(8,128)S(1)} %copy.97) | copy-start | bytes 393220
  29.9 75.9 %copy-start.21 = (f32[256,128]{1,0:T(8,128)}, f32[256,128]{1,0:T(8,128)S(1)}, u32[]{:S(2)}) copy-start(f32[256,128]{1,0:T(8,128)S(1)} %copy.96) | copy-start | bytes 393220
  101.6 23.0 %copy-start.30 = (f32[1536]{0:T(1024)}, f32[1536]{0:T(1024)S(1)}, u32[]{:S(2)}) copy-start(f32[1536]{0:T(1024)S(1)} %reshape.334) | copy-start | bytes 18436
  163.5 74.1 %copy-start.2 = (f32[256,1536]{1,0:T(8,128)}, f32[256,1536]{1,0:T(8,128)S(1)}, u32[]{:S(2)}) copy-start(f32[256,1536]{1,0:T(8,128)S(1)} %get-tuple-element.83) | copy-start | bytes 4718596
  163.6 74.1 %copy-start.34 = (f32[256]{0:T(256)}, f32[256]{0:T(256)S(1)}, u32[]{:S(2)}) copy-start(f32[256]{0:T(256)S(1)} %add_rsqrt_fusion) | copy-start | bytes 3076
  163.6 74.0 %copy-start.28 = (f32[1536]{0:T(1024)}, f32[1536]{0:T(1024)S(1)}, u32[]{:S(2)}) copy-start(f32[1536]{0:T(1024)S(1)} %reshape.338) | copy-start | bytes 18436
  237.7 14.7 %copy-start.48 = (bf16[1,2048,1536]{2,1,0:T(8,128)(2,1)S(1)}, bf16[1,2048,1536]{2,1,0:T(8,128)(2,1)}, u32[]{:S(2)}) copy-start(bf16[1,2048,1536]{2,1,0:T(8,128)(2,1)} %get-tuple-element.30) | copy-start | bytes 18874372
  252.4 27.7 %slice-start.4 = ((s8[6291456]{0:T(1024)(128)(4,1)}), s8[2097152]{0:T(1024)(128)(4,1)S(1)}, s32[]{:S(2)}) async-start(s8[6291456]{0:T(1024)(128)(4,1)} %bitcast.285), calls=%async_computation.18 | async-start | bytes 4194304
  261.2 18.8 %slice-start.5 = ((s8[6291456]{0:T(1024)(128)(4,1)}), s8[4194304]{0:T(1024)(128)(4,1)S(1)}, s32[]{:S(2)}) async-start(s8[6291456]{0:T(1024)(128)(4,1)} %bitcast.285), calls=%async_computation.19 | async-start | bytes 8388608
  337.6 63.4 %copy-start.3 = (f32[256,1536]{1,0:T(8,128)S(1)}, f32[256,1536]{1,0:T(8,128)}, u32[]{:S(2)}) copy-start(f32[256,1536]{1,0:T(8,128)} %copy-done.2) | copy-start | bytes 4718596
  337.6 63.4 %copy-start.29 = (f32[1536]{0:T(1024)S(1)}, f32[1536]{0:T(1024)}, u32[]{:S(2)}) copy-start(f32[1536]{0:T(1024)} %copy-done.28) | copy-start | bytes 18436
  337.6 63.4 %copy-start.35 = (f32[256]{0:T(256)S(1)}, f32[256]{0:T(256)}, u32[]{:S(2)}) copy-start(f32[256]{0:T(256)} %copy-done.34) | copy-start | bytes 3076
  407.2 21.4 %slice-start = ((s8[15728640]{0:T(1024)(128)(4,1)}), s8[3145728]{0:T(1024)(128)(4,1)S(1)}, s32[]{:S(2)}) async-start(s8[15728640]{0:T(1024)(128)(4,1)} %bitcast.235), calls=%async_computation.14 | async-start | bytes 6291456
  414.3 14.4 %copy-start.8 = (bf16[256,1536]{0,1:T(8,128)(2,1)S(1)}, bf16[256,1536]{0,1:T(8,128)(2,1)}, u32[]{:S(2)}) copy-start(bf16[256,1536]{0,1:T(8,128)(2,1)} %copy.106) | copy-start | bytes 2359300
  447.1 25.1 %copy-start.7 = (bf16[256,1536]{1,0:T(8,128)(2,1)S(1)}, bf16[256,1536]{1,0:T(8,128)(2,1)}, u32[]{:S(2)}) copy-start(bf16[256,1536]{1,0:T(8,128)(2,1)} %param.15) | copy-start | bytes 2359300
  447.1 25.1 %copy-start.31 = (f32[1536]{0:T(1024)S(1)}, f32[1536]{0:T(1024)}, u32[]{:S(2)}) copy-start(f32[1536]{0:T(1024)} %copy-done.30) | copy-start | bytes 18436
  447.1 25.1 %copy-start.37 = (f32[256]{0:T(256)S(1)}, f32[256]{0:T(256)}, u32[]{:S(2)}) copy-start(f32[256]{0:T(256)} %copy-done.36) | copy-start | bytes 3076
  447.1 26.4 %copy-start.1 = (f32[256,1536]{1,0:T(8,128)S(1)}, f32[256,1536]{1,0:T(8,128)}, u32[]{:S(2)}) copy-start(f32[256,1536]{1,0:T(8,128)} %copy-done) | copy-start | bytes 4718596
  574.2 47.6 %reduce-scatter.18.cloned.1.call-start = ((), (), s32[]{:S(2)}) async-start(), calls=%async_computation.10 | async-start | bytes 1474560
  583.7 107.2 %reduce-scatter.22.cloned.1.call-start = ((), (), s32[]{:S(2)}) async-start(), calls=%async_computation.12 | async-start | bytes 4423680
  589.5 170.5 %reduce-scatter.20.cloned.1.call-start = ((), (), s32[]{:S(2)}) async-start(), calls=%async_computation.11 | async-start | bytes 4423680
  595.2 233.8 %reduce-scatter.24.cloned.1.call-start = ((), (), s32[]{:S(2)}) async-start(), calls=%async_computation.13 | async-start | bytes 4423680
  (37 other events, 210.6 us)
Sparse Core Ops, SparseCore 0:
  10.3 33.0 all-gather.4
  45.0 65.9 all-gather.6
  112.6 66.6 all-gather.8
  180.7 66.6 all-gather.10
  574.4 15.7 reduce-scatter.15
  592.9 28.8 reduce-scatter.17
  624.2 66.7 reduce-scatter.21
  693.3 66.6 reduce-scatter.19
  762.3 66.6 reduce-scatter.23

commit v3 on v2

--- a/solution.py
+++ b/solution.py
@@ -344,13 +344,475 @@
     )(*fulls)
 
 
+def spans(total, most):
+    return [(at, min(most, total - at)) for at in range(0, total, most)]
+
+
+def remote(src, dst, send_sem, recv_sem, peer):
+    return pltpu.make_async_remote_copy(
+        src_ref=src,
+        dst_ref=dst,
+        send_sem=send_sem,
+        recv_sem=recv_sem,
+        device_id={"col": peer},
+        device_id_type=MESH,
+    )
+
+
+def ffn_forward_kernel(
+    normed,
+    cotangent,
+    gate_t,
+    up_t,
+    normed_rows,
+    out_rows,
+    hidden,
+    silu,
+    slope,
+    land,
+    tiles,
+    send_sem,
+    recv_sem,
+    keep_sem,
+    tile_sem,
+):
+    chip, beside, above, across, core = plane_places()
+    low, high = chip % 2, chip // 2
+    own_rows = normed.shape[0]
+    half = own_rows // 2
+    mine, partner = chip * 2 + core, chip * 2 + 1 - core
+    to_x, to_y, far = beside * 2 + core, above * 2 + core, across * 2 + core
+    greet((partner, to_x, to_y))
+    sources = (normed, cotangent)
+    full_rows = (normed_rows, out_rows)
+
+    def copy(a, k, slot, part, peer, own=False):
+        if part is None:
+            spot = land.at[a, slot]
+            src = sources[a] if own else spot
+        else:
+            spot = land.at[a, slot, pl.ds(part * half, half), :]
+            src = spot
+        return remote(src, spot, send_sem.at[a, k], recv_sem.at[a, k], peer)
+
+    def first(a):
+        copy(a, 1, mine, None, to_x, True).start()
+        copy(a, 2, mine, None, to_y, True).start()
+        copy(a, 0, mine, None, partner, True).start()
+
+    def second(a):
+        copy(a, 1, to_x, None, to_x).wait_recv()
+        copy(a, 3, to_x, 0, to_y).start()
+        copy(a, 5, to_x, None, partner).start()
+        copy(a, 2, to_y, None, to_y).wait_recv()
+        copy(a, 4, to_y, 1, to_x).start()
+        copy(a, 6, to_y, None, partner).start()
+
+    def third(a):
+        copy(a, 3, far, 0, to_y).wait_recv()
+        copy(a, 7, far, 0, partner).start()
+        copy(a, 4, far, 1, to_x).wait_recv()
+        copy(a, 8, far, 1, partner).start()
+
+    def landed(a, k):
+        slot = (partner, beside * 2 + 1 - core, above * 2 + 1 - core)[k]
+        copy(a, (0, 5, 6)[k], slot, None, partner).wait_recv()
+
+    def landed_far(a):
+        copy(a, 7, across * 2 + 1 - core, 0, partner).wait_recv()
+        copy(a, 8, across * 2 + 1 - core, 1, partner).wait_recv()
+
+    def sent(a):
+        for k, slot, part in (
+            (0, mine, None), (1, mine, None), (2, mine, None), (3, to_x, 0), (4, to_y, 1),
+            (5, to_x, None), (6, to_y, None), (7, far, 0), (8, far, 1),
+        ):
+            copy(a, k, slot, part, partner).wait_send()
+
+    def spread(index):
+        return pl.ds(pl.multiple_of(index * own_rows, own_rows), own_rows)
+
+    def keep(a, slot):
+        return pltpu.make_async_copy(
+            land.at[a, slot], full_rows[a].at[spread(slot), :], keep_sem.at[a, slot]
+        )
+
+    def put(kind, slot, parity):
+        target = (hidden, silu, slope)[kind]
+        return pltpu.make_async_copy(
+            tiles.at[kind, parity], target.at[spread(slot), :], tile_sem.at[kind, parity]
+        )
+
+    land[0, mine] = normed[...]
+    land[1, mine] = cotangent[...]
+    first(0)
+
+    def step(s, _):
+        flip = s // 2
+        at_chip = (high + flip // 2) % 2 * 2 + (low + flip) % 2
+        slot = at_chip * 2 + (core + s) % 2
+        parity = s % 2
+
+        @pl.when(s == 1)
+        def _():
+            landed(0, 0)
+
+        @pl.when(s == 2)
+        def _():
+            second(0)
+
+        @pl.when(s == 3)
+        def _():
+            landed(0, 1)
+
+        @pl.when(s == 4)
+        def _():
+            first(1)
+
+        @pl.when(s == 5)
+        def _():
+            landed(0, 2)
+            third(0)
+
+        @pl.when(s == 7)
+        def _():
+            landed_far(0)
+
+        keep(0, slot).start()
+
+        @pl.when(s >= 2)
+        def _():
+            for kind in range(3):
+                put(kind, slot, parity).wait()
+
+        for at, wide in spans(gate_t.shape[0], 512):
+            cut = slice(at, at + wide)
+            gate = dot_nt(land[0, slot], gate_t[cut, :])
+            up = dot_nt(land[0, slot], up_t[cut, :])
+            sigma = 1.0 / (1.0 + jnp.exp(-gate))
+            smooth = gate * sigma
+            tiles[0, parity, :, cut] = (smooth * up).astype(BF16)
+            tiles[1, parity, :, cut] = smooth.astype(BF16)
+            tiles[2, parity, :, cut] = (up * sigma * (1.0 + gate * (1.0 - sigma))).astype(BF16)
+        for kind in range(3):
+            put(kind, slot, parity).start()
+        return 0
+
+    lax.fori_loop(0, 8, step, 0)
+    second(1)
+    landed(1, 0)
+    third(1)
+    landed(1, 1)
+    landed(1, 2)
+    landed_far(1)
+
+    def store(slot, _):
+        keep(1, slot).start()
+        return 0
+
+    lax.fori_loop(0, 8, store, 0)
+
+    def drain(slot, _):
+        keep(0, slot).wait()
+        keep(1, slot).wait()
+        return 0
+
+    for parity in range(2):
+        for kind in range(3):
+            put(kind, 0, parity).wait()
+    lax.fori_loop(0, 8, drain, 0)
+    sent(0)
+    sent(1)
+
+
+def ffn_forward(normed, cotangent, gate_t, up_t, ident):
+    rows, depth = normed.shape
+    wide = gate_t.shape[0]
+    total = rows * 8
+    vmem = pl.BlockSpec(memory_space=pltpu.VMEM)
+    anywhere = pl.BlockSpec(memory_space=pl.ANY)
+    return pl.pallas_call(
+        ffn_forward_kernel,
+        out_shape=[jax.ShapeDtypeStruct((total, depth), BF16)] * 2
+        + [jax.ShapeDtypeStruct((total, wide), BF16)] * 3,
+        in_specs=[vmem] * 4,
+        out_specs=[anywhere] * 5,
+        scratch_shapes=[
+            pltpu.VMEM((2, 8, rows, depth), BF16),
+            pltpu.VMEM((3, 2, rows, wide), BF16),
+            pltpu.SemaphoreType.DMA((2, 9)),
+            pltpu.SemaphoreType.DMA((2, 9)),
+            pltpu.SemaphoreType.DMA((2, 8)),
+            pltpu.SemaphoreType.DMA((3, 2)),
+        ],
+        compiler_params=pltpu.CompilerParams(collective_id=ident, has_side_effects=True),
+        name="ffn_forward",
+    )(normed, cotangent, gate_t, up_t)
+
+
+def ffn_backward_kernel(
+    out_rows,
+    hidden,
+    silu,
+    slope,
+    gate_t,
+    up_t,
+    down,
+    gate_grad,
+    up_grad,
+    branch_own,
+    normed_own,
+    out_in,
+    tiles_in,
+    tiles_out,
+    give,
+    near,
+    made,
+    side,
+    land,
+    near_send,
+    near_recv,
+    side_send,
+    side_recv,
+    land_send,
+    land_recv,
+    in_sem,
+    tile_sem,
+):
+    chip, beside, above, across, core = plane_places()
+    low, high = chip % 2, chip // 2
+    own_rows = branch_own.shape[0]
+    half = own_rows // 2
+    depth = branch_own.shape[1]
+    partner = chip * 2 + 1 - core
+    to_x, to_y = beside * 2 + core, above * 2 + core
+    greet((partner, to_x, to_y))
+    finals = (branch_own, normed_own)
+
+    def spread(index):
+        return pl.ds(pl.multiple_of(index * own_rows, own_rows), own_rows)
+
+    def slot_of(s):
+        flip = 3 - s // 2
+        at_chip = (high + flip // 2) % 2 * 2 + (low + flip) % 2
+        return at_chip * 2 + (core + 1 + s) % 2
+
+    def near_copy(a, j):
+        return remote(
+            give.at[a, j], near.at[a, j], near_send.at[a, j], near_recv.at[a, j], partner
+        )
+
+    def side_copy(a, part):
+        return remote(
+            made.at[a, 0, pl.ds(part * half, half), :], side.at[a, part],
+            side_send.at[a, part], side_recv.at[a, part], to_x if part == 0 else to_y,
+        )
+
+    def land_copy(a, which, part):
+        k = which * 2 + part
+        return remote(
+            made.at[a, 1 + which, pl.ds(part * half, half), :],
+            land.at[a, which, pl.ds(part * half, half), :],
+            land_send.at[a, k], land_recv.at[a, k], to_x if which == 0 else to_y,
+        )
+
+    def fold(a, which, part):
+        def tile(t, _):
+            at = pl.multiple_of(t * 16, 16)
+            spot = pl.ds(pl.multiple_of(part * half + at, 16), 16)
+            left = made[a, 1 + which, spot, :].astype(F32)
+            right = side[a, 1 - which, pl.ds(at, 16), :].astype(F32)
+            made[a, 1 + which, spot, :] = (left + right).astype(BF16)
+            return 0
+
+        lax.fori_loop(0, half // 16, tile, 0)
+
+    def fetch(kind, s, parity):
+        if kind == 0:
+            return pltpu.make_async_copy(
+                out_rows.at[spread(slot_of(s)), :], out_in.at[parity], in_sem.at[0, parity]
+            )
+        source = (hidden, silu, slope)[kind - 1]
+        return pltpu.make_async_copy(
+            source.at[spread(slot_of(s)), :], tiles_in.at[kind - 1, parity], in_sem.at[kind, parity]
+        )
+
+    def put(kind, s, parity):
+        target = (gate_grad, up_grad)[kind]
+        return pltpu.make_async_copy(
+            tiles_out.at[kind, parity], target.at[spread(slot_of(s)), :],
+            tile_sem.at[kind, parity],
+        )
+
+    def sides(a):
+        side_copy(a, 0).wait_recv()
+        fold(a, 1, 0)
+        land_copy(a, 1, 0).start()
+        side_copy(a, 1).wait_recv()
+        fold(a, 0, 1)
+        land_copy(a, 0, 1).start()
+
+    def deliver(a, s, partial):
+        j = s // 2
+
+        @pl.when(s % 2 == 0)
+        def _():
+            give[a, j] = partial().astype(BF16)
+            near_copy(a, j).start()
+
+        @pl.when(s % 2 == 1)
+        def _():
+            total = partial()
+            near_copy(a, j).wait_recv()
+            total = total + near[a, j].astype(F32)
+
+            @pl.when(j < 3)
+            def _():
+                made[a, (3 - j) % 3] = total.astype(BF16)
+
+            @pl.when(j == 0)
+            def _():
+                side_copy(a, 0).start()
+                side_copy(a, 1).start()
+
+            @pl.when(j == 1)
+            def _():
+                land_copy(a, 1, 1).start()
+
+            @pl.when(j == 2)
+            def _():
+                land_copy(a, 0, 0).start()
+                sides(a)
+
+            @pl.when(j == 3)
+            def _():
+                finals[a][...] = total
+
+    fetch(1, 0, 0).start()
+
+    def branch_step(s, _):
+        parity = s % 2
+
+        @pl.when(s < 7)
+        def _():
+            fetch(1, s + 1, (s + 1) % 2).start()
+
+        @pl.when(s == 6)
+        def _():
+            for kind in (0, 2, 3):
+                fetch(kind, 0, 0).start()
+
+        fetch(1, s, parity).wait()
+        deliver(0, s, lambda: dot_nn(tiles_in[0, parity], down[...]))
+        return 0
+
+    lax.fori_loop(0, 8, branch_step, 0)
+
+    def normed_step(s, _):
+        parity = s % 2
+
+        @pl.when(s < 7)
+        def _():
+            for kind in (0, 2, 3):
+                fetch(kind, s + 1, (s + 1) % 2).start()
+
+        for kind in (0, 2, 3):
+            fetch(kind, s, parity).wait()
+
+        @pl.when(s >= 2)
+        def _():
+            for kind in range(2):
+                put(kind, s, parity).wait()
+
+        for at, wide in spans(down.shape[0], 512):
+            cut = slice(at, at + wide)
+            hidden_grad = dot_nt(out_in[parity], down[cut, :])
+            tiles_out[0, parity, :, cut] = (
+                hidden_grad * tiles_in[2, parity, :, cut].astype(F32)
+            ).astype(BF16)
+            tiles_out[1, parity, :, cut] = (
+                hidden_grad * tiles_in[1, parity, :, cut].astype(F32)
+            ).astype(BF16)
+        for kind in range(2):
+            put(kind, s, parity).start()
+        deliver(
+            1, s,
+            lambda: dot_nn(tiles_out[0, parity], gate_t[...])
+            + dot_nn(tiles_out[1, parity], up_t[...]),
+        )
+        return 0
+
+    lax.fori_loop(0, 8, normed_step, 0)
+    for a in range(2):
+        for which in range(2):
+            for part in range(2):
+                land_copy(a, which, part).wait_recv()
+
+        def tile(t, _, a=a):
+            spot = pl.ds(pl.multiple_of(t * 16, 16), 16)
+            finals[a][spot, :] = (
+                finals[a][spot, :]
+                + land[a, 0, spot, :].astype(F32)
+                + land[a, 1, spot, :].astype(F32)
+            )
+            return 0
+
+        lax.fori_loop(0, own_rows // 16, tile, 0)
+    for a in range(2):
+        for j in range(4):
+            near_copy(a, j).wait_send()
+        for part in range(2):
+            side_copy(a, part).wait_send()
+            for which in range(2):
+                land_copy(a, which, part).wait_send()
+    for kind in range(2):
+        for parity in range(2):
+            put(kind, parity, parity).wait()
+
+
+def ffn_backward(out_rows, hidden, silu, slope, gate_t, up_t, down, ident):
+    total, depth = out_rows.shape
+    wide = down.shape[0]
+    rows = total // 8
+    vmem = pl.BlockSpec(memory_space=pltpu.VMEM)
+    anywhere = pl.BlockSpec(memory_space=pl.ANY)
+    dma = pltpu.SemaphoreType.DMA
+    return pl.pallas_call(
+        ffn_backward_kernel,
+        out_shape=[jax.ShapeDtypeStruct((total, wide), BF16)] * 2
+        + [jax.ShapeDtypeStruct((rows, depth), F32)] * 2,
+        in_specs=[anywhere] * 4 + [vmem] * 3,
+        out_specs=[anywhere] * 2 + [vmem] * 2,
+        scratch_shapes=[
+            pltpu.VMEM((2, rows, depth), BF16),
+            pltpu.VMEM((3, 2, rows, wide), BF16),
+            pltpu.VMEM((2, 2, rows, wide), BF16),
+            pltpu.VMEM((2, 4, rows, depth), BF16),
+            pltpu.VMEM((2, 4, rows, depth), BF16),
+            pltpu.VMEM((2, 3, rows, depth), BF16),
+            pltpu.VMEM((2, 2, rows // 2, depth), BF16),
+            pltpu.VMEM((2, 2, rows, depth), BF16),
+            dma((2, 4)),
+            dma((2, 4)),
+            dma((2, 2)),
+            dma((2, 2)),
+            dma((2, 4)),
+            dma((2, 4)),
+            dma((4, 2)),
+            dma((2, 2)),
+        ],
+        compiler_params=pltpu.CompilerParams(collective_id=ident, has_side_effects=True),
+        name="ffn_backward",
+    )(out_rows, hidden, silu, slope, gate_t, up_t, down)
+
+
 def gather_row(block):
     return lax.all_gather(block, "row", axis=block.ndim - 1, tiled=True)
 
 
 def scatter_row(full):
     return lax.psum_scatter(
-        full.astype(BF16), "row", scatter_dimension=full.ndim - 1, tiled=True
+        full.astype(BF16), "row", scatter_dimension=0, tiled=True
     )
 
 
@@ -460,34 +922,44 @@
     second_rms = rms_scale(residual)
     second_unit = residual * second_rms
     second_normed = (second_unit * second_gain.astype(F32)).astype(BF16)
-    normed_rows, out_rows = (
-        member[0] for member in gather_col([second_normed[None], out_grad[None]], 3)
-    )
-    gate_act = dot_nt(normed_rows, gate_t)
-    up_act = dot_nt(normed_rows, up_t)
-    sigmoid_gate = jax.nn.sigmoid(gate_act)
-    silu_gate = gate_act * sigmoid_gate
-    hidden = (silu_gate * up_act).astype(BF16)
-    down_grad = dot_tn(hidden, out_rows).astype(BF16)
+    kernels = col_parts == 8
+    if kernels:
+        normed_rows, out_rows, hidden, silu_gate, slope = ffn_forward(
+            second_normed, out_grad, gate_t, up_t, 3
+        )
+    else:
+        normed_rows, out_rows = (
+            member[0] for member in gather_col([second_normed[None], out_grad[None]], 3)
+        )
+        gate_act = dot_nt(normed_rows, gate_t)
+        up_act = dot_nt(normed_rows, up_t)
+        sigmoid_gate = jax.nn.sigmoid(gate_act)
+        silu_gate = gate_act * sigmoid_gate
+        slope = up_act * sigmoid_gate * (1.0 + gate_act * (1.0 - sigmoid_gate))
+        hidden = (silu_gate * up_act).astype(BF16)
+    down_grad = dot_tn(out_rows, hidden).astype(BF16)
     down_grad, out_rows = lax.optimization_barrier((down_grad, out_rows))
     down_grad_own = scatter_row(down_grad)
-    hidden_grad = dot_nt(out_rows, down_block)
-    up_grad_act = (hidden_grad * silu_gate).astype(BF16)
-    gate_grad_act = (
-        hidden_grad * up_act * sigmoid_gate * (1.0 + gate_act * (1.0 - sigmoid_gate))
-    ).astype(BF16)
-    normed_part = (dot_nn(gate_grad_act, gate_t) + dot_nn(up_grad_act, up_t)).astype(BF16)
-    branch_part = dot_nn(hidden, down_block).astype(BF16)
-    gate_grad_t = dot_tn(gate_grad_act, normed_rows).astype(BF16)
-    up_grad_t = dot_tn(up_grad_act, normed_rows).astype(BF16)
-    gate_grad_t, up_grad_t, normed_part = lax.optimization_barrier(
-        (gate_grad_t, up_grad_t, normed_part)
-    )
-    gate_grad_own = scatter_row(gate_grad_t)
-    up_grad_own = scatter_row(up_grad_t)
-    normed_grad, branch_out = (
-        member[0] for member in scatter_col([normed_part[None], branch_part[None]], 4)
-    )
+    if kernels:
+        gate_grad_act, up_grad_act, branch_out, normed_grad = ffn_backward(
+            out_rows, hidden, silu_gate, slope, gate_t, up_t, down_block, 4
+        )
+    else:
+        hidden_grad = dot_nt(out_rows, down_block)
+        up_grad_act = (hidden_grad * silu_gate).astype(BF16)
+        gate_grad_act = (hidden_grad * slope).astype(BF16)
+        normed_part = dot_nn(gate_grad_act, gate_t) + dot_nn(up_grad_act, up_t)
+        branch_part = dot_nn(hidden, down_block)
+        normed_grad, branch_out = (
+            member[0] for member in scatter_col([normed_part[None], branch_part[None]], 4)
+        )
+    gate_grad = dot_tn(normed_rows, gate_grad_act).astype(BF16)
+    up_grad = dot_tn(normed_rows, up_grad_act).astype(BF16)
+    gate_grad, up_grad, normed_grad = lax.optimization_barrier(
+        (gate_grad, up_grad, normed_grad)
+    )
+    gate_grad_own = scatter_row(gate_grad)
+    up_grad_own = scatter_row(up_grad)
     layer_out = residual + branch_out
     second_gain_grad = jnp.sum(normed_grad * second_unit, axis=0)
     unit_grad = normed_grad * second_gain.astype(F32)
@@ -522,6 +994,7 @@
     both_rows = lax.dynamic_update_slice_in_dim(
         jnp.zeros((row_tokens, 2 * KVH * HD), BF16), both_part, window_start, 0
     )
+    both_rows, down_grad_own = lax.optimization_barrier((both_rows, down_grad_own))
     both_grad = scatter_col([both_rows[None]], 5)[0][0]
     key_grad, value_grad = both_grad[:, : KVH * HD], both_grad[:, KVH * HD :]
     query_wide = rounded_wide(query_grad.reshape(own_rows, HQ, HD))
@@ -568,9 +1041,12 @@
             small_flat.astype(BF16),
         ]
     )
+    wide_grads, gate_grad_own, up_grad_own = lax.optimization_barrier(
+        (wide_grads, gate_grad_own, up_grad_own)
+    )
     wide_part, thin_part = scatter_col([wide_grads, thin_grads], 6)
-    wide_out = scatter_row(wide_part).astype(F32)
-    thin_out = scatter_row(thin_part).astype(F32)
+    wide_out = scatter_row(wide_part.transpose(2, 0, 1)).astype(F32).transpose(1, 2, 0)
+    thin_out = scatter_row(thin_part.transpose(2, 0, 1)).astype(F32).transpose(1, 2, 0)
     query_w_out, output_w_out = wide_out[0], wide_out[1]
     key_w_out, value_w_out, small_out = thin_out[0], thin_out[1], thin_out[2]
     small_out = small_out.reshape(-1)
@@ -590,9 +1066,9 @@
         small_list[2],
         output_w_out.T,
         small_list[4],
-        gate_grad_own.astype(F32).T,
-        up_grad_own.astype(F32).T,
-        down_grad_own.astype(F32),
+        gate_grad_own.astype(F32),
+        up_grad_own.astype(F32),
+        down_grad_own.astype(F32).T,
     )
 
 

time: 852 us -> 637 us (0.75)
  the two profiles are of different devices: /device:TPU:8 before, /device:TPU:0 now
where the time goes in v3:
time: 637 us; the launch traced here: 626 us
  Pallas kernels  279 us (44%)
  matrix products  114 us (18%)
  waiting for transfers between devices  78.6 us (12%)
  local copies, waits for them, and re-layouts  67.3 us (11%)
  other arithmetic  53.5 us (8%)
  blocking collectives  18.1 us (3%)
  between operations  15 us (2%)
    pallas_call x2, Pallas kernels, plane_scatter(): pl.pallas_call(functools.partial(plane_scatter_kernel, count), out_shape=...  76.3 us
    pallas_call x2, Pallas kernels, plane_gather(): pl.pallas_call(functools.partial(plane_gather_kernel, count), out_shape=o...  70.8 us
    pallas_call x1, Pallas kernels, ffn_backward(): pl.pallas_call(ffn_backward_kernel, out_shape=[jax.ShapeDtypeStruct((tota...  70.1 us
    pallas_call x1, Pallas kernels, ffn_forward(): pl.pallas_call(ffn_forward_kernel, out_shape=[jax.ShapeDtypeStruct((total...  62.1 us
    unnamed x14, waiting for transfers between devices  46.2 us
    dot_general x7, matrix products, dot_tn(): lax.dot_general(left, right, (((0,), (0,)), ((), ())), preferred_element_...  45.6 us
    all_gather x4, waiting for transfers between devices, gather_row(): return lax.all_gather(block, 'row', axis=block.ndim - 1, tiled=True)  32.4 us
    unnamed x91, local copies, waits for them, and re-layouts  31.2 us
  transfers between devices with their start and end apart: 9, of which 5 were waited for; matrix products, arithmetic and copies ran while one was open for 34% of the time, Pallas kernels for 35%

profile of v3, /device:TPU:0, one launch (start us, length us, event | category | flops | bytes accessed | tf_op | source)
XLA Modules:
  0.0 626.0 jit_solution(494994876967949783)
XLA Ops:
  11.4 18.1 %all_gather.16.refs_1_ = bf16[3,32,1536]{2,1,0:T(8,128)(2,1)} all-gather(bf16[3,32,384]{2,1,0:T(8,128)(2,1)S(1)} %pad_maximum_fusion.5), channel_id=1, replica_groups=mesh['row'=4,'col'=8] {'row'}, dimensions={2}, use_global_device_ids=true | all-gather | bytes 368640 | tf_op jit(solution)/shard_map/all_gather | solution.py:810
  31.9 13.3 %all-gather.5.cloned.1.call-done.refs_0_ = bf16[2,192,1536]{2,1,0:T(8,128)(2,1)} async-done(((bf16[2,192,384]{2,1,0:T(8,128)(2,1)}), bf16[2,192,1536]{2,1,0:T(8,128)(2,1)}) %all-gather.5.cloned.1.call-update) | async-done | bytes 1179664 | tf_op jit(solution)/shard_map/all_gather | solution.py:810
  45.1 56.1 %plane_gather.2 = (bf16[2,1536,1536]{2,1,0:T(8,128)(2,1)}, bf16[3,256,1536]{2,1,0:T(8,128)(2,1)}) custom-call(bf16[2,192,1536]{2,1,0:T(8,128)(2,1)} %all-gather.5.cloned.1.call-done.refs_0_, bf16[3,32,1536]{2,1,0:T(8,128)(2,1)} %all_gather.16.refs_1_), custom_call_target="tpu_custom_call" | custom-call | tf_op jit(solution)/shard_map/plane_gather/pallas_call | solution.py:180
  108.3 14.7 %plane_gather.3 = bf16[1,2048,512]{2,1,0:T(8,128)(2,1)} custom-call(bf16[1,256,512]{2,1,0:T(8,128)(2,1)} %maximum_bitcast_fusion.refs_0_), custom_call_target="tpu_custom_call" | custom-call | tf_op jit(solution)/shard_map/plane_gather/pallas_call | solution.py:180
  126.3 5.1 fusion.23
  135.8 6.9 %fusion.95 = (f32[2,6,256]{2,1,0:T(8,128)S(1)}, f32[2,6,256,1280]{2,3,1,0:T(8,128)}) fusion(bf16[1280,2,128,1]{0,2,3,1:T(8,128)(2,1)S(1)} %bitcast.212, bf16[256,2,6,128]{0,3,2,1:T(8,128)(2,1)S(1)} %fusion.56, pred[256,1280]{0,1:T(8,128)(4,1)S(1)} %compare_and_fusion), kind=kOutput, calls=%fused_computation.151 | convolution fusion | flops 1018426368 | bytes 17510400 | tf_op jit(solution)/shard_map/tkgd,skd->kgts/dot_general | solution.py:72
  142.7 7.7 %fusion.3 = f32[2,6,256]{2,1,0:T(8,128)S(1)} fusion(f32[2,6,256,1280]{2,3,1,0:T(8,128)} %get-tuple-element.100, f32[2,6,256]{2,1,0:T(8,128)S(1)} %get-tuple-element.99), kind=kLoop, calls=%fused_computation.9 | loop fusion | flops 7861248 | bytes 15753216 | tf_op jit(solution)/shard_map/reduce_sum | solution.py:914
  150.4 7.6 %fusion.57 = bf16[2,128,6,256]{3,1,2,0:T(8,128)(2,1)S(1)} fusion(bf16[1280,2,128,1]{0,2,3,1:T(8,128)(2,1)S(1)} %bitcast.222, f32[2,6,256,1280]{2,3,1,0:T(8,128)} %get-tuple-element.100, f32[2,6,256]{2,1,0:T(8,128)S(1)} %fusion.3, f32[2,6,256]{2,1,0:T(8,128)S(1)} %get-tuple-element.99), kind=kOutput, calls=%fused_computation.76 | convolution fusion | flops 1018822656 | bytes 17195008 | tf_op jit(solution)/shard_map/kgts,skd->tkgd/dot_general | solution.py:917
  158.0 4.2 multiply_reduce_fusion.2
  163.4 19.1 %all-gather.9.cloned.1.call-done.up_t = bf16[1120,1536]{1,0:T(8,128)(2,1)} async-done(((bf16[1120,384]{1,0:T(8,128)(2,1)}), bf16[1120,1536]{1,0:T(8,128)(2,1)}) %all-gather.9.cloned.1.call-update) | async-done | bytes 3440656 | tf_op jit(solution)/shard_map/all_gather | solution.py:810
  182.4 62.1 %ffn_forward.1 = (bf16[2048,1536]{1,0:T(8,128)(2,1)}, bf16[2048,1536]{1,0:T(8,128)(2,1)}, bf16[2048,1120]{1,0:T(8,128)(2,1)}, bf16[2048,1120]{1,0:T(8,128)(2,1)}, bf16[2048,1120]{1,0:T(8,128)(2,1)}) custom-call(bf16[256,1536]{1,0:T(8,128)(2,1)} %multiply_convert_fusion.1.normed, bf16[256,1536]{1,0:T(8,128)(2,1)} %cotangent.1, ...), custom_call_target="tpu_custom_call" | custom-call | tf_op jit(solution)/shard_map/ffn_forward/pallas_call | solution.py:534
  244.5 12.2 %convolution_convert_fusion.4 = bf16[1536,1120]{0,1:T(8,128)(2,1)} fusion(bf16[2048,1536]{1,0:T(8,128)(2,1)} %get-tuple-element.41.out_rows, bf16[2048,1120]{1,0:T(8,128)(2,1)} %get-tuple-element.40.hidden), kind=kOutput, calls=%fused_computation.19 | convolution fusion | flops 7048151040 | bytes 14319616 | tf_op jit(solution)/shard_map/dot_general | solution.py:60
  256.7 5.7 copy.135
  262.5 70.1 %ffn_backward.1 = (bf16[2048,1120]{1,0:T(8,128)(2,1)}, bf16[2048,1120]{1,0:T(8,128)(2,1)}, f32[256,1536]{1,0:T(8,128)}, f32[256,1536]{1,0:T(8,128)}) custom-call(bf16[2048,1536]{1,0:T(8,128)(2,1)} %get-tuple-element.41.out_rows, bf16[2048,1120]{1,0:T(8,128)(2,1)} %get-tuple-element.40.hidden, bf16[2048,1120]{1,0:T(8,128)(2,1)} %get-tuple-element.42.silu, ...), custom_call_target="tpu_custom_call" | custom-call | tf_op jit(solution)/shard_map/ffn_backward/pallas_call | solution.py:780
  332.6 12.3 %convolution_convert_fusion.3 = bf16[1536,1120]{0,1:T(8,128)(2,1)} fusion(bf16[2048,1536]{1,0:T(8,128)(2,1)} %get-tuple-element.45, bf16[2048,1120]{1,0:T(8,128)(2,1)} %get-tuple-element.46), kind=kOutput, calls=%fused_computation.18 | convolution fusion | flops 7048151040 | bytes 14319616 | tf_op jit(solution)/shard_map/dot_general | solution.py:60
  344.9 11.1 %convolution_convert_fusion.2 = bf16[1536,1120]{0,1:T(8,128)(2,1)} fusion(bf16[2048,1536]{1,0:T(8,128)(2,1)} %get-tuple-element.45, bf16[2048,1120]{1,0:T(8,128)(2,1)S(1)} %copy-done.36), kind=kOutput, calls=%fused_computation.17 | convolution fusion | flops 7048151040 | bytes 14319616 | tf_op jit(solution)/shard_map/dot_general | solution.py:60
  356.0 5.7 copy.137
  367.7 4.6 fusion.37
  373.8 12.7 %fusion = (f32[2,6,256]{2,1,0:T(8,128)S(1)}, f32[2,1280,256,6]{2,1,3,0:T(8,128)}) fusion(f32[2,6,256,1280]{2,3,1,0:T(8,128)} %get-tuple-element.100, f32[2,6,256]{2,1,0:T(8,128)S(1)} %log_add_fusion, bf16[1280,2,128,1]{0,2,3,1:T(8,128)(2,1)S(1)} %bitcast.223, bf16[256,2,6,128]{0,3,2,1:T(8,128)(2,1)S(1)} %bitcast.208), kind=kOutput, calls=%fused_computation.2 | convolution fusion | flops 1018426368 | bytes 32923648 | tf_op jit(solution)/shard_map/tkgd,skd->kgts/dot_general | solution.py:974
  389.4 7.6 %fusion.2 = bf16[2,6,256,1280]{2,3,1,0:T(8,128)(2,1)S(1)} fusion(f32[2,1280,256,6]{2,1,3,0:T(8,128)} %get-tuple-element.104, f32[2,6,256,1280]{2,3,1,0:T(8,128)S(1)} %bitcast.204, f32[2,6,256]{2,1,0:T(8,128)S(1)} %get-tuple-element.103, f32[2,6,256]{2,1,0:T(8,128)S(1)} %log_add_fusion), kind=kLoop, calls=%fused_computation.4 | loop fusion | flops 15728640 | bytes 39346176 | tf_op jit(solution)/shard_map/convert_element_type | solution.py:982
  400.1 5.7 copy.139
  405.9 9.1 %fusion.33 = bf16[2,128,1280]{2,1,0:T(8,128)(2,1)} fusion(bf16[256,2,6,128]{0,3,2,1:T(8,128)(2,1)S(1)} %bitcast.209, f32[2,6,256,1280]{2,3,1,0:T(8,128)} %get-tuple-element.100, f32[2,6,256]{2,1,0:T(8,128)S(1)} %log_add_fusion), kind=kOutput, calls=%fused_computation.41 | convolution fusion | flops 1014824960 | bytes 17182720 | tf_op jit(solution)/shard_map/kgts,tkgd->skd/dot_general | solution.py:977
  417.2 6.8 %fusion.36 = bf16[2,128,1280]{2,1,0:T(8,128)(2,1)} fusion(bf16[256,2,6,128]{0,3,2,1:T(8,128)(2,1)S(1)} %copy-done.2, bf16[2,6,256,1280]{2,3,1,0:T(8,128)(2,1)} %copy-done), kind=kOutput, calls=%fused_computation.44 | convolution fusion | flops 1007288320 | bytes 9306112 | tf_op jit(solution)/shard_map/kgts,tkgd->skd/dot_general | solution.py:988
  431.7 8.1 %dynamic_update_slice.3 = bf16[2048,512]{1,0:T(8,128)(2,1)} dynamic-update-slice(bf16[2048,512]{1,0:T(8,128)(2,1)} %broadcast_in_dim.79, bf16[1280,512]{1,0:T(8,128)(2,1)} %pad_maximum_fusion.2, s32[]{:T(128)S(6)} %min.4, s32[]{:T(128)} %constant.42.clone.1) | dynamic-update-slice | bytes 2621444 | tf_op jit(solution)/shard_map/dynamic_update_slice | solution.py:994
  443.5 3.7 fusion.10
  447.2 5.0 fusion.15
  452.1 8.4 %pad_maximum_fusion.refs_0_ = bf16[2,1536,1536]{2,1,0:T(8,128)(2,1)} fusion(bf16[1,1536,1536]{2,1,0:T(8,128)(2,1)} %fusion.10, bf16[1,1536,1536]{2,1,0:T(8,128)(2,1)} %fusion.9), kind=kLoop, calls=%fused_computation.11 | loop fusion | flops 4718592 | bytes 18874368 | tf_op jit(solution)/shard_map/stack | solution.py:1031
  462.7 16.8 %plane_scatter.2 = f32[1,256,512]{2,1,0:T(8,128)} custom-call(bf16[1,2048,512]{2,1,0:T(8,128)(2,1)} %bitcast.207), custom_call_target="tpu_custom_call" | custom-call | tf_op jit(solution)/shard_map/plane_scatter/pallas_call | solution.py:335
  488.8 7.0 %reduce-scatter.20.cloned.1.call-done = bf16[384,1120]{1,0:T(8,128)(2,1)} async-done(((bf16[1536,1120]{1,0:T(8,128)(2,1)}), bf16[384,1120]{1,0:T(8,128)(2,1)}) %reduce-scatter.20.cloned.1.call-update) | async-done | bytes 860176
  504.7 59.5 %plane_scatter.3 = (f32[2,192,1536]{2,1,0:T(8,128)}, f32[3,32,1536]{2,1,0:T(8,128)}) custom-call(bf16[2,1536,1536]{2,1,0:T(8,128)(2,1)} %pad_maximum_fusion.refs_0_, bf16[3,256,1536]{2,1,0:T(8,128)(2,1)} %pad_maximum_fusion.1.refs_1_), custom_call_target="tpu_custom_call" | custom-call | tf_op jit(solution)/shard_map/plane_scatter/pallas_call | solution.py:335
  576.9 10.2 %reduce-scatter.22.cloned.1.call-done = bf16[384,96]{1,0:T(8,128)(2,1)} async-done(((bf16[1536,96]{1,0:T(8,128)(2,1)}), bf16[384,96]{1,0:T(8,128)(2,1)}) %reduce-scatter.22.cloned.1.call-update) | async-done | bytes 73744
  590.0 27.0 %reduce-scatter.24.cloned.1.call-done = bf16[384,384]{1,0:T(8,128)(2,1)} async-done(((bf16[1536,384]{1,0:T(8,128)(2,1)}), bf16[384,384]{1,0:T(8,128)(2,1)}) %reduce-scatter.24.cloned.1.call-update) | async-done | bytes 294928
  (210 shorter events, 87.1 us)
Async XLA Ops:
  7.2 38.0 %all-gather.5.cloned.1.call-start = ((), (), s32[]{:S(2)}) async-start(), calls=%async_computation.5 | async-start | bytes 1474560 | tf_op jit(solution)/shard_map/all_gather | solution.py:810
  9.0 2.4 copy-start.28
  9.0 154.3 %all-gather.7.cloned.1.call-start = ((), (), s32[]{:S(2)}) async-start(), calls=%async_computation.6 | async-start | bytes 4300800 | tf_op jit(solution)/shard_map/all_gather | solution.py:810
  9.1 20.4 %copy-start.3 = (bf16[256,1536]{1,0:T(8,128)(2,1)S(1)}, bf16[256,1536]{1,0:T(8,128)(2,1)}, u32[]{:S(2)}) copy-start(bf16[256,1536]{1,0:T(8,128)(2,1)} %param.15) | copy-start | bytes 2359300
  9.8 19.9 %copy-start.30 = (s32[1,16]{1,0:T(1,128)S(1)}, s32[1,16]{1,0:T(1,128)}, u32[]{:S(2)}) copy-start(s32[1,16]{1,0:T(1,128)} %param.17) | copy-start | bytes 196
  9.8 172.6 %all-gather.9.cloned.1.call-start = ((), (), s32[]{:S(2)}) async-start(), calls=%async_computation.7 | async-start | bytes 4300800 | tf_op jit(solution)/shard_map/all_gather | solution.py:810
  10.5 251.9 %all-gather.11.cloned.1.call-start = ((), (), s32[]{:S(2)}) async-start(), calls=%async_computation.8 | async-start | bytes 4300800 | tf_op jit(solution)/shard_map/all_gather | solution.py:810
  11.1 449.4 %reduce-scatter.16.cloned.1.call-start = ((), (), s32[]{:S(2)}) async-start(), calls=%async_computation.9 | async-start | bytes 4423680
  30.6 70.7 %copy-start.18 = (f32[256,128]{0,1:T(8,128)}, f32[256,128]{0,1:T(8,128)S(1)}, u32[]{:S(2)}) copy-start(f32[256,128]{0,1:T(8,128)S(1)} %get-tuple-element.93) | copy-start | bytes 393220
  30.7 76.4 %copy-start.23 = (f32[256,128]{1,0:T(8,128)}, f32[256,128]{1,0:T(8,128)S(1)}, u32[]{:S(2)}) copy-start(f32[256,128]{1,0:T(8,128)S(1)} %copy.97) | copy-start | bytes 393220
  30.8 76.6 %copy-start.21 = (f32[256,128]{1,0:T(8,128)}, f32[256,128]{1,0:T(8,128)S(1)}, u32[]{:S(2)}) copy-start(f32[256,128]{1,0:T(8,128)S(1)} %copy.96) | copy-start | bytes 393220
  126.2 9.6 %copy-start.9 = (bf16[1280,256]{0,1:T(8,128)(2,1)}, bf16[1280,256]{0,1:T(8,128)(2,1)S(1)}, u32[]{:S(2)}) copy-start(bf16[1280,256]{0,1:T(8,128)(2,1)S(1)} %copy.100) | copy-start | bytes 1966084
  135.8 6.9 %copy-start.1 = (bf16[256,2,6,128]{0,3,2,1:T(8,128)(2,1)}, bf16[256,2,6,128]{0,3,2,1:T(8,128)(2,1)S(1)}, u32[]{:S(2)}) copy-start(bf16[256,2,6,128]{0,3,2,1:T(8,128)(2,1)S(1)} %fusion.56) | copy-start | bytes 2359300
  142.7 7.7 %copy-start.15 = (bf16[1280,256]{0,1:T(8,128)(2,1)S(1)}, bf16[1280,256]{0,1:T(8,128)(2,1)}, u32[]{:S(2)}) copy-start(bf16[1280,256]{0,1:T(8,128)(2,1)} %copy.99) | copy-start | bytes 1966084
  150.4 7.6 %copy-start.4 = (bf16[256,1536]{1,0:T(8,128)(2,1)S(1)}, bf16[256,1536]{1,0:T(8,128)(2,1)}, u32[]{:S(2)}) copy-start(bf16[256,1536]{1,0:T(8,128)(2,1)} %param.15) | copy-start | bytes 2359300
  158.0 4.3 copy-start.26
  262.4 218.3 %reduce-scatter.18.cloned.1.call-start = ((), (), s32[]{:S(2)}) async-start(), calls=%async_computation.10 | async-start | bytes 4423680
  332.5 12.3 %copy-start.36 = (bf16[2048,1120]{1,0:T(8,128)(2,1)S(1)}, bf16[2048,1120]{1,0:T(8,128)(2,1)}, u32[]{:S(2)}) copy-start(bf16[2048,1120]{1,0:T(8,128)(2,1)} %get-tuple-element.47) | copy-start | bytes 13762564
  361.7 134.1 %reduce-scatter.20.cloned.1.call-start = ((), (), s32[]{:S(2)}) async-start(), calls=%async_computation.11 | async-start | bytes 4423680
  373.8 12.8 %slice-start = ((s8[15728640]{0:T(1024)(128)(4,1)}), s8[4194304]{0:T(1024)(128)(4,1)S(1)}, s32[]{:S(2)}) async-start(s8[15728640]{0:T(1024)(128)(4,1)} %bitcast.203), calls=%async_computation.14 | async-start | bytes 8388608
  373.8 12.9 %slice-start.1 = ((s8[15728640]{0:T(1024)(128)(4,1)}), s8[4194304]{0:T(1024)(128)(4,1)S(1)}, s32[]{:S(2)}) async-start(s8[15728640]{0:T(1024)(128)(4,1)} %bitcast.203), calls=%async_computation.15 | async-start | bytes 8388608
  373.8 14.7 %slice-start.2 = ((s8[15728640]{0:T(1024)(128)(4,1)}), s8[4194304]{0:T(1024)(128)(4,1)S(1)}, s32[]{:S(2)}) async-start(s8[15728640]{0:T(1024)(128)(4,1)} %bitcast.203), calls=%async_computation.16 | async-start | bytes 8388608
  373.8 15.6 %slice-start.3 = ((s8[15728640]{0:T(1024)(128)(4,1)}), s8[3145728]{0:T(1024)(128)(4,1)S(1)}, s32[]{:S(2)}) async-start(s8[15728640]{0:T(1024)(128)(4,1)} %bitcast.203), calls=%async_computation.17 | async-start | bytes 6291456
  389.4 7.6 %copy-start.10 = (bf16[1280,256]{0,1:T(8,128)(2,1)S(1)}, bf16[1280,256]{0,1:T(8,128)(2,1)}, u32[]{:S(2)}) copy-start(bf16[1280,256]{0,1:T(8,128)(2,1)} %copy-done.9) | copy-start | bytes 1966084
  397.0 3.1 copy-start
  405.8 181.4 %reduce-scatter.22.cloned.1.call-start = ((), (), s32[]{:S(2)}) async-start(), calls=%async_computation.12 | async-start | bytes 491520
  417.2 8.9 %copy-start.19 = (f32[256,128]{0,1:T(8,128)S(1)}, f32[256,128]{0,1:T(8,128)}, u32[]{:S(2)}) copy-start(f32[256,128]{0,1:T(8,128)} %copy-done.18) | copy-start | bytes 393220
  431.7 8.2 %copy-start.5 = (bf16[256,1536]{1,0:T(8,128)(2,1)S(1)}, bf16[256,1536]{1,0:T(8,128)(2,1)}, u32[]{:S(2)}) copy-start(bf16[256,1536]{1,0:T(8,128)(2,1)} %param.15) | copy-start | bytes 2359300
  431.7 8.2 %copy-start.25 = (bf16[256,12,128]{0,2,1:T(8,128)(2,1)S(1)}, bf16[256,12,128]{0,2,1:T(8,128)(2,1)}, u32[]{:S(2)}) copy-start(bf16[256,12,128]{0,2,1:T(8,128)(2,1)} %get-tuple-element.67) | copy-start | bytes 2359300
  439.8 3.7 copy-start.27
  480.7 3.7 copy-start.24
  566.3 50.7 %reduce-scatter.24.cloned.1.call-start = ((), (), s32[]{:S(2)}) async-start(), calls=%async_computation.13 | async-start | bytes 1474560
  (18 other events, 33.7 us)
Sparse Core Ops, SparseCore 0:
  10.2 34.9 all-gather.4
  46.7 67.3 all-gather.6
  115.7 66.6 all-gather.8
  183.9 66.6 all-gather.10
  262.5 66.5 reduce-scatter.15
  361.8 64.9 reduce-scatter.17
  429.1 66.6 reduce-scatter.19
  566.4 20.7 reduce-scatter.21
  589.5 27.4 reduce-scatter.23

commit v4 on v3

--- a/solution.py
+++ b/solution.py
@@ -359,195 +359,288 @@
     )
 
 
-def ffn_forward_kernel(
-    normed,
+def block_gather(source, land, send_sem, recv_sem):
+    chip, beside, above, across, core = plane_places()
+    half = source.shape[0] // 2
+    mine, partner, other = chip * 2 + core, chip * 2 + 1 - core, 1 - core
+    to_x, to_y, far = beside * 2 + core, above * 2 + core, across * 2 + core
+
+    def copy(k, slot, part, peer, own=False):
+        spot = land.at[slot] if part is None else land.at[slot, pl.ds(part * half, half), :]
+        return remote(source if own else spot, spot, send_sem.at[k], recv_sem.at[k], peer)
+
+    def first():
+        greet((partner, to_x, to_y))
+        copy(1, mine, None, to_x, True).start()
+        copy(2, mine, None, to_y, True).start()
+        copy(0, mine, None, partner, True).start()
+
+    def second():
+        copy(1, to_x, None, to_x).wait_recv()
+        copy(3, to_x, 0, to_y).start()
+        copy(5, to_x, None, partner).start()
+        copy(2, to_y, None, to_y).wait_recv()
+        copy(4, to_y, 1, to_x).start()
+        copy(6, to_y, None, partner).start()
+
+    def third():
+        copy(3, far, 0, to_y).wait_recv()
+        copy(7, far, 0, partner).start()
+        copy(4, far, 1, to_x).wait_recv()
+        copy(8, far, 1, partner).start()
+
+    def landed(k):
+        slot = (partner, beside * 2 + other, above * 2 + other)[k]
+        copy((0, 5, 6)[k], slot, None, partner).wait_recv()
+
+    def landed_far():
+        copy(7, across * 2 + other, 0, partner).wait_recv()
+        copy(8, across * 2 + other, 1, partner).wait_recv()
+
+    def sent():
+        for k, slot, part in (
+            (0, mine, None), (1, mine, None), (2, mine, None), (3, to_x, 0), (4, to_y, 1),
+            (5, to_x, None), (6, to_y, None), (7, far, 0), (8, far, 1),
+        ):
+            copy(k, slot, part, partner).wait_send()
+
+    return first, second, third, landed, landed_far, sent
+
+
+def spread(index, rows):
+    return pl.ds(pl.multiple_of(index * rows, rows), rows)
+
+
+def ffn_gate_kernel(
+    normed, gate_t, normed_rows, gate_act, land, tiles, send_sem, recv_sem, keep_sem, tile_sem
+):
+    chip, _, _, _, core = plane_places()
+    low, high = chip % 2, chip // 2
+    rows = normed.shape[0]
+    first, second, third, landed, landed_far, sent = block_gather(
+        normed, land, send_sem, recv_sem
+    )
+
+    def keep(slot):
+        return pltpu.make_async_copy(
+            land.at[slot], normed_rows.at[spread(slot, rows), :], keep_sem.at[slot]
+        )
+
+    def put(slot, parity):
+        return pltpu.make_async_copy(
+            tiles.at[parity], gate_act.at[spread(slot, rows), :], tile_sem.at[parity]
+        )
+
+    first()
+    land[chip * 2 + core] = normed[...]
+
+    def step(s, _):
+        flip = s // 2
+        at_chip = (high + flip // 2) % 2 * 2 + (low + flip) % 2
+        slot = at_chip * 2 + (core + s) % 2
+        parity = s % 2
+
+        @pl.when(s == 1)
+        def _():
+            landed(0)
+
+        @pl.when(s == 2)
+        def _():
+            second()
+
+        @pl.when(s == 3)
+        def _():
+            landed(1)
+
+        @pl.when(s == 5)
+        def _():
+            landed(2)
+
+        @pl.when(s == 6)
+        def _():
+            third()
+
+        @pl.when(s == 7)
+        def _():
+            landed_far()
+
+        keep(slot).start()
+
+        @pl.when(s >= 2)
+        def _():
+            put(slot, parity).wait()
+
+        for at, wide in spans(gate_t.shape[0], 512):
+            tiles[parity, :, at : at + wide] = dot_nt(land[slot], gate_t[at : at + wide, :])
+        put(slot, parity).start()
+        return 0
+
+    lax.fori_loop(0, 8, step, 0)
+    for parity in range(2):
+        put(0, parity).wait()
+
+    def drain(slot, _):
+        keep(slot).wait()
+        return 0
+
+    lax.fori_loop(0, 8, drain, 0)
+    sent()
+
+
+def ffn_gate(normed, gate_t, ident):
+    rows, depth = normed.shape
+    wide = gate_t.shape[0]
+    dma = pltpu.SemaphoreType.DMA
+    return pl.pallas_call(
+        ffn_gate_kernel,
+        out_shape=[
+            jax.ShapeDtypeStruct((rows * 8, depth), BF16),
+            jax.ShapeDtypeStruct((rows * 8, wide), F32),
+        ],
+        in_specs=[pl.BlockSpec(memory_space=pltpu.VMEM)] * 2,
+        out_specs=[pl.BlockSpec(memory_space=pl.ANY)] * 2,
+        scratch_shapes=[
+            pltpu.VMEM((8, rows, depth), BF16),
+            pltpu.VMEM((2, rows, wide), F32),
+            dma((9,)),
+            dma((9,)),
+            dma((8,)),
+            dma((2,)),
+        ],
+        compiler_params=pltpu.CompilerParams(collective_id=ident, has_side_effects=True),
+        name="ffn_gate",
+    )(normed, gate_t)
+
+
+def ffn_up_kernel(
     cotangent,
-    gate_t,
     up_t,
     normed_rows,
+    gate_act,
     out_rows,
     hidden,
     silu,
     slope,
     land,
+    rows_in,
+    gate_in,
     tiles,
     send_sem,
     recv_sem,
     keep_sem,
+    in_sem,
     tile_sem,
 ):
-    chip, beside, above, across, core = plane_places()
-    low, high = chip % 2, chip // 2
-    own_rows = normed.shape[0]
-    half = own_rows // 2
-    mine, partner = chip * 2 + core, chip * 2 + 1 - core
-    to_x, to_y, far = beside * 2 + core, above * 2 + core, across * 2 + core
-    greet((partner, to_x, to_y))
-    sources = (normed, cotangent)
-    full_rows = (normed_rows, out_rows)
-
-    def copy(a, k, slot, part, peer, own=False):
-        if part is None:
-            spot = land.at[a, slot]
-            src = sources[a] if own else spot
-        else:
-            spot = land.at[a, slot, pl.ds(part * half, half), :]
-            src = spot
-        return remote(src, spot, send_sem.at[a, k], recv_sem.at[a, k], peer)
-
-    def first(a):
-        copy(a, 1, mine, None, to_x, True).start()
-        copy(a, 2, mine, None, to_y, True).start()
-        copy(a, 0, mine, None, partner, True).start()
-
-    def second(a):
-        copy(a, 1, to_x, None, to_x).wait_recv()
-        copy(a, 3, to_x, 0, to_y).start()
-        copy(a, 5, to_x, None, partner).start()
-        copy(a, 2, to_y, None, to_y).wait_recv()
-        copy(a, 4, to_y, 1, to_x).start()
-        copy(a, 6, to_y, None, partner).start()
-
-    def third(a):
-        copy(a, 3, far, 0, to_y).wait_recv()
-        copy(a, 7, far, 0, partner).start()
-        copy(a, 4, far, 1, to_x).wait_recv()
-        copy(a, 8, far, 1, partner).start()
-
-    def landed(a, k):
-        slot = (partner, beside * 2 + 1 - core, above * 2 + 1 - core)[k]
-        copy(a, (0, 5, 6)[k], slot, None, partner).wait_recv()
-
-    def landed_far(a):
-        copy(a, 7, across * 2 + 1 - core, 0, partner).wait_recv()
-        copy(a, 8, across * 2 + 1 - core, 1, partner).wait_recv()
-
-    def sent(a):
-        for k, slot, part in (
-            (0, mine, None), (1, mine, None), (2, mine, None), (3, to_x, 0), (4, to_y, 1),
-            (5, to_x, None), (6, to_y, None), (7, far, 0), (8, far, 1),
-        ):
-            copy(a, k, slot, part, partner).wait_send()
-
-    def spread(index):
-        return pl.ds(pl.multiple_of(index * own_rows, own_rows), own_rows)
-
-    def keep(a, slot):
+    chip, _, _, _, core = plane_places()
+    rows = cotangent.shape[0]
+    first, second, third, landed, landed_far, sent = block_gather(
+        cotangent, land, send_sem, recv_sem
+    )
+
+    def fetch(kind, s, parity):
+        source = (normed_rows, gate_act)[kind]
+        target = (rows_in, gate_in)[kind]
         return pltpu.make_async_copy(
-            land.at[a, slot], full_rows[a].at[spread(slot), :], keep_sem.at[a, slot]
-        )
-
-    def put(kind, slot, parity):
+            source.at[spread(s, rows), :], target.at[parity], in_sem.at[kind, parity]
+        )
+
+    def keep(slot):
+        return pltpu.make_async_copy(
+            land.at[slot], out_rows.at[spread(slot, rows), :], keep_sem.at[slot]
+        )
+
+    def put(kind, s, parity):
         target = (hidden, silu, slope)[kind]
         return pltpu.make_async_copy(
-            tiles.at[kind, parity], target.at[spread(slot), :], tile_sem.at[kind, parity]
-        )
-
-    land[0, mine] = normed[...]
-    land[1, mine] = cotangent[...]
-    first(0)
+            tiles.at[kind, parity], target.at[spread(s, rows), :], tile_sem.at[kind, parity]
+        )
+
+    first()
+    fetch(0, 0, 0).start()
+    fetch(1, 0, 0).start()
+    land[chip * 2 + core] = cotangent[...]
 
     def step(s, _):
-        flip = s // 2
-        at_chip = (high + flip // 2) % 2 * 2 + (low + flip) % 2
-        slot = at_chip * 2 + (core + s) % 2
         parity = s % 2
 
-        @pl.when(s == 1)
-        def _():
-            landed(0, 0)
-
-        @pl.when(s == 2)
-        def _():
-            second(0)
-
-        @pl.when(s == 3)
-        def _():
-            landed(0, 1)
-
-        @pl.when(s == 4)
-        def _():
-            first(1)
-
-        @pl.when(s == 5)
-        def _():
-            landed(0, 2)
-            third(0)
+        @pl.when(s < 7)
+        def _():
+            fetch(0, s + 1, 1 - parity).start()
+            fetch(1, s + 1, 1 - parity).start()
 
         @pl.when(s == 7)
         def _():
-            landed_far(0)
-
-        keep(0, slot).start()
+            second()
 
         @pl.when(s >= 2)
         def _():
             for kind in range(3):
-                put(kind, slot, parity).wait()
-
-        for at, wide in spans(gate_t.shape[0], 512):
+                put(kind, s, parity).wait()
+
+        fetch(0, s, parity).wait()
+        fetch(1, s, parity).wait()
+        for at, wide in spans(up_t.shape[0], 512):
             cut = slice(at, at + wide)
-            gate = dot_nt(land[0, slot], gate_t[cut, :])
-            up = dot_nt(land[0, slot], up_t[cut, :])
+            up = dot_nt(rows_in[parity], up_t[cut, :])
+            gate = gate_in[parity, :, cut]
             sigma = 1.0 / (1.0 + jnp.exp(-gate))
             smooth = gate * sigma
             tiles[0, parity, :, cut] = (smooth * up).astype(BF16)
             tiles[1, parity, :, cut] = smooth.astype(BF16)
             tiles[2, parity, :, cut] = (up * sigma * (1.0 + gate * (1.0 - sigma))).astype(BF16)
         for kind in range(3):
-            put(kind, slot, parity).start()
+            put(kind, s, parity).start()
         return 0
 
     lax.fori_loop(0, 8, step, 0)
-    second(1)
-    landed(1, 0)
-    third(1)
-    landed(1, 1)
-    landed(1, 2)
-    landed_far(1)
+    landed(0)
+    third()
+    landed(1)
+    landed(2)
+    landed_far()
 
     def store(slot, _):
-        keep(1, slot).start()
+        keep(slot).start()
         return 0
 
+    def drain(slot, _):
+        keep(slot).wait()
+        return 0
+
     lax.fori_loop(0, 8, store, 0)
-
-    def drain(slot, _):
-        keep(0, slot).wait()
-        keep(1, slot).wait()
-        return 0
-
     for parity in range(2):
         for kind in range(3):
             put(kind, 0, parity).wait()
     lax.fori_loop(0, 8, drain, 0)
-    sent(0)
-    sent(1)
-
-
-def ffn_forward(normed, cotangent, gate_t, up_t, ident):
-    rows, depth = normed.shape
-    wide = gate_t.shape[0]
-    total = rows * 8
+    sent()
+
+
+def ffn_up(cotangent, up_t, normed_rows, gate_act, ident):
+    rows, depth = cotangent.shape
+    wide = up_t.shape[0]
+    dma = pltpu.SemaphoreType.DMA
     vmem = pl.BlockSpec(memory_space=pltpu.VMEM)
     anywhere = pl.BlockSpec(memory_space=pl.ANY)
     return pl.pallas_call(
-        ffn_forward_kernel,
-        out_shape=[jax.ShapeDtypeStruct((total, depth), BF16)] * 2
-        + [jax.ShapeDtypeStruct((total, wide), BF16)] * 3,
-        in_specs=[vmem] * 4,
-        out_specs=[anywhere] * 5,
+        ffn_up_kernel,
+        out_shape=[jax.ShapeDtypeStruct((rows * 8, depth), BF16)]
+        + [jax.ShapeDtypeStruct((rows * 8, wide), BF16)] * 3,
+        in_specs=[vmem, vmem, anywhere, anywhere],
+        out_specs=[anywhere] * 4,
         scratch_shapes=[
-            pltpu.VMEM((2, 8, rows, depth), BF16),
+            pltpu.VMEM((8, rows, depth), BF16),
+            pltpu.VMEM((2, rows, depth), BF16),
+            pltpu.VMEM((2, rows, wide), F32),
             pltpu.VMEM((3, 2, rows, wide), BF16),
-            pltpu.SemaphoreType.DMA((2, 9)),
-            pltpu.SemaphoreType.DMA((2, 9)),
-            pltpu.SemaphoreType.DMA((2, 8)),
-            pltpu.SemaphoreType.DMA((3, 2)),
+            dma((9,)),
+            dma((9,)),
+            dma((8,)),
+            dma((2, 2)),
+            dma((3, 2)),
         ],
         compiler_params=pltpu.CompilerParams(collective_id=ident, has_side_effects=True),
-        name="ffn_forward",
-    )(normed, cotangent, gate_t, up_t)
+        name="ffn_up",
+    )(cotangent, up_t, normed_rows, gate_act)
 
 
 def ffn_backward_kernel(
@@ -832,6 +925,546 @@
     ]
 
 
+def line_remote(src, dst, send_sem, recv_sem, peer):
+    return pltpu.make_async_remote_copy(
+        src_ref=src,
+        dst_ref=dst,
+        send_sem=send_sem,
+        recv_sem=recv_sem,
+        device_id={"row": peer},
+        device_id_type=MESH,
+    )
+
+
+def greet_grid(peers, place, places):
+    barrier = pltpu.get_barrier_semaphore()
+    for peer in peers:
+        pl.semaphore_signal(barrier, inc=1, device_id={"col": peer}, device_id_type=MESH)
+
+    @pl.when(place > 0)
+    def _():
+        pl.semaphore_signal(barrier, inc=1, device_id={"row": place - 1}, device_id_type=MESH)
+
+    @pl.when(place < places - 1)
+    def _():
+        pl.semaphore_signal(barrier, inc=1, device_id={"row": place + 1}, device_id_type=MESH)
+
+    edge = (place == 0) | (place == places - 1)
+
+    @pl.when(edge)
+    def _():
+        pl.semaphore_wait(barrier, len(peers) + 1)
+
+    @pl.when(jnp.logical_not(edge))
+    def _():
+        pl.semaphore_wait(barrier, len(peers) + 2)
+
+
+def grid_gather_kernel(count, places, *refs):
+    ins, outs = refs[:count], refs[count : 2 * count]
+    send_sem, recv_sem, line_send, line_recv, own_sem = refs[2 * count :]
+    place = lax.axis_index("row")
+    chip, beside, above, across, core = plane_places()
+    mine, partner, other = chip * 2 + core, chip * 2 + 1 - core, 1 - core
+    to_x, to_y, far = beside * 2 + core, above * 2 + core, across * 2 + core
+    every = range(count)
+    greet_grid((partner, to_x, to_y), place, places)
+
+    def view(i, slot, line, part):
+        size, wide = ins[i].shape
+        spot = pl.ds(pl.multiple_of(line * wide, wide), wide)
+        if part is None:
+            return outs[i].at[pl.ds(pl.multiple_of(slot * size, size), size), spot]
+        half = size // 2
+        return outs[i].at[pl.ds(pl.multiple_of(slot * size + part * half, half), half), spot]
+
+    def copies(k, slot, line, part, peer, own=False):
+        return [
+            remote(
+                ins[i] if own else view(i, slot, line, part),
+                view(i, slot, line, part),
+                send_sem.at[i, line, k],
+                recv_sem.at[i, line, k],
+                peer,
+            )
+            for i in every
+        ]
+
+    def line_copies(line, sem_at, peer, own=False):
+        return [
+            line_remote(
+                ins[i] if own else view(i, mine, line, None),
+                view(i, mine, line, None),
+                line_send.at[i, sem_at],
+                line_recv.at[i, line],
+                peer,
+            )
+            for i in every
+        ]
+
+    def start(cs):
+        for c in cs:
+            c.start()
+
+    def wait_recv(cs):
+        for c in cs:
+            c.wait_recv()
+
+    def first(line, own=False):
+        start(copies(1, mine, line, None, to_x, own))
+        start(copies(2, mine, line, None, to_y, own))
+        start(copies(0, mine, line, None, partner, own))
+
+    def second(line):
+        wait_recv(copies(1, to_x, line, None, to_x))
+        start(copies(3, to_x, line, 0, to_y))
+        start(copies(5, to_x, line, None, partner))
+        wait_recv(copies(2, to_y, line, None, to_y))
+        start(copies(4, to_y, line, 1, to_x))
+        start(copies(6, to_y, line, None, partner))
+
+    def third(line):
+        wait_recv(copies(3, far, line, 0, to_y))
+        start(copies(7, far, line, 0, partner))
+        wait_recv(copies(4, far, line, 1, to_x))
+        start(copies(8, far, line, 1, partner))
+
+    def last(line):
+        wait_recv(copies(0, partner, line, None, partner))
+        wait_recv(copies(5, beside * 2 + other, line, None, partner))
+        wait_recv(copies(6, above * 2 + other, line, None, partner))
+        wait_recv(copies(7, across * 2 + other, line, 0, partner))
+        wait_recv(copies(8, across * 2 + other, line, 1, partner))
+        for k, slot, part in (
+            (0, mine, None), (1, mine, None), (2, mine, None), (3, to_x, 0), (4, to_y, 1),
+            (5, to_x, None), (6, to_y, None), (7, far, 0), (8, far, 1),
+        ):
+            for c in copies(k, slot, line, part, partner):
+                c.wait_send()
+
+    def both(distance, body):
+        @pl.when((distance >= 1) & (place - distance >= 0))
+        def _():
+            body(place - distance)
+
+        @pl.when((distance >= 1) & (place + distance < places))
+        def _():
+            body(place + distance)
+
+        @pl.when(distance == 0)
+        def _():
+            body(place)
+
+    @pl.when(place < places - 1)
+    def _():
+        start(line_copies(place, place, place + 1, True))
+
+    @pl.when(place > 0)
+    def _():
+        start(line_copies(place, places, place - 1, True))
+
+    first(place, True)
+    own = [
+        pltpu.make_async_copy(ins[i], view(i, mine, place, None), own_sem.at[i]) for i in every
+    ]
+    start(own)
+
+    def step(t, _):
+        @pl.when((t >= 1) & (place - t >= 0))
+        def _():
+            line = place - t
+            wait_recv(line_copies(line, line, place))
+
+            @pl.when(place < places - 1)
+            def _():
+                start(line_copies(line, line, place + 1))
+
+            first(line)
+
+        @pl.when((t >= 1) & (place + t < places))
+        def _():
+            line = place + t
+            wait_recv(line_copies(line, line, place))
+
+            @pl.when(place > 0)
+            def _():
+                start(line_copies(line, line, place - 1))
+
+            first(line)
+
+        both(t - 1, second)
+        both(t - 2, third)
+        return 0
+
+    lax.fori_loop(0, places + 2, step, 0)
+
+    def finish(line, _):
+        last(line)
+
+        @pl.when((line < place) & (place < places - 1))
+        def _():
+            for c in line_copies(line, line, place):
+                c.wait_send()
+
+        @pl.when((line > place) & (place > 0))
+        def _():
+            for c in line_copies(line, line, place):
+                c.wait_send()
+
+        return 0
+
+    lax.fori_loop(0, places, finish, 0)
+
+    @pl.when(place < places - 1)
+    def _():
+        for c in line_copies(place, place, place):
+            c.wait_send()
+
+    @pl.when(place > 0)
+    def _():
+        for c in line_copies(place, places, place):
+            c.wait_send()
+
+    for c in own:
+        c.wait()
+
+
+def grid_gather(shards, ident):
+    count = len(shards)
+    places, parts = lax.axis_size("row"), lax.axis_size("col")
+    dma = pltpu.SemaphoreType.DMA
+    anywhere = pl.BlockSpec(memory_space=pl.ANY)
+    return pl.pallas_call(
+        functools.partial(grid_gather_kernel, count, places),
+        out_shape=[
+            jax.ShapeDtypeStruct((s.shape[0] * parts, s.shape[1] * places), s.dtype)
+            for s in shards
+        ],
+        in_specs=[anywhere] * count,
+        out_specs=[anywhere] * count,
+        scratch_shapes=[
+            dma((count, places, 9)),
+            dma((count, places, 9)),
+            dma((count, places + 1)),
+            dma((count, places)),
+            dma((count,)),
+        ],
+        compiler_params=pltpu.CompilerParams(collective_id=ident, has_side_effects=True),
+        name="grid_gather",
+    )(*shards)
+
+
+def grid_scatter_kernel(count, places, *refs):
+    ins, outs = refs[:count], refs[count : 2 * count]
+    scratch = refs[2 * count :]
+    near, made, side, land, line_in, line_out = (
+        scratch[i * count : (i + 1) * count] for i in range(6)
+    )
+    (
+        near_send, near_recv, side_send, side_recv, land_send, land_recv, line_send, line_recv,
+    ) = scratch[6 * count :]
+    place = lax.axis_index("row")
+    chip, beside, above, across, core = plane_places()
+    partner = chip * 2 + 1 - core
+    to_x, to_y = beside * 2 + core, above * 2 + core
+    order = (across, beside, above, chip)
+    every = range(count)
+    greet_grid((partner, to_x, to_y), place, places)
+
+    def source(i, slot, line, at, size):
+        rows, wide = outs[i].shape
+        return (
+            pl.ds(pl.multiple_of(slot * rows + at, size), size),
+            pl.ds(pl.multiple_of(line * wide, wide), wide),
+        )
+
+    def near_copy(i, line, j):
+        rows = outs[i].shape[0]
+        return remote(
+            ins[i].at[source(i, order[j] * 2 + 1 - core, line, 0, rows)],
+            near[i].at[line, j],
+            near_send.at[i, line, j], near_recv.at[i, line, j], partner,
+        )
+
+    def halves(i, part):
+        half = outs[i].shape[0] // 2
+        return pl.ds(part * half, half)
+
+    def side_copy(i, line, part):
+        return remote(
+            made[i].at[line, 0, halves(i, part), :], side[i].at[line, part],
+            side_send.at[i, line, part], side_recv.at[i, line, part],
+            to_x if part == 0 else to_y,
+        )
+
+    def land_copy(i, line, which, part):
+        k = which * 2 + part
+        return remote(
+            made[i].at[line, 1 + which, halves(i, part), :],
+            land[i].at[line, which, halves(i, part), :],
+            land_send.at[i, line, k], land_recv.at[i, line, k],
+            to_x if which == 0 else to_y,
+        )
+
+    def up_copy(i, line):
+        return line_remote(
+            line_out[i].at[line], line_in[i].at[line],
+            line_send.at[i, line], line_recv.at[i, line], place + 1,
+        )
+
+    def down_copy(i, line):
+        target = jnp.where(line == place - 1, places, line)
+        return line_remote(
+            line_out[i].at[line], line_in[i].at[target],
+            line_send.at[i, line], line_recv.at[i, target], place - 1,
+        )
+
+    def each(size, body):
+        def tile(t, _):
+            body(pl.multiple_of(t * 16, 16))
+            return 0
+
+        lax.fori_loop(0, size // 16, tile, 0)
+
+    def combine(i, line, j):
+        def body(at):
+            spot = pl.ds(at, 16)
+            left = ins[i][source(i, order[j] * 2 + core, line, at, 16)].astype(F32)
+            made[i][line, j, spot, :] = (left + near[i][line, j, spot, :].astype(F32)).astype(
+                BF16
+            )
+
+        each(outs[i].shape[0], body)
+
+    def fold(i, line, which, part):
+        half = outs[i].shape[0] // 2
+
+        def body(at):
+            spot = pl.ds(pl.multiple_of(part * half + at, 16), 16)
+            left = made[i][line, 1 + which, spot, :].astype(F32)
+            right = side[i][line, 1 - which, pl.ds(at, 16), :].astype(F32)
+            made[i][line, 1 + which, spot, :] = (left + right).astype(BF16)
+
+        each(half, body)
+
+    def sequence(q):
+        up = places - 1 - place
+        return jnp.where(q < up, places - 1 - q, q - up)
+
+    def first(line):
+        for i in every:
+            near_copy(i, line, 0).wait_recv()
+            combine(i, line, 0)
+            side_copy(i, line, 0).start()
+            side_copy(i, line, 1).start()
+        for i in every:
+            near_copy(i, line, 1).wait_recv()
+            combine(i, line, 1)
+            land_copy(i, line, 0, 0).start()
+            near_copy(i, line, 2).wait_recv()
+            combine(i, line, 2)
+            land_copy(i, line, 1, 1).start()
+
+    def second(line):
+        for i in every:
+            side_copy(i, line, 0).wait_recv()
+            fold(i, line, 1, 0)
+            land_copy(i, line, 1, 0).start()
+            side_copy(i, line, 1).wait_recv()
+            fold(i, line, 0, 1)
+            land_copy(i, line, 0, 1).start()
+
+    def arrived(i, slot):
+        line_remote(
+            line_out[i].at[0], line_in[i].at[slot],
+            line_send.at[i, 0], line_recv.at[i, slot], place,
+        ).wait_recv()
+
+    def third(line):
+        for i in every:
+            near_copy(i, line, 3).wait_recv()
+            for which in range(2):
+                for part in range(2):
+                    land_copy(i, line, which, part).wait_recv()
+
+        @pl.when((line > place) & (place > 0))
+        def _():
+            for i in every:
+                arrived(i, line)
+
+        @pl.when((line < place) & (place < places - 1))
+        def _():
+            for i in every:
+                arrived(i, line)
+
+        @pl.when((line == place) & (place > 0))
+        def _():
+            for i in every:
+                arrived(i, place)
+
+        @pl.when((line == place) & (place < places - 1))
+        def _():
+            for i in every:
+                arrived(i, places)
+
+        def total(i, at):
+            spot = pl.ds(at, 16)
+            value = ins[i][source(i, chip * 2 + core, line, at, 16)].astype(F32)
+            value += near[i][line, 3, spot, :].astype(F32)
+            value += land[i][line, 0, spot, :].astype(F32)
+            value += land[i][line, 1, spot, :].astype(F32)
+            return value
+
+        for i in every:
+            relays = ((line > place) & (place > 0)) | ((line < place) & (place < places - 1))
+
+            @pl.when((line != place) & relays)
+            def _(i=i):
+                def body(at):
+                    spot = pl.ds(at, 16)
+                    line_out[i][line, spot, :] = (
+                        total(i, at) + line_in[i][line, spot, :].astype(F32)
+                    ).astype(BF16)
+
+                each(outs[i].shape[0], body)
+
+            @pl.when((line != place) & jnp.logical_not(relays))
+            def _(i=i):
+                def body(at):
+                    line_out[i][line, pl.ds(at, 16), :] = total(i, at).astype(BF16)
+
+                each(outs[i].shape[0], body)
+
+            @pl.when(line > place)
+            def _(i=i):
+                up_copy(i, line).start()
+
+            @pl.when(line < place)
+            def _(i=i):
+                down_copy(i, line).start()
+
+            @pl.when(line == place)
+            def _(i=i):
+                def body(at):
+                    outs[i][pl.ds(at, 16), :] = total(i, at)
+
+                each(outs[i].shape[0], body)
+
+                @pl.when(place > 0)
+                def _():
+                    def more(at):
+                        spot = pl.ds(at, 16)
+                        outs[i][spot, :] += line_in[i][place, spot, :].astype(F32)
+
+                    each(outs[i].shape[0], more)
+
+                @pl.when(place < places - 1)
+                def _():
+                    def more(at):
+                        spot = pl.ds(at, 16)
+                        outs[i][spot, :] += line_in[i][places, spot, :].astype(F32)
+
+                    each(outs[i].shape[0], more)
+
+    def begin(q, _):
+        line = sequence(q)
+        for j in range(4):
+            for i in every:
+                near_copy(i, line, j).start()
+        return 0
+
+    lax.fori_loop(0, places, begin, 0)
+
+    def step(t, _):
+        @pl.when(t < places)
+        def _():
+            first(sequence(t))
+
+        @pl.when((t >= 1) & (t - 1 < places))
+        def _():
+            second(sequence(t - 1))
+
+        @pl.when(t >= 2)
+        def _():
+            third(sequence(t - 2))
+
+        return 0
+
+    lax.fori_loop(0, places + 2, step, 0)
+
+    def finish(line, _):
+        for i in every:
+            for j in range(4):
+                near_copy(i, line, j).wait_send()
+            for part in range(2):
+                side_copy(i, line, part).wait_send()
+                for which in range(2):
+                    land_copy(i, line, which, part).wait_send()
+
+            @pl.when(line != place)
+            def _(i=i):
+                up_copy(i, line).wait_send()
+
+        return 0
+
+    lax.fori_loop(0, places, finish, 0)
+
+
+def grid_scatter(fulls, ident):
+    count = len(fulls)
+    places, parts = lax.axis_size("row"), lax.axis_size("col")
+    shapes = [(f.shape[0] // parts, f.shape[1] // places) for f in fulls]
+    dma = pltpu.SemaphoreType.DMA
+    vmem = pl.BlockSpec(memory_space=pltpu.VMEM)
+    scratch = []
+    scratch += [pltpu.VMEM((places, 4) + s, BF16) for s in shapes]
+    scratch += [pltpu.VMEM((places, 3) + s, BF16) for s in shapes]
+    scratch += [pltpu.VMEM((places, 2, s[0] // 2, s[1]), BF16) for s in shapes]
+    scratch += [pltpu.VMEM((places, 2) + s, BF16) for s in shapes]
+    scratch += [pltpu.VMEM((places + 1,) + s, BF16) for s in shapes]
+    scratch += [pltpu.VMEM((places,) + s, BF16) for s in shapes]
+    return pl.pallas_call(
+        functools.partial(grid_scatter_kernel, count, places),
+        out_shape=[jax.ShapeDtypeStruct(s, F32) for s in shapes],
+        in_specs=[vmem] * count,
+        out_specs=[vmem] * count,
+        scratch_shapes=scratch
+        + [
+            dma((count, places, 4)),
+            dma((count, places, 4)),
+            dma((count, places, 2)),
+            dma((count, places, 2)),
+            dma((count, places, 4)),
+            dma((count, places, 4)),
+            dma((count, places)),
+            dma((count, places + 1)),
+        ],
+        compiler_params=pltpu.CompilerParams(collective_id=ident, has_side_effects=True),
+        name="grid_scatter",
+    )(*fulls)
+
+
+def gather_weights(blocks, ident):
+    places = lax.axis_size("row")
+    if lax.axis_size("col") == 8 and places > 1 and blocks[0].shape[1] % 128 == 0:
+        return grid_gather(blocks, ident)
+    return [
+        full[0] for full in gather_col([gather_row(block)[None] for block in blocks], ident)
+    ]
+
+
+def scatter_weights(fulls, ident):
+    places = lax.axis_size("row")
+    if lax.axis_size("col") == 8 and places > 1 and fulls[0].shape[1] // places % 128 == 0:
+        return grid_scatter(fulls, ident)
+    return [
+        lax.psum_scatter(
+            part[0].astype(BF16), "row", scatter_dimension=1, tiled=True
+        ).astype(F32)
+        for part in scatter_col([full[None] for full in fulls], ident)
+    ]
+
+
 def shards(
     hidden_in,
     out_grad,
@@ -859,14 +1492,17 @@
     small_sizes = [member.shape[0] for member in smalls]
     packed_small = jnp.concatenate(smalls)
     packed_small = jnp.pad(packed_small, (0, k_own * depth_own - packed_small.shape[0]))
-    wide_own = gather_row(jnp.stack([q_weight.T, o_weight.T]))
-    thin_own = gather_row(
-        jnp.stack([k_weight.T, v_weight.T, packed_small.reshape(k_own, depth_own)])
-    )
-    wide_full, thin_full = gather_col([wide_own, thin_own], 1)
-    query_t, output_t = wide_full[0], wide_full[1]
-    key_t, value_t = thin_full[0], thin_full[1]
-    small_flat = thin_full[2].reshape(col_parts, k_own, row_parts, depth_own)
+    query_t, output_t, key_t, value_t, small_t = gather_weights(
+        [
+            q_weight.T,
+            o_weight.T,
+            k_weight.T,
+            v_weight.T,
+            packed_small.reshape(k_own, depth_own),
+        ],
+        1,
+    )
+    small_flat = small_t.reshape(col_parts, k_own, row_parts, depth_own)
     small_flat = small_flat.transpose(2, 0, 1, 3).reshape(row_parts * col_parts, -1)
     small_full, offset = [], 0
     for size in small_sizes:
@@ -924,9 +1560,8 @@
     second_normed = (second_unit * second_gain.astype(F32)).astype(BF16)
     kernels = col_parts == 8
     if kernels:
-        normed_rows, out_rows, hidden, silu_gate, slope = ffn_forward(
-            second_normed, out_grad, gate_t, up_t, 3
-        )
+        normed_rows, gate_act = ffn_gate(second_normed, gate_t, 3)
+        out_rows, hidden, silu_gate, slope = ffn_up(out_grad, up_t, normed_rows, gate_act, 7)
     else:
         normed_rows, out_rows = (
             member[0] for member in gather_col([second_normed[None], out_grad[None]], 3)
@@ -1028,27 +1663,18 @@
         small_flat, ((0, 0), (0, k_own * depth_own - small_flat.shape[1]))
     ).reshape(row_parts, col_parts, k_own, depth_own)
     small_flat = small_flat.transpose(1, 2, 0, 3).reshape(col_parts * k_own, depth)
-    wide_grads = jnp.stack(
+    query_w = dot_tn(query_base_grad, first_normed).astype(BF16)
+    query_w, gate_grad_own = lax.optimization_barrier((query_w, gate_grad_own))
+    query_w_out, output_w_out, key_w_out, value_w_out, small_out = scatter_weights(
         [
-            dot_tn(query_base_grad, first_normed).astype(BF16),
+            query_w,
             dot_tn(attended_grad, mixed).astype(BF16),
-        ]
-    )
-    thin_grads = jnp.stack(
-        [
             dot_tn(key_base_grad, first_normed).astype(BF16),
             dot_tn(value_base_grad, first_normed).astype(BF16),
             small_flat.astype(BF16),
-        ]
-    )
-    wide_grads, gate_grad_own, up_grad_own = lax.optimization_barrier(
-        (wide_grads, gate_grad_own, up_grad_own)
-    )
-    wide_part, thin_part = scatter_col([wide_grads, thin_grads], 6)
-    wide_out = scatter_row(wide_part.transpose(2, 0, 1)).astype(F32).transpose(1, 2, 0)
-    thin_out = scatter_row(thin_part.transpose(2, 0, 1)).astype(F32).transpose(1, 2, 0)
-    query_w_out, output_w_out = wide_out[0], wide_out[1]
-    key_w_out, value_w_out, small_out = thin_out[0], thin_out[1], thin_out[2]
+        ],
+        6,
+    )
     small_out = small_out.reshape(-1)
     small_list, offset = [], 0
     for size in small_sizes:

time: 637 us -> 595 us (0.934)
  the two profiles are of different devices: /device:TPU:0 before, /device:TPU:8 now
where the time goes in v4:
time: 595 us; the launch traced here: 584 us
  Pallas kernels  350 us (59%)
  matrix products  109 us (18%)
  local copies, waits for them, and re-layouts  63.7 us (11%)
  other arithmetic  42.7 us (7%)
  between operations  15.4 us (3%)
    pallas_call x1, Pallas kernels, grid_scatter(): pl.pallas_call(functools.partial(grid_scatter_kernel, count, places), out...  93.8 us
    pallas_call x1, Pallas kernels, grid_gather(): pl.pallas_call(functools.partial(grid_gather_kernel, count, places), out_...  83.6 us
    pallas_call x1, Pallas kernels, ffn_backward(): pl.pallas_call(ffn_backward_kernel, out_shape=[jax.ShapeDtypeStruct((tota...  68.4 us
    dot_general x7, matrix products, dot_tn(): lax.dot_general(left, right, (((0,), (0,)), ((), ())), preferred_element_...  46.6 us
    pallas_call x1, Pallas kernels, ffn_up(): pl.pallas_call(ffn_up_kernel, out_shape=[jax.ShapeDtypeStruct((rows * 8,...  38 us
    pallas_call x1, Pallas kernels, ffn_gate(): pl.pallas_call(ffn_gate_kernel, out_shape=[jax.ShapeDtypeStruct((rows * 8...  35.5 us
    unnamed x101, local copies, waits for them, and re-layouts  31 us
    pallas_call x1, Pallas kernels, plane_scatter(): pl.pallas_call(functools.partial(plane_scatter_kernel, count), out_shape=...  15.8 us
  transfers between devices with their start and end apart: 6, of which 0 were waited for; matrix products, arithmetic and copies ran while one was open for 34% of the time, Pallas kernels for 60%

profile of v4, /device:TPU:8, one launch (start us, length us, event | category | flops | bytes accessed | tf_op | source)
XLA Modules:
  0.0 583.8 jit_solution(11829349706639253744)
XLA Ops:
  10.3 83.6 %grid_gather.1 = (bf16[1536,1536]{1,0:T(8,128)(2,1)}, bf16[1536,1536]{1,0:T(8,128)(2,1)}, bf16[256,1536]{1,0:T(8,128)(2,1)}, bf16[256,1536]{1,0:T(8,128)(2,1)}, bf16[256,1536]{1,0:T(8,128)(2,1)}) custom-call(bf16[192,384]{1,0:T(8,128)(2,1)} %bitcast.178, bf16[192,384]{1,0:T(8,128)(2,1)} %bitcast.179, bf16[32,384]{1,0:T(8,128)(2,1)} %bitcast.182, ...), custom_call_target="tpu_custom_call" | custom-call | tf_op jit(solution)/shard_map/grid_gather/pallas_call | solution.py:1137
  101.0 15.2 %plane_gather.1 = bf16[1,2048,512]{2,1,0:T(8,128)(2,1)} custom-call(bf16[1,256,512]{2,1,0:T(8,128)(2,1)} %maximum_bitcast_fusion.refs_0_), custom_call_target="tpu_custom_call" | custom-call | tf_op jit(solution)/shard_map/plane_gather/pallas_call | solution.py:180
  119.1 5.1 convolution_add_fusion.3
  131.8 7.1 %fusion.62 = (f32[2,6,256]{2,1,0:T(8,128)S(1)}, f32[2,6,256,1280]{2,3,1,0:T(8,128)}) fusion(bf16[1280,2,128,1]{0,2,3,1:T(8,128)(2,1)S(1)} %bitcast.151, bf16[256,2,6,128]{0,3,2,1:T(8,128)(2,1)S(1)} %fusion.31, pred[256,1280]{0,1:T(8,128)(4,1)S(1)} %compare_and_fusion), kind=kOutput, calls=%fused_computation.117 | convolution fusion | flops 1018426368 | bytes 17510400 | tf_op jit(solution)/shard_map/tkgd,skd->kgts/dot_general | solution.py:72
  139.0 7.7 %fusion.3 = f32[2,6,256]{2,1,0:T(8,128)S(1)} fusion(f32[2,6,256,1280]{2,3,1,0:T(8,128)} %get-tuple-element.107, f32[2,6,256]{2,1,0:T(8,128)S(1)} %get-tuple-element.106), kind=kLoop, calls=%fused_computation.9 | loop fusion | flops 7861248 | bytes 15753216 | tf_op jit(solution)/shard_map/reduce_sum | solution.py:1550
  146.7 7.4 %fusion.32 = bf16[2,128,6,256]{3,1,2,0:T(8,128)(2,1)S(1)} fusion(bf16[1280,2,128,1]{0,2,3,1:T(8,128)(2,1)S(1)} %bitcast.164, f32[2,6,256,1280]{2,3,1,0:T(8,128)} %get-tuple-element.107, f32[2,6,256]{2,1,0:T(8,128)S(1)} %fusion.3, f32[2,6,256]{2,1,0:T(8,128)S(1)} %get-tuple-element.106), kind=kOutput, calls=%fused_computation.58 | convolution fusion | flops 1018822656 | bytes 17195008 | tf_op jit(solution)/shard_map/kgts,skd->tkgd/dot_general | solution.py:1553
  156.8 35.5 %ffn_gate.1 = (bf16[2048,1536]{1,0:T(8,128)(2,1)}, f32[2048,1120]{1,0:T(8,128)}) custom-call(bf16[256,1536]{1,0:T(8,128)(2,1)} %multiply_convert_fusion.1.normed, bf16[1120,1536]{1,0:T(8,128)(2,1)} %all-gather.6.cloned.1.call-done.gate_t), custom_call_target="tpu_custom_call" | custom-call | tf_op jit(solution)/shard_map/ffn_gate/pallas_call | solution.py:494
  192.4 38.0 %ffn_up.1 = (bf16[2048,1536]{1,0:T(8,128)(2,1)}, bf16[2048,1120]{1,0:T(8,128)(2,1)}, bf16[2048,1120]{1,0:T(8,128)(2,1)}, bf16[2048,1120]{1,0:T(8,128)(2,1)}) custom-call(bf16[256,1536]{1,0:T(8,128)(2,1)} %cotangent.1, bf16[1120,1536]{1,0:T(8,128)(2,1)} %all-gather.4.cloned.1.call-done.up_t, bf16[2048,1536]{1,0:T(8,128)(2,1)} %get-tuple-element.48.normed_rows, ...), custom_call_target="tpu_custom_call" | custom-call | tf_op jit(solution)/shard_map/ffn_up/pallas_call | solution.py:624
  230.3 12.2 %convolution_convert_fusion.4 = bf16[1536,1120]{0,1:T(8,128)(2,1)} fusion(bf16[2048,1536]{1,0:T(8,128)(2,1)} %get-tuple-element.52.out_rows, bf16[2048,1120]{1,0:T(8,128)(2,1)} %get-tuple-element.51.hidden), kind=kOutput, calls=%fused_computation.18 | convolution fusion | flops 7048151040 | bytes 14319616 | tf_op jit(solution)/shard_map/dot_general | solution.py:60
  242.6 5.8 copy.135
  248.4 68.4 %ffn_backward.1 = (bf16[2048,1120]{1,0:T(8,128)(2,1)}, bf16[2048,1120]{1,0:T(8,128)(2,1)}, f32[256,1536]{1,0:T(8,128)}, f32[256,1536]{1,0:T(8,128)}) custom-call(bf16[2048,1536]{1,0:T(8,128)(2,1)} %get-tuple-element.52.out_rows, bf16[2048,1120]{1,0:T(8,128)(2,1)} %get-tuple-element.51.hidden, bf16[2048,1120]{1,0:T(8,128)(2,1)} %get-tuple-element.53.silu, ...), custom_call_target="tpu_custom_call" | custom-call | tf_op jit(solution)/shard_map/ffn_backward/pallas_call | solution.py:873
  316.9 12.4 %convolution_convert_fusion.2 = bf16[1536,1120]{0,1:T(8,128)(2,1)} fusion(bf16[2048,1536]{1,0:T(8,128)(2,1)} %get-tuple-element.48.normed_rows, bf16[2048,1120]{1,0:T(8,128)(2,1)} %get-tuple-element.57), kind=kOutput, calls=%fused_computation.16 | convolution fusion | flops 7048151040 | bytes 14319616 | tf_op jit(solution)/shard_map/dot_general | solution.py:60
  329.3 11.1 %convolution_convert_fusion.3 = bf16[1536,1120]{0,1:T(8,128)(2,1)} fusion(bf16[2048,1536]{1,0:T(8,128)(2,1)} %get-tuple-element.48.normed_rows, bf16[2048,1120]{1,0:T(8,128)(2,1)S(1)} %copy-done.36), kind=kOutput, calls=%fused_computation.17 | convolution fusion | flops 7048151040 | bytes 14319616 | tf_op jit(solution)/shard_map/dot_general | solution.py:60
  340.4 5.7 copy.137
  349.1 3.0 multiply_add_fusion
  352.1 3.7 convolution_convert_fusion.7
  356.1 5.9 %copy.139 = bf16[1536,1120]{1,0:T(8,128)(2,1)} copy(bf16[1536,1120]{0,1:T(8,128)(2,1)} %convolution_convert_fusion.2) | data formatting | bytes 6881280
  362.0 8.4 %fusion.13 = bf16[2,128,1280]{2,1,0:T(8,128)(2,1)S(1)} fusion(bf16[256,2,6,128]{0,3,2,1:T(8,128)(2,1)S(1)} %bitcast.147, f32[2,6,256,1280]{2,3,1,0:T(8,128)} %get-tuple-element.107, f32[2,6,256]{2,1,0:T(8,128)S(1)} %log_add_fusion), kind=kOutput, calls=%fused_computation.26 | convolution fusion | flops 1014824960 | bytes 17182720 | tf_op jit(solution)/shard_map/kgts,tkgd->skd/dot_general | solution.py:1612
  370.4 12.9 %fusion = (f32[2,6,256]{2,1,0:T(8,128)S(1)}, f32[2,1280,256,6]{2,1,3,0:T(8,128)}) fusion(f32[2,6,256,1280]{2,3,1,0:T(8,128)} %get-tuple-element.107, f32[2,6,256]{2,1,0:T(8,128)S(1)} %log_add_fusion, bf16[1280,2,128,1]{0,2,3,1:T(8,128)(2,1)S(1)} %bitcast.165, bf16[256,2,6,128]{0,3,2,1:T(8,128)(2,1)S(1)} %bitcast.148), kind=kOutput, calls=%fused_computation.2 | convolution fusion | flops 1018426368 | bytes 32923648 | tf_op jit(solution)/shard_map/tkgd,skd->kgts/dot_general | solution.py:1609
  384.4 9.9 %fusion.2 = bf16[2,6,256,1280]{2,3,1,0:T(8,128)(2,1)} fusion(f32[2,1280,256,6]{2,1,3,0:T(8,128)} %get-tuple-element.111, f32[2,6,256,1280]{2,3,1,0:T(8,128)S(1)} %bitcast.143, f32[2,6,256]{2,1,0:T(8,128)S(1)} %get-tuple-element.110, f32[2,6,256]{2,1,0:T(8,128)S(1)} %log_add_fusion), kind=kLoop, calls=%fused_computation.4 | loop fusion | flops 15728640 | bytes 39346176 | tf_op jit(solution)/shard_map/convert_element_type | solution.py:1617
  395.4 6.7 %fusion.16 = bf16[2,128,1280]{2,1,0:T(8,128)(2,1)} fusion(bf16[256,2,6,128]{0,3,2,1:T(8,128)(2,1)S(1)} %copy-done.4, bf16[2,6,256,1280]{2,3,1,0:T(8,128)(2,1)} %fusion.2), kind=kOutput, calls=%fused_computation.29 | convolution fusion | flops 1007288320 | bytes 9306112 | tf_op jit(solution)/shard_map/kgts,tkgd->skd/dot_general | solution.py:1623
  405.4 4.5 multiply_convert_fusion
  415.0 8.0 %dynamic_update_slice.3 = bf16[2048,512]{1,0:T(8,128)(2,1)} dynamic-update-slice(bf16[2048,512]{1,0:T(8,128)(2,1)} %broadcast_in_dim.79, bf16[1280,512]{1,0:T(8,128)(2,1)} %pad_maximum_fusion, s32[]{:T(128)S(6)} %min.4, s32[]{:T(128)} %constant.42.clone.1) | dynamic-update-slice | bytes 2621444 | tf_op jit(solution)/shard_map/dynamic_update_slice | solution.py:1629
  423.0 3.7 convolution_convert_fusion.1.refs_0_
  426.7 3.6 convolution_convert_fusion.refs_1_
  430.4 2.5 fusion.63
  432.9 2.3 copy.136
  435.2 15.8 %plane_scatter.1 = f32[1,256,512]{2,1,0:T(8,128)} custom-call(bf16[1,2048,512]{2,1,0:T(8,128)(2,1)} %bitcast.146), custom_call_target="tpu_custom_call" | custom-call | tf_op jit(solution)/shard_map/plane_scatter/pallas_call | solution.py:335
  464.7 2.3 convolution_convert_fusion.6.refs_2_
  468.4 93.8 %grid_scatter.1 = (f32[192,384]{1,0:T(8,128)}, f32[192,384]{1,0:T(8,128)}, f32[32,384]{1,0:T(8,128)}, f32[32,384]{1,0:T(8,128)}, f32[32,384]{1,0:T(8,128)}) custom-call(bf16[1536,1536]{1,0:T(8,128)(2,1)} %convolution_convert_fusion.1.refs_0_, bf16[1536,1536]{1,0:T(8,128)(2,1)} %convolution_convert_fusion.refs_1_, ...), custom_call_target="tpu_custom_call" | custom-call | tf_op jit(solution)/shard_map/grid_scatter/pallas_call | solution.py:1426
  563.0 2.5 convert_element_type.240
  567.9 2.3 copy.140
  (200 shorter events, 61.6 us)
Async XLA Ops:
  7.2 2.3 copy-start.34
  7.2 2.3 copy-start.31
  7.2 2.3 copy-start.32
  7.2 2.3 copy-start.33
  7.2 149.6 %all-gather.6.cloned.1.call-start = ((), (), s32[]{:S(2)}) async-start(), calls=%async_computation.4 | async-start | bytes 4300800 | tf_op jit(solution)/shard_map/all_gather | solution.py:903
  8.0 184.4 %all-gather.4.cloned.1.call-start = ((), (), s32[]{:S(2)}) async-start(), calls=%async_computation.3 | async-start | bytes 4300800 | tf_op jit(solution)/shard_map/all_gather | solution.py:903
  8.7 239.7 %all-gather.8.cloned.1.call-start = ((), (), s32[]{:S(2)}) async-start(), calls=%async_computation.5 | async-start | bytes 4300800 | tf_op jit(solution)/shard_map/all_gather | solution.py:903
  9.4 423.4 %reduce-scatter.10.cloned.1.call-start = ((), (), s32[]{:S(2)}) async-start(), calls=%async_computation.6 | async-start | bytes 4423680
  119.0 12.8 %copy-start.8 = (bf16[1280,256]{0,1:T(8,128)(2,1)}, bf16[1280,256]{0,1:T(8,128)(2,1)S(1)}, u32[]{:S(2)}) copy-start(bf16[1280,256]{0,1:T(8,128)(2,1)S(1)} %copy.100) | copy-start | bytes 1966084
  131.8 7.1 %copy-start.3 = (bf16[256,2,6,128]{0,3,2,1:T(8,128)(2,1)}, bf16[256,2,6,128]{0,3,2,1:T(8,128)(2,1)S(1)}, u32[]{:S(2)}) copy-start(bf16[256,2,6,128]{0,3,2,1:T(8,128)(2,1)S(1)} %fusion.31) | copy-start | bytes 2359300
  139.0 7.7 %copy-start.12 = (bf16[1280,256]{0,1:T(8,128)(2,1)S(1)}, bf16[1280,256]{0,1:T(8,128)(2,1)}, u32[]{:S(2)}) copy-start(bf16[1280,256]{0,1:T(8,128)(2,1)} %copy.99) | copy-start | bytes 1966084
  139.0 15.1 %slice-start.6 = ((s8[4718592]{0:T(1024)(128)(4,1)}), s8[524288]{0:T(1024)(128)(4,1)S(1)}, s32[]{:S(2)}) async-start(s8[4718592]{0:T(1024)(128)(4,1)} %bitcast.189), calls=%async_computation.15 | async-start | bytes 1048576
  146.7 7.4 %copy-start.1 = (bf16[256,1536]{1,0:T(8,128)(2,1)S(1)}, bf16[256,1536]{1,0:T(8,128)(2,1)}, u32[]{:S(2)}) copy-start(bf16[256,1536]{1,0:T(8,128)(2,1)} %param.15) | copy-start | bytes 2359300
  146.7 7.4 %slice-start.7 = ((s8[4718592]{0:T(1024)(128)(4,1)}), s8[4194304]{0:T(1024)(128)(4,1)S(1)}, s32[]{:S(2)}) async-start(s8[4718592]{0:T(1024)(128)(4,1)} %bitcast.189), calls=%async_computation.16 | async-start | bytes 8388608
  248.4 214.2 %reduce-scatter.12.cloned.1.call-start = ((), (), s32[]{:S(2)}) async-start(), calls=%async_computation.7 | async-start | bytes 4423680
  316.9 12.4 %copy-start.36 = (bf16[2048,1120]{1,0:T(8,128)(2,1)S(1)}, bf16[2048,1120]{1,0:T(8,128)(2,1)}, u32[]{:S(2)}) copy-start(bf16[2048,1120]{1,0:T(8,128)(2,1)} %get-tuple-element.56) | copy-start | bytes 13762564
  346.1 221.8 %reduce-scatter.14.cloned.1.call-start = ((), (), s32[]{:S(2)}) async-start(), calls=%async_computation.8 | async-start | bytes 4423680
  362.0 8.4 %copy-start.13 = (bf16[1280,256]{0,1:T(8,128)(2,1)S(1)}, bf16[1280,256]{0,1:T(8,128)(2,1)}, u32[]{:S(2)}) copy-start(bf16[1280,256]{0,1:T(8,128)(2,1)} %copy.99) | copy-start | bytes 1966084
  362.0 21.3 %slice-start = ((s8[15728640]{0:T(1024)(128)(4,1)}), s8[4194304]{0:T(1024)(128)(4,1)S(1)}, s32[]{:S(2)}) async-start(s8[15728640]{0:T(1024)(128)(4,1)} %bitcast.142), calls=%async_computation.9 | async-start | bytes 8388608
  362.0 21.3 %slice-start.1 = ((s8[15728640]{0:T(1024)(128)(4,1)}), s8[4194304]{0:T(1024)(128)(4,1)S(1)}, s32[]{:S(2)}) async-start(s8[15728640]{0:T(1024)(128)(4,1)} %bitcast.142), calls=%async_computation.10 | async-start | bytes 8388608
  370.4 12.9 %slice-start.2 = ((s8[15728640]{0:T(1024)(128)(4,1)}), s8[4194304]{0:T(1024)(128)(4,1)S(1)}, s32[]{:S(2)}) async-start(s8[15728640]{0:T(1024)(128)(4,1)} %bitcast.142), calls=%async_computation.11 | async-start | bytes 8388608
  370.4 14.0 %slice-start.3 = ((s8[15728640]{0:T(1024)(128)(4,1)}), s8[3145728]{0:T(1024)(128)(4,1)S(1)}, s32[]{:S(2)}) async-start(s8[15728640]{0:T(1024)(128)(4,1)} %bitcast.142), calls=%async_computation.12 | async-start | bytes 6291456
  402.1 3.3 copy-start.9
  405.4 4.5 copy-start.15
  415.0 8.0 %copy-start.2 = (bf16[256,1536]{1,0:T(8,128)(2,1)S(1)}, bf16[256,1536]{1,0:T(8,128)(2,1)}, u32[]{:S(2)}) copy-start(bf16[256,1536]{1,0:T(8,128)(2,1)} %param.15) | copy-start | bytes 2359300
  423.0 3.7 copy-start.24
  423.0 7.3 %slice-start.4 = ((s8[4718592]{0:T(1024)(128)(4,1)}), s8[4194304]{0:T(1024)(128)(4,1)S(1)}, s32[]{:S(2)}) async-start(s8[4718592]{0:T(1024)(128)(4,1)} %bitcast.187), calls=%async_computation.13 | async-start | bytes 8388608
  426.7 3.6 slice-start.5
  454.4 3.1 copy-start.16
  454.4 3.1 copy-start.22
  572.3 2.9 copy-start.28
  572.3 3.6 copy-start.26
  (19 other events, 26.6 us)
Sparse Core Ops, SparseCore 0:
  9.6 81.5 all-gather.5
  92.8 68.6 all-gather.3
  163.1 66.6 all-gather.7
  248.5 88.3 reduce-scatter.9
  346.2 88.4 reduce-scatter.11
  436.9 66.6 reduce-scatter.13

commit v5 on v4

--- a/solution.py
+++ b/solution.py
@@ -899,6 +899,38 @@
     )(out_rows, hidden, silu, slope, gate_t, up_t, down)
 
 
+def weight_grad_kernel(left, right, out):
+    for at, wide in spans(right.shape[1], 512):
+        out[:, at : at + wide] = lax.dot_general(
+            left[...],
+            right[:, at : at + wide],
+            (((0,), (0,)), ((), ())),
+            preferred_element_type=F32,
+        ).astype(out.dtype)
+
+
+def weight_grad(left, right):
+    rows, depth = left.shape
+    wide = right.shape[1]
+    tile = 256
+    return pl.pallas_call(
+        weight_grad_kernel,
+        grid=(depth // tile,),
+        out_shape=jax.ShapeDtypeStruct((depth, wide), BF16),
+        in_specs=[
+            pl.BlockSpec((rows, tile), lambda i: (0, i)),
+            pl.BlockSpec((rows, wide), lambda i: (0, 0)),
+        ],
+        out_specs=pl.BlockSpec((tile, wide), lambda i: (i, 0)),
+        cost_estimate=pl.CostEstimate(
+            flops=2 * rows * depth * wide,
+            bytes_accessed=2 * (rows * depth + rows * wide + depth * wide),
+            transcendentals=0,
+        ),
+        name="weight_grad",
+    )(left, right)
+
+
 def gather_row(block):
     return lax.all_gather(block, "row", axis=block.ndim - 1, tiled=True)
 
@@ -960,19 +992,23 @@
         pl.semaphore_wait(barrier, len(peers) + 2)
 
 
-def grid_gather_kernel(count, places, *refs):
-    ins, outs = refs[:count], refs[count : 2 * count]
-    send_sem, recv_sem, line_send, line_recv, own_sem = refs[2 * count :]
+def grid_gather_kernel(count, extra, places, *refs):
+    both_count = count + extra
+    ins, outs = refs[:both_count], refs[both_count : 2 * both_count]
+    send_sem, recv_sem, line_send, line_recv, own_sem = refs[2 * both_count :]
     place = lax.axis_index("row")
     chip, beside, above, across, core = plane_places()
     mine, partner, other = chip * 2 + core, chip * 2 + 1 - core, 1 - core
     to_x, to_y, far = beside * 2 + core, above * 2 + core, across * 2 + core
     every = range(count)
+    others = range(count, both_count)
     greet_grid((partner, to_x, to_y), place, places)
 
     def view(i, slot, line, part):
         size, wide = ins[i].shape
         spot = pl.ds(pl.multiple_of(line * wide, wide), wide)
+        if i >= count:
+            return outs[i].at[:, spot]
         if part is None:
             return outs[i].at[pl.ds(pl.multiple_of(slot * size, size), size), spot]
         half = size // 2
@@ -990,7 +1026,7 @@
             for i in every
         ]
 
-    def line_copies(line, sem_at, peer, own=False):
+    def line_copies(line, sem_at, peer, own=False, which=every):
         return [
             line_remote(
                 ins[i] if own else view(i, mine, line, None),
@@ -999,7 +1035,7 @@
                 line_recv.at[i, line],
                 peer,
             )
-            for i in every
+            for i in which
         ]
 
     def start(cs):
@@ -1058,16 +1094,32 @@
     @pl.when(place < places - 1)
     def _():
         start(line_copies(place, place, place + 1, True))
+        start(line_copies(place, place, place + 1, True, others))
 
     @pl.when(place > 0)
     def _():
         start(line_copies(place, places, place - 1, True))
+        start(line_copies(place, places, place - 1, True, others))
 
     first(place, True)
     own = [
-        pltpu.make_async_copy(ins[i], view(i, mine, place, None), own_sem.at[i]) for i in every
+        pltpu.make_async_copy(ins[i], view(i, mine, place, None), own_sem.at[i])
+        for i in range(both_count)
     ]
     start(own)
+
+    def pass_on(line):
+        @pl.when(line != place)
+        def _():
+            wait_recv(line_copies(line, line, place, False, others))
+
+        @pl.when((line < place) & (place < places - 1))
+        def _():
+            start(line_copies(line, line, place + 1, False, others))
+
+        @pl.when((line > place) & (place > 0))
+        def _():
+            start(line_copies(line, line, place - 1, False, others))
 
     def step(t, _):
         @pl.when((t >= 1) & (place - t >= 0))
@@ -1093,22 +1145,22 @@
             first(line)
 
         both(t - 1, second)
+        if extra:
+            both(t - 1, pass_on)
         both(t - 2, third)
         return 0
 
     lax.fori_loop(0, places + 2, step, 0)
 
+    everything = range(both_count)
+
     def finish(line, _):
         last(line)
-
-        @pl.when((line < place) & (place < places - 1))
-        def _():
-            for c in line_copies(line, line, place):
-                c.wait_send()
-
-        @pl.when((line > place) & (place > 0))
-        def _():
-            for c in line_copies(line, line, place):
+        relays = ((line < place) & (place < places - 1)) | ((line > place) & (place > 0))
+
+        @pl.when(relays)
+        def _():
+            for c in line_copies(line, line, place, False, everything):
                 c.wait_send()
 
         return 0
@@ -1117,41 +1169,42 @@
 
     @pl.when(place < places - 1)
     def _():
-        for c in line_copies(place, place, place):
+        for c in line_copies(place, place, place, False, everything):
             c.wait_send()
 
     @pl.when(place > 0)
     def _():
-        for c in line_copies(place, places, place):
+        for c in line_copies(place, places, place, False, everything):
             c.wait_send()
 
     for c in own:
         c.wait()
 
 
-def grid_gather(shards, ident):
-    count = len(shards)
+def grid_gather(shards, lines, ident):
+    count, extra = len(shards), len(lines)
     places, parts = lax.axis_size("row"), lax.axis_size("col")
     dma = pltpu.SemaphoreType.DMA
     anywhere = pl.BlockSpec(memory_space=pl.ANY)
     return pl.pallas_call(
-        functools.partial(grid_gather_kernel, count, places),
+        functools.partial(grid_gather_kernel, count, extra, places),
         out_shape=[
             jax.ShapeDtypeStruct((s.shape[0] * parts, s.shape[1] * places), s.dtype)
             for s in shards
-        ],
-        in_specs=[anywhere] * count,
-        out_specs=[anywhere] * count,
+        ]
+        + [jax.ShapeDtypeStruct((s.shape[0], s.shape[1] * places), s.dtype) for s in lines],
+        in_specs=[anywhere] * (count + extra),
+        out_specs=[anywhere] * (count + extra),
         scratch_shapes=[
             dma((count, places, 9)),
             dma((count, places, 9)),
-            dma((count, places + 1)),
-            dma((count, places)),
-            dma((count,)),
+            dma((count + extra, places + 1)),
+            dma((count + extra, places)),
+            dma((count + extra,)),
         ],
         compiler_params=pltpu.CompilerParams(collective_id=ident, has_side_effects=True),
         name="grid_gather",
-    )(*shards)
+    )(*shards, *lines)
 
 
 def grid_scatter_kernel(count, places, *refs):
@@ -1444,13 +1497,12 @@
     )(*fulls)
 
 
-def gather_weights(blocks, ident):
+def gather_weights(blocks, lines, ident):
     places = lax.axis_size("row")
     if lax.axis_size("col") == 8 and places > 1 and blocks[0].shape[1] % 128 == 0:
-        return grid_gather(blocks, ident)
-    return [
-        full[0] for full in gather_col([gather_row(block)[None] for block in blocks], ident)
-    ]
+        return grid_gather(blocks, lines, ident)
+    fulls = gather_col([gather_row(block)[None] for block in blocks], ident)
+    return [full[0] for full in fulls] + [gather_row(line) for line in lines]
 
 
 def scatter_weights(fulls, ident):
@@ -1492,16 +1544,17 @@
     small_sizes = [member.shape[0] for member in smalls]
     packed_small = jnp.concatenate(smalls)
     packed_small = jnp.pad(packed_small, (0, k_own * depth_own - packed_small.shape[0]))
-    query_t, output_t, key_t, value_t, small_t = gather_weights(
-        [
-            q_weight.T,
-            o_weight.T,
-            k_weight.T,
-            v_weight.T,
-            packed_small.reshape(k_own, depth_own),
-        ],
+    query_t, key_t, value_t, small_t, output_line = gather_weights(
+        [q_weight.T, k_weight.T, v_weight.T, packed_small.reshape(k_own, depth_own)],
+        [o_weight.T],
         1,
     )
+    gate_own, up_own, down_own, small_t = lax.optimization_barrier(
+        (gate_weight.T, up_weight.T, down_weight, small_t)
+    )
+    gate_t = gather_row(gate_own)
+    up_t = gather_row(up_own)
+    down_block = gather_row(down_own)
     small_flat = small_t.reshape(col_parts, k_own, row_parts, depth_own)
     small_flat = small_flat.transpose(2, 0, 1, 3).reshape(row_parts * col_parts, -1)
     small_full, offset = [], 0
@@ -1510,9 +1563,6 @@
         offset += size
     query_offset, key_offset, value_offset, first_gain, second_gain = small_full
 
-    gate_t = gather_row(gate_weight.T)
-    up_t = gather_row(up_weight.T)
-    down_block = gather_row(down_weight)
 
     own_rows = hidden_in.shape[0]
     row_tokens = own_rows * col_parts
@@ -1532,7 +1582,9 @@
     queries = rotate_pairs(query_base.reshape(own_rows, HQ, HD), cosines, sines).astype(BF16)
     keys_own = rotate_pairs(key_base.reshape(own_rows, KVH, HD), cosines, sines).astype(BF16)
     both_own = jnp.concatenate([keys_own.reshape(own_rows, KVH * HD), value_own], axis=1)
-    both_all = gather_col([both_own[None]], 2)[0][0]
+    both_all, output_t = (
+        member[0] for member in gather_col([both_own[None], output_line[None]], 2)
+    )
     window = min(own_rows + MAXLEN, row_tokens)
     window_start = jnp.clip(col_place * own_rows - MAXLEN, 0, row_tokens - window)
     key_slots = window_start + jnp.arange(window, dtype=jnp.int32)
@@ -1572,7 +1624,7 @@
         silu_gate = gate_act * sigmoid_gate
         slope = up_act * sigmoid_gate * (1.0 + gate_act * (1.0 - sigmoid_gate))
         hidden = (silu_gate * up_act).astype(BF16)
-    down_grad = dot_tn(out_rows, hidden).astype(BF16)
+    down_grad = weight_grad(out_rows, hidden)
     down_grad, out_rows = lax.optimization_barrier((down_grad, out_rows))
     down_grad_own = scatter_row(down_grad)
     if kernels:
@@ -1588,12 +1640,11 @@
         normed_grad, branch_out = (
             member[0] for member in scatter_col([normed_part[None], branch_part[None]], 4)
         )
-    gate_grad = dot_tn(normed_rows, gate_grad_act).astype(BF16)
-    up_grad = dot_tn(normed_rows, up_grad_act).astype(BF16)
-    gate_grad, up_grad, normed_grad = lax.optimization_barrier(
-        (gate_grad, up_grad, normed_grad)
-    )
+    gate_grad = weight_grad(normed_rows, gate_grad_act)
+    gate_grad, up_grad_act = lax.optimization_barrier((gate_grad, up_grad_act))
     gate_grad_own = scatter_row(gate_grad)
+    up_grad = weight_grad(normed_rows, up_grad_act)
+    up_grad, normed_grad = lax.optimization_barrier((up_grad, normed_grad))
     up_grad_own = scatter_row(up_grad)
     layer_out = residual + branch_out
     second_gain_grad = jnp.sum(normed_grad * second_unit, axis=0)

time: 595 us -> 560 us (0.941)
  matrix products: 109 us -> 62.9 us
  waiting for transfers between devices: 2.15 us -> 43.8 us
  local copies, waits for them, and re-layouts: 63.7 us -> 47 us
    all_gather x3, waiting for transfers between devices: 0.04 us -> 42.3 us  [gather_row(): return lax.all_gather(block, 'row', axis=block.ndim - 1, tiled=True)]
    dot_general x7 -> x4, matrix products: 46.6 us -> 10 us  [dot_tn(): lax.dot_general(left, right, (((0,), (0,)), ((), ())), preferred_element_...]
    pallas_call x1, Pallas kernels: 15.2 us -> 35.5 us  [plane_gather(): pl.pallas_call(functools.partial(plane_gather_kernel, count), out_shape=o...]
    pallas_call x1, Pallas kernels: 93.8 us -> 76.4 us  [grid_scatter(): pl.pallas_call(functools.partial(grid_scatter_kernel, count, places), out...]
    unnamed x101 -> x116, local copies, waits for them, and re-layouts: 31 us -> 19.5 us
    pallas_call x1 -> x4, Pallas kernels: 83.6 us -> 76.9 us  [the longest x3 39.3 us: weight_grad(): pl.pallas_call(weight_grad_kernel, grid=(depth // tile,), out_shape=jax.S...]
  transfers between devices with their start and end apart: 6 -> 6, of which waited for: 0 -> 2; matrix products, arithmetic and copies ran while one was open for 34% -> 23% of each run, Pallas kernels for 60% -> 56%
where the time goes in v5:
time: 560 us; the launch traced here: 553 us
  Pallas kernels  346 us (62%)
  matrix products  62.9 us (11%)
  local copies, waits for them, and re-layouts  47 us (8%)
  waiting for transfers between devices  43.8 us (8%)
  other arithmetic  37.7 us (7%)
  between operations  15.4 us (3%)
    pallas_call x1, Pallas kernels, grid_scatter(): pl.pallas_call(functools.partial(grid_scatter_kernel, count, places), out...  76.4 us
    pallas_call x1, Pallas kernels, ffn_backward(): pl.pallas_call(ffn_backward_kernel, out_shape=[jax.ShapeDtypeStruct((tota...  69.7 us
    all_gather x3, waiting for transfers between devices, gather_row(): return lax.all_gather(block, 'row', axis=block.ndim - 1, tiled=True)  42.3 us
    pallas_call x3, Pallas kernels, weight_grad(): pl.pallas_call(weight_grad_kernel, grid=(depth // tile,), out_shape=jax.S...  39.3 us
    pallas_call x1, Pallas kernels, grid_gather(): pl.pallas_call(functools.partial(grid_gather_kernel, count, extra, places...  37.6 us
    pallas_call x1, Pallas kernels, ffn_up(): pl.pallas_call(ffn_up_kernel, out_shape=[jax.ShapeDtypeStruct((rows * 8,...  35.9 us
    pallas_call x1, Pallas kernels, ffn_gate(): pl.pallas_call(ffn_gate_kernel, out_shape=[jax.ShapeDtypeStruct((rows * 8...  35.8 us
    pallas_call x1, Pallas kernels, plane_gather(): pl.pallas_call(functools.partial(plane_gather_kernel, count), out_shape=o...  35.5 us
  transfers between devices with their start and end apart: 6, of which 2 were waited for; matrix products, arithmetic and copies ran while one was open for 23% of the time, Pallas kernels for 56%

profile of v5, /device:TPU:8, one launch (start us, length us, event | category | flops | bytes accessed | tf_op | source)
XLA Modules:
  0.0 552.8 jit_solution(5554320429406409606)
XLA Ops:
  7.2 3.4 concatenate.42
  11.3 37.6 %grid_gather.1 = (bf16[1536,1536]{1,0:T(8,128)(2,1)}, bf16[256,1536]{1,0:T(8,128)(2,1)}, bf16[256,1536]{1,0:T(8,128)(2,1)}, bf16[256,1536]{1,0:T(8,128)(2,1)}, bf16[192,1536]{1,0:T(8,128)(2,1)}) custom-call(bf16[192,384]{1,0:T(8,128)(2,1)} %bitcast.180, bf16[32,384]{1,0:T(8,128)(2,1)} %bitcast.184, bf16[32,384]{1,0:T(8,128)(2,1)} %bitcast.185, ...), custom_call_target="tpu_custom_call" | custom-call | tf_op jit(solution)/shard_map/grid_gather/pallas_call | solution.py:1189
  55.9 35.5 %plane_gather.1 = (bf16[1,2048,512]{2,1,0:T(8,128)(2,1)}, bf16[1,1536,1536]{2,1,0:T(8,128)(2,1)}) custom-call(bf16[1,256,512]{2,1,0:T(8,128)(2,1)} %maximum_bitcast_fusion.refs_0_, bf16[1,192,1536]{2,1,0:T(8,128)(2,1)} %bitcast.175), custom_call_target="tpu_custom_call" | custom-call | tf_op jit(solution)/shard_map/plane_gather/pallas_call | solution.py:180
  93.4 5.1 convolution_add_fusion.2
  102.5 6.8 %fusion.72 = (f32[2,6,256]{2,1,0:T(8,128)S(1)}, f32[2,6,256,1280]{2,3,1,0:T(8,128)}) fusion(bf16[1280,2,128,1]{0,2,3,1:T(8,128)(2,1)S(1)} %bitcast.152, bf16[256,2,6,128]{0,3,2,1:T(8,128)(2,1)S(1)} %fusion.41, pred[256,1280]{0,1:T(8,128)(4,1)S(1)} %compare_and_fusion), kind=kOutput, calls=%fused_computation.118 | convolution fusion | flops 1018426368 | bytes 17510400 | tf_op jit(solution)/shard_map/tkgd,skd->kgts/dot_general | solution.py:72
  109.6 7.7 %fusion.3 = f32[2,6,256]{2,1,0:T(8,128)S(1)} fusion(f32[2,6,256,1280]{2,3,1,0:T(8,128)} %get-tuple-element.163, f32[2,6,256]{2,1,0:T(8,128)S(1)} %get-tuple-element.162), kind=kLoop, calls=%fused_computation.9 | loop fusion | flops 7861248 | bytes 15753216 | tf_op jit(solution)/shard_map/reduce_sum | solution.py:1602
  117.3 7.4 %fusion.42 = bf16[2,128,6,256]{3,1,2,0:T(8,128)(2,1)S(1)} fusion(bf16[1280,2,128,1]{0,2,3,1:T(8,128)(2,1)S(1)} %bitcast.165, f32[2,6,256,1280]{2,3,1,0:T(8,128)} %get-tuple-element.163, f32[2,6,256]{2,1,0:T(8,128)S(1)} %fusion.3, f32[2,6,256]{2,1,0:T(8,128)S(1)} %get-tuple-element.162), kind=kOutput, calls=%fused_computation.59 | convolution fusion | flops 1018822656 | bytes 17195008 | tf_op jit(solution)/shard_map/kgts,skd->tkgd/dot_general | solution.py:1605
  127.4 35.8 %ffn_gate.1 = (bf16[2048,1536]{1,0:T(8,128)(2,1)}, f32[2048,1120]{1,0:T(8,128)}) custom-call(bf16[256,1536]{1,0:T(8,128)(2,1)} %multiply_convert_fusion.1.normed, bf16[1120,1536]{1,0:T(8,128)(2,1)} %all-gather.6.cloned.1.call-done.gate_t), custom_call_target="tpu_custom_call" | custom-call | tf_op jit(solution)/shard_map/ffn_gate/pallas_call | solution.py:494
  163.2 23.0 %all-gather.4.cloned.1.call-done.up_t = bf16[1120,1536]{1,0:T(8,128)(2,1)} async-done(((bf16[1120,384]{1,0:T(8,128)(2,1)}), bf16[1120,1536]{1,0:T(8,128)(2,1)}) %all-gather.4.cloned.1.call-update) | async-done | bytes 3440656 | tf_op jit(solution)/shard_map/all_gather | solution.py:935
  186.2 35.9 %ffn_up.1 = (bf16[2048,1536]{1,0:T(8,128)(2,1)}, bf16[2048,1120]{1,0:T(8,128)(2,1)}, bf16[2048,1120]{1,0:T(8,128)(2,1)}, bf16[2048,1120]{1,0:T(8,128)(2,1)}) custom-call(bf16[256,1536]{1,0:T(8,128)(2,1)} %cotangent.1, bf16[1120,1536]{1,0:T(8,128)(2,1)} %all-gather.4.cloned.1.call-done.up_t, bf16[2048,1536]{1,0:T(8,128)(2,1)} %get-tuple-element.60.normed_rows.left, ...), custom_call_target="tpu_custom_call" | custom-call | tf_op jit(solution)/shard_map/ffn_up/pallas_call | solution.py:624
  222.1 13.0 %weight_grad.3 = bf16[1536,1120]{1,0:T(8,128)(2,1)} custom-call(bf16[2048,1536]{1,0:T(8,128)(2,1)} %get-tuple-element.64.left.out_rows, bf16[2048,1120]{1,0:T(8,128)(2,1)} %get-tuple-element.63.right.hidden), custom_call_target="tpu_custom_call" | custom-call | flops 7046430720 | bytes 14319616 | tf_op jit(solution)/shard_map/weight_grad/pallas_call | solution.py:916
  235.2 19.3 %all-gather.8.cloned.1.call-done.down = bf16[1120,1536]{1,0:T(8,128)(2,1)} async-done(((bf16[1120,384]{1,0:T(8,128)(2,1)}), bf16[1120,1536]{1,0:T(8,128)(2,1)}) %all-gather.8.cloned.1.call-update) | async-done | bytes 3440656 | tf_op jit(solution)/shard_map/all_gather | solution.py:935
  254.5 69.7 %ffn_backward.1 = (bf16[2048,1120]{1,0:T(8,128)(2,1)}, bf16[2048,1120]{1,0:T(8,128)(2,1)}, f32[256,1536]{1,0:T(8,128)}, f32[256,1536]{1,0:T(8,128)}) custom-call(bf16[2048,1536]{1,0:T(8,128)(2,1)} %get-tuple-element.64.left.out_rows, bf16[2048,1120]{1,0:T(8,128)(2,1)} %get-tuple-element.63.right.hidden, bf16[2048,1120]{1,0:T(8,128)(2,1)} %get-tuple-element.65.silu, ...), custom_call_target="tpu_custom_call" | custom-call | tf_op jit(solution)/shard_map/ffn_backward/pallas_call | solution.py:873
  324.2 12.9 %weight_grad.4 = bf16[1536,1120]{1,0:T(8,128)(2,1)} custom-call(bf16[2048,1536]{1,0:T(8,128)(2,1)} %get-tuple-element.60.normed_rows.left, bf16[2048,1120]{1,0:T(8,128)(2,1)} %get-tuple-element.69.right), custom_call_target="tpu_custom_call" | custom-call | flops 7046430720 | bytes 14319616 | tf_op jit(solution)/shard_map/weight_grad/pallas_call | solution.py:916
  337.2 13.4 %weight_grad.5 = bf16[1536,1120]{1,0:T(8,128)(2,1)} custom-call(bf16[2048,1536]{1,0:T(8,128)(2,1)} %get-tuple-element.60.normed_rows.left, bf16[2048,1120]{1,0:T(8,128)(2,1)} %get-tuple-element.71.right), custom_call_target="tpu_custom_call" | custom-call | flops 7046430720 | bytes 14319616 | tf_op jit(solution)/shard_map/weight_grad/pallas_call | solution.py:916
  352.6 3.1 multiply_add_fusion
  359.5 12.7 %fusion = (f32[2,6,256]{2,1,0:T(8,128)S(1)}, f32[2,1280,256,6]{2,1,3,0:T(8,128)}) fusion(f32[2,6,256,1280]{2,3,1,0:T(8,128)} %get-tuple-element.163, f32[2,6,256]{2,1,0:T(8,128)S(1)} %log_add_fusion, bf16[1280,2,128,1]{0,2,3,1:T(8,128)(2,1)S(1)} %bitcast.166, bf16[256,2,6,128]{0,3,2,1:T(8,128)(2,1)S(1)} %bitcast.148), kind=kOutput, calls=%fused_computation.2 | convolution fusion | flops 1018426368 | bytes 32923648 | tf_op jit(solution)/shard_map/tkgd,skd->kgts/dot_general | solution.py:1660
  375.0 7.6 %fusion.2 = bf16[2,6,256,1280]{2,3,1,0:T(8,128)(2,1)S(1)} fusion(f32[2,1280,256,6]{2,1,3,0:T(8,128)} %get-tuple-element.167, f32[2,6,256,1280]{2,3,1,0:T(8,128)S(1)} %bitcast.144, f32[2,6,256]{2,1,0:T(8,128)S(1)} %get-tuple-element.166, f32[2,6,256]{2,1,0:T(8,128)S(1)} %log_add_fusion), kind=kLoop, calls=%fused_computation.4 | loop fusion | flops 15728640 | bytes 39346176 | tf_op jit(solution)/shard_map/convert_element_type | solution.py:1668
  382.6 3.1 copy-done
  385.7 3.5 fusion.23
  389.2 3.7 fusion.20
  394.0 4.4 multiply_convert_fusion
  407.5 8.1 %dynamic_update_slice.3 = bf16[2048,512]{1,0:T(8,128)(2,1)} dynamic-update-slice(bf16[2048,512]{1,0:T(8,128)(2,1)} %broadcast_in_dim.83, bf16[1280,512]{1,0:T(8,128)(2,1)} %pad_maximum_fusion, s32[]{:T(128)S(6)} %min.4, s32[]{:T(128)} %constant.42.clone.1) | dynamic-update-slice | bytes 2621444 | tf_op jit(solution)/shard_map/dynamic_update_slice | solution.py:1680
  415.6 3.7 convolution_convert_fusion.1.refs_0_
  419.3 3.6 convolution_convert_fusion.refs_1_
  422.9 2.5 fusion.73
  425.5 15.6 %plane_scatter.1 = f32[1,256,512]{2,1,0:T(8,128)} custom-call(bf16[1,2048,512]{2,1,0:T(8,128)(2,1)} %bitcast.147), custom_call_target="tpu_custom_call" | custom-call | tf_op jit(solution)/shard_map/plane_scatter/pallas_call | solution.py:335
  452.2 76.4 %grid_scatter.1 = (f32[192,384]{1,0:T(8,128)}, f32[192,384]{1,0:T(8,128)}, f32[32,384]{1,0:T(8,128)}, f32[32,384]{1,0:T(8,128)}, f32[32,384]{1,0:T(8,128)}) custom-call(bf16[1536,1536]{1,0:T(8,128)(2,1)} %convolution_convert_fusion.1.refs_0_, bf16[1536,1536]{1,0:T(8,128)(2,1)} %convolution_convert_fusion.refs_1_, ...), custom_call_target="tpu_custom_call" | custom-call | tf_op jit(solution)/shard_map/grid_scatter/pallas_call | solution.py:1479
  530.9 2.5 convert_bitcast_fusion
  533.4 2.7 copy.101
  537.3 3.0 fusion.37
  540.3 2.5 copy.100
  (212 shorter events, 52.2 us)
Async XLA Ops:
  7.2 120.2 %all-gather.6.cloned.1.call-start = ((), (), s32[]{:S(2)}) async-start(), calls=%async_computation.4 | async-start | bytes 4300800 | tf_op jit(solution)/shard_map/all_gather | solution.py:935
  48.9 137.3 %all-gather.4.cloned.1.call-start = ((), (), s32[]{:S(2)}) async-start(), calls=%async_computation.3 | async-start | bytes 4300800 | tf_op jit(solution)/shard_map/all_gather | solution.py:935
  49.7 204.8 %all-gather.8.cloned.1.call-start = ((), (), s32[]{:S(2)}) async-start(), calls=%async_computation.5 | async-start | bytes 4300800 | tf_op jit(solution)/shard_map/all_gather | solution.py:935
  50.4 375.0 %reduce-scatter.4.cloned.1.call-start = ((), (), s32[]{:S(2)}) async-start(), calls=%async_computation.6 | async-start | bytes 4423680 | tf_op jit(solution)/shard_map/reduce_scatter | solution.py:939
  51.3 42.1 %copy-start.27 = (f32[1536]{0:T(1024)}, f32[1536]{0:T(1024)S(1)}, u32[]{:S(2)}) copy-start(f32[1536]{0:T(1024)S(1)} %reshape.307) | copy-start | bytes 18436
  52.0 41.4 %copy-start.37 = (f32[256]{0:T(256)}, f32[256]{0:T(256)S(1)}, u32[]{:S(2)}) copy-start(f32[256]{0:T(256)S(1)} %add_rsqrt_fusion.1) | copy-start | bytes 3076
  93.4 9.1 %copy-start.8 = (bf16[1280,256]{0,1:T(8,128)(2,1)}, bf16[1280,256]{0,1:T(8,128)(2,1)S(1)}, u32[]{:S(2)}) copy-start(bf16[1280,256]{0,1:T(8,128)(2,1)S(1)} %copy.84) | copy-start | bytes 1966084
  102.4 6.8 %copy-start.4 = (bf16[256,2,6,128]{0,3,2,1:T(8,128)(2,1)}, bf16[256,2,6,128]{0,3,2,1:T(8,128)(2,1)S(1)}, u32[]{:S(2)}) copy-start(bf16[256,2,6,128]{0,3,2,1:T(8,128)(2,1)S(1)} %fusion.41) | copy-start | bytes 2359300
  109.5 7.8 %copy-start.12 = (bf16[1280,256]{0,1:T(8,128)(2,1)}, bf16[1280,256]{0,1:T(8,128)(2,1)S(1)}, u32[]{:S(2)}) copy-start(bf16[1280,256]{0,1:T(8,128)(2,1)S(1)} %copy.83) | copy-start | bytes 1966084
  109.6 16.7 %copy-start.29 = (f32[1536]{0:T(1024)}, f32[1536]{0:T(1024)S(1)}, u32[]{:S(2)}) copy-start(f32[1536]{0:T(1024)S(1)} %reshape.311) | copy-start | bytes 18436
  109.6 15.1 %slice-start.6 = ((s8[4718592]{0:T(1024)(128)(4,1)}), s8[524288]{0:T(1024)(128)(4,1)S(1)}, s32[]{:S(2)}) async-start(s8[4718592]{0:T(1024)(128)(4,1)} %bitcast.191), calls=%async_computation.15 | async-start | bytes 1048576
  117.3 7.4 %copy-start.2 = (bf16[256,1536]{1,0:T(8,128)(2,1)S(1)}, bf16[256,1536]{1,0:T(8,128)(2,1)}, u32[]{:S(2)}) copy-start(bf16[256,1536]{1,0:T(8,128)(2,1)} %param.15) | copy-start | bytes 2359300
  117.3 7.4 %slice-start.7 = ((s8[4718592]{0:T(1024)(128)(4,1)}), s8[4194304]{0:T(1024)(128)(4,1)S(1)}, s32[]{:S(2)}) async-start(s8[4718592]{0:T(1024)(128)(4,1)} %bitcast.191), calls=%async_computation.16 | async-start | bytes 8388608
  126.3 36.9 %copy-start.34 = (f32[256]{0:T(256)}, f32[256]{0:T(256)S(1)}, u32[]{:S(2)}) copy-start(f32[256]{0:T(256)S(1)} %add_rsqrt_fusion) | copy-start | bytes 3076
  235.2 214.3 %reduce-scatter.6.cloned.1.call-start = ((), (), s32[]{:S(2)}) async-start(), calls=%async_computation.7 | async-start | bytes 4423680 | tf_op jit(solution)/shard_map/reduce_scatter | solution.py:939
  337.1 13.4 %copy-start.6 = (f32[256,1536]{1,0:T(8,128)S(1)}, f32[256,1536]{1,0:T(8,128)}, u32[]{:S(2)}) copy-start(f32[256,1536]{1,0:T(8,128)} %get-tuple-element.73) | copy-start | bytes 4718596
  337.2 203.2 %reduce-scatter.8.cloned.1.call-start = ((), (), s32[]{:S(2)}) async-start(), calls=%async_computation.8 | async-start | bytes 4423680 | tf_op jit(solution)/shard_map/reduce_scatter | solution.py:939
  350.6 5.1 slice-start.8
  359.4 12.8 %slice-start = ((s8[15728640]{0:T(1024)(128)(4,1)}), s8[4194304]{0:T(1024)(128)(4,1)S(1)}, s32[]{:S(2)}) async-start(s8[15728640]{0:T(1024)(128)(4,1)} %bitcast.143), calls=%async_computation.9 | async-start | bytes 8388608
  359.5 12.8 %slice-start.1 = ((s8[15728640]{0:T(1024)(128)(4,1)}), s8[4194304]{0:T(1024)(128)(4,1)S(1)}, s32[]{:S(2)}) async-start(s8[15728640]{0:T(1024)(128)(4,1)} %bitcast.143), calls=%async_computation.10 | async-start | bytes 8388608
  359.5 14.7 %slice-start.2 = ((s8[15728640]{0:T(1024)(128)(4,1)}), s8[4194304]{0:T(1024)(128)(4,1)S(1)}, s32[]{:S(2)}) async-start(s8[15728640]{0:T(1024)(128)(4,1)} %bitcast.143), calls=%async_computation.11 | async-start | bytes 8388608
  359.5 15.6 %slice-start.3 = ((s8[15728640]{0:T(1024)(128)(4,1)}), s8[3145728]{0:T(1024)(128)(4,1)S(1)}, s32[]{:S(2)}) async-start(s8[15728640]{0:T(1024)(128)(4,1)} %bitcast.143), calls=%async_computation.12 | async-start | bytes 6291456
  375.0 10.7 %copy-start.5 = (bf16[256,2,6,128]{0,3,2,1:T(8,128)(2,1)S(1)}, bf16[256,2,6,128]{0,3,2,1:T(8,128)(2,1)}, u32[]{:S(2)}) copy-start(bf16[256,2,6,128]{0,3,2,1:T(8,128)(2,1)} %copy-done.4) | copy-start | bytes 2359300
  407.5 8.1 %copy-start.3 = (bf16[256,1536]{1,0:T(8,128)(2,1)S(1)}, bf16[256,1536]{1,0:T(8,128)(2,1)}, u32[]{:S(2)}) copy-start(bf16[256,1536]{1,0:T(8,128)(2,1)} %param.15) | copy-start | bytes 2359300
  407.5 8.1 %copy-start.28 = (f32[1536]{0:T(1024)S(1)}, f32[1536]{0:T(1024)}, u32[]{:S(2)}) copy-start(f32[1536]{0:T(1024)} %copy-done.27) | copy-start | bytes 18436
  407.5 8.1 %copy-start.38 = (f32[256]{0:T(256)S(1)}, f32[256]{0:T(256)}, u32[]{:S(2)}) copy-start(f32[256]{0:T(256)} %copy-done.37) | copy-start | bytes 3076
  415.6 3.7 copy-start.24
  415.6 7.3 %slice-start.4 = ((s8[4718592]{0:T(1024)(128)(4,1)}), s8[4194304]{0:T(1024)(128)(4,1)S(1)}, s32[]{:S(2)}) async-start(s8[4718592]{0:T(1024)(128)(4,1)} %bitcast.189), calls=%async_computation.13 | async-start | bytes 8388608
  425.5 17.3 %copy-start.16 = (f32[256,128]{1,0:T(8,128)S(1)}, f32[256,128]{1,0:T(8,128)}, u32[]{:S(2)}) copy-start(f32[256,128]{1,0:T(8,128)} %copy-done.15) | copy-start | bytes 393220
  452.2 77.2 %copy-start.17 = (bf16[384,1120]{1,0:T(8,128)(2,1)S(1)}, bf16[384,1120]{1,0:T(8,128)(2,1)}, u32[]{:S(2)}) copy-start(bf16[384,1120]{1,0:T(8,128)(2,1)} %reduce-scatter.6.cloned.1.call-done) | copy-start | bytes 2580484
  540.3 3.9 copy-start.31
  540.3 4.5 copy-start.25
  (27 other events, 49.1 us)
Sparse Core Ops, SparseCore 0:
  49.0 68.8 all-gather.5
  119.6 66.6 all-gather.3
  187.8 66.6 all-gather.7
  256.7 66.4 reduce-scatter.3
  337.3 65.4 reduce-scatter.5
  404.9 66.6 reduce-scatter.7

commit v6 on v5

--- a/solution.py
+++ b/solution.py
@@ -66,11 +66,6 @@
 
 def rounded_wide(values):
     return lax.optimization_barrier(values.astype(BF16)).astype(F32)
-
-
-def masked_scores(query_heads, keys_window, visible, score_scale):
-    scores = jnp.einsum("tkgd,skd->kgts", query_heads, keys_window, preferred_element_type=F32)
-    return jnp.where(visible, scores * score_scale, -jnp.inf)
 
 
 def plane_places():
@@ -931,6 +926,129 @@
     )(left, right)
 
 
+def fill_mask(places, starts, mask):
+    rows, window = mask.shape
+    keys = places[0] + lax.broadcasted_iota(jnp.int32, (rows, window), 1)
+    slots = places[1] + lax.broadcasted_iota(jnp.int32, (rows, window), 0)
+    mask[...] = jnp.where((keys >= starts[...]) & (keys <= slots), 0.0, -jnp.inf)
+
+
+def head_probs(query, keys, mask, score_scale):
+    scores = dot_nt(query[...], keys[...]) * score_scale + mask[...]
+    expanded = jnp.exp(scores - jnp.max(scores, axis=-1, keepdims=True))
+    return expanded * (1.0 / jnp.sum(expanded, axis=-1, keepdims=True))
+
+
+def attention_forward_kernel(score_scale, places, starts, query, keys, values, mixed, mask):
+    @pl.when(pl.program_id(0) == 0)
+    def _():
+        fill_mask(places, starts, mask)
+
+    probs = head_probs(query, keys, mask, score_scale)
+    mixed[...] = dot_nn(probs.astype(BF16), values[...]).astype(BF16)
+
+
+def attention_backward_kernel(
+    score_scale,
+    group,
+    places,
+    starts,
+    query,
+    cotangent,
+    keys,
+    values,
+    query_grad,
+    both_grad,
+    mask,
+    key_acc,
+    value_acc,
+):
+    head = pl.program_id(0)
+    window, wide = keys.shape
+
+    @pl.when(head == 0)
+    def _():
+        fill_mask(places, starts, mask)
+        both_grad[...] = jnp.zeros(both_grad.shape, both_grad.dtype)
+
+    @pl.when(head % group == 0)
+    def _():
+        key_acc[...] = jnp.zeros(key_acc.shape, F32)
+        value_acc[...] = jnp.zeros(value_acc.shape, F32)
+
+    probs = head_probs(query, keys, mask, score_scale)
+    prob_grad = dot_nt(cotangent[...], values[...])
+    value_acc[...] += dot_tn(probs.astype(BF16), cotangent[...])
+    centre = jnp.sum(probs * prob_grad, axis=-1, keepdims=True)
+    score_grad = (probs * (prob_grad - centre)).astype(BF16)
+    query_grad[...] = (dot_nn(score_grad, keys[...]) * score_scale).astype(BF16)
+    key_acc[...] += dot_tn(score_grad, query[...])
+
+    @pl.when(head % group == group - 1)
+    def _():
+        rows = pl.ds(pl.multiple_of(places[0], 128), window)
+        half = both_grad.shape[1] // 2
+        at = head // group * wide
+        both_grad[rows, pl.ds(pl.multiple_of(at, wide), wide)] = (
+            key_acc[...] * score_scale
+        ).astype(BF16)
+        both_grad[rows, pl.ds(pl.multiple_of(half + at, wide), wide)] = value_acc[...].astype(
+            BF16
+        )
+
+
+def attention_specs(rows, window, wide, group, kv_heads):
+    smem = pl.BlockSpec(memory_space=pltpu.SMEM)
+    starts = pl.BlockSpec((rows, 1), lambda h: (0, 0))
+    head = pl.BlockSpec((rows, wide), lambda h: (0, h))
+    keys = pl.BlockSpec((window, wide), lambda h: (0, h // group))
+    values = pl.BlockSpec((window, wide), lambda h: (0, kv_heads + h // group))
+    return smem, starts, head, keys, values
+
+
+def attention_forward(places, starts, queries, both_window, wide, kv_heads):
+    rows, window = queries.shape[0], both_window.shape[0]
+    heads = queries.shape[1] // wide
+    smem, first, head, keys, values = attention_specs(
+        rows, window, wide, heads // kv_heads, kv_heads
+    )
+    return pl.pallas_call(
+        functools.partial(attention_forward_kernel, 1.0 / math.sqrt(wide)),
+        grid=(heads,),
+        out_shape=jax.ShapeDtypeStruct(queries.shape, BF16),
+        in_specs=[smem, first, head, keys, values],
+        out_specs=head,
+        scratch_shapes=[pltpu.VMEM((rows, window), F32)],
+        name="attention_forward",
+    )(places, starts, queries, both_window, both_window)
+
+
+def attention_backward(
+    places, starts, queries, cotangent, both_window, wide, kv_heads, row_tokens
+):
+    rows, window = queries.shape[0], both_window.shape[0]
+    heads = queries.shape[1] // wide
+    group = heads // kv_heads
+    smem, first, head, keys, values = attention_specs(rows, window, wide, group, kv_heads)
+    full = (row_tokens, 2 * kv_heads * wide)
+    return pl.pallas_call(
+        functools.partial(attention_backward_kernel, 1.0 / math.sqrt(wide), group),
+        grid=(heads,),
+        out_shape=[
+            jax.ShapeDtypeStruct(queries.shape, BF16),
+            jax.ShapeDtypeStruct(full, BF16),
+        ],
+        in_specs=[smem, first, head, head, keys, values],
+        out_specs=[head, pl.BlockSpec(full, lambda h: (0, 0))],
+        scratch_shapes=[
+            pltpu.VMEM((rows, window), F32),
+            pltpu.VMEM((window, wide), F32),
+            pltpu.VMEM((window, wide), F32),
+        ],
+        name="attention_backward",
+    )(places, starts, queries, cotangent, both_window, both_window)
+
+
 def gather_row(block):
     return lax.all_gather(block, "row", axis=block.ndim - 1, tiled=True)
 
@@ -1002,7 +1120,7 @@
     to_x, to_y, far = beside * 2 + core, above * 2 + core, across * 2 + core
     every = range(count)
     others = range(count, both_count)
-    greet_grid((partner, to_x, to_y), place, places)
+    greet_grid((partner, to_x, to_y) if count else (), place, places)
 
     def view(i, slot, line, part):
         size, wide = ins[i].shape
@@ -1196,8 +1314,8 @@
         in_specs=[anywhere] * (count + extra),
         out_specs=[anywhere] * (count + extra),
         scratch_shapes=[
-            dma((count, places, 9)),
-            dma((count, places, 9)),
+            dma((max(count, 1), places, 9)),
+            dma((max(count, 1), places, 9)),
             dma((count + extra, places + 1)),
             dma((count + extra, places)),
             dma((count + extra,)),
@@ -1497,12 +1615,11 @@
     )(*fulls)
 
 
-def gather_weights(blocks, lines, ident):
+def gather_lines(lines, ident):
     places = lax.axis_size("row")
-    if lax.axis_size("col") == 8 and places > 1 and blocks[0].shape[1] % 128 == 0:
-        return grid_gather(blocks, lines, ident)
-    fulls = gather_col([gather_row(block)[None] for block in blocks], ident)
-    return [full[0] for full in fulls] + [gather_row(line) for line in lines]
+    if lax.axis_size("col") == 8 and places > 1 and lines[0].shape[1] % 128 == 0:
+        return grid_gather([], lines, ident)
+    return [gather_row(line) for line in lines]
 
 
 def scatter_weights(fulls, ident):
@@ -1544,13 +1661,21 @@
     small_sizes = [member.shape[0] for member in smalls]
     packed_small = jnp.concatenate(smalls)
     packed_small = jnp.pad(packed_small, (0, k_own * depth_own - packed_small.shape[0]))
-    query_t, key_t, value_t, small_t, output_line = gather_weights(
-        [q_weight.T, k_weight.T, v_weight.T, packed_small.reshape(k_own, depth_own)],
-        [o_weight.T],
+    *plane_lines, output_line = gather_lines(
+        [
+            q_weight.T,
+            k_weight.T,
+            v_weight.T,
+            packed_small.reshape(k_own, depth_own),
+            o_weight.T,
+        ],
         1,
     )
-    gate_own, up_own, down_own, small_t = lax.optimization_barrier(
-        (gate_weight.T, up_weight.T, down_weight, small_t)
+    gate_own, up_own, down_own, output_line = lax.optimization_barrier(
+        (gate_weight.T, up_weight.T, down_weight, output_line)
+    )
+    query_t, key_t, value_t, small_t = (
+        member[0] for member in gather_col([line[None] for line in plane_lines], 8)
     )
     gate_t = gather_row(gate_own)
     up_t = gather_row(up_own)
@@ -1570,8 +1695,6 @@
     query_slots = col_place * own_rows + jnp.arange(own_rows, dtype=jnp.int32)
     query_starts = seq_starts(query_slots, lengths)
     cosines, sines = rope_tables(query_slots - query_starts, HD)
-    group_size = HQ // KVH
-    score_scale = 1.0 / math.sqrt(HD)
     inputs_wide = hidden_in.astype(F32)
     first_rms = rms_scale(inputs_wide)
     first_unit = inputs_wide * first_rms
@@ -1587,25 +1710,11 @@
     )
     window = min(own_rows + MAXLEN, row_tokens)
     window_start = jnp.clip(col_place * own_rows - MAXLEN, 0, row_tokens - window)
-    key_slots = window_start + jnp.arange(window, dtype=jnp.int32)
-    key_starts = seq_starts(key_slots, lengths)
-    visible = (query_starts[:, None] == key_starts[None, :]) & (
-        key_slots[None, :] <= query_slots[:, None]
-    )
     both_window = lax.dynamic_slice_in_dim(both_all, window_start, window, 0)
-    keys_window = both_window[:, : KVH * HD].reshape(window, KVH, HD)
-    values_window = both_window[:, KVH * HD :].reshape(window, KVH, HD)
-    query_heads = queries.reshape(own_rows, KVH, group_size, HD)
-    scores = masked_scores(query_heads, keys_window, visible, score_scale)
-    peak = jnp.max(scores, axis=-1, keepdims=True)
-    expanded = jnp.exp(scores - peak)
-    totals = jnp.sum(expanded, axis=-1, keepdims=True)
-    probs = expanded / totals
-    log_total = peak + jnp.log(totals)
-    mixed = jnp.einsum(
-        "kgts,skd->tkgd", probs.astype(BF16), values_window, preferred_element_type=F32
-    )
-    mixed = mixed.reshape(own_rows, HQ * HD).astype(BF16)
+    places = jnp.stack([window_start, col_place * own_rows]).astype(jnp.int32)
+    starts = query_starts.astype(jnp.int32)[:, None]
+    queries = queries.reshape(own_rows, HQ * HD)
+    mixed = attention_forward(places, starts, queries, both_window, HD, KVH)
     residual = inputs_wide + dot_nt(mixed, output_t)
     second_rms = rms_scale(residual)
     second_unit = residual * second_rms
@@ -1654,36 +1763,13 @@
     )
     attended_grad = residual_grad.astype(BF16)
     mixed_grad = dot_nn(attended_grad, output_t).astype(BF16)
-    grad_heads = mixed_grad.reshape(own_rows, KVH, group_size, HD)
-    scores = masked_scores(query_heads, keys_window, visible, score_scale)
-    probs = jnp.exp(scores - log_total)
-    prob_grad = jnp.einsum(
-        "tkgd,skd->kgts", grad_heads, values_window, preferred_element_type=F32
-    )
-    value_part = jnp.einsum(
-        "kgts,tkgd->skd", probs.astype(BF16), grad_heads, preferred_element_type=F32
-    )
-    score_grad = (
-        probs * (prob_grad - jnp.sum(probs * prob_grad, axis=-1, keepdims=True))
-    ).astype(BF16)
-    query_grad = (
-        jnp.einsum("kgts,skd->tkgd", score_grad, keys_window, preferred_element_type=F32)
-        * score_scale
-    )
-    key_part = (
-        jnp.einsum("kgts,tkgd->skd", score_grad, query_heads, preferred_element_type=F32)
-        * score_scale
-    )
-    both_part = jnp.concatenate(
-        [key_part.reshape(window, KVH * HD), value_part.reshape(window, KVH * HD)], axis=1
-    ).astype(BF16)
-    both_rows = lax.dynamic_update_slice_in_dim(
-        jnp.zeros((row_tokens, 2 * KVH * HD), BF16), both_part, window_start, 0
+    query_grad, both_rows = attention_backward(
+        places, starts, queries, mixed_grad, both_window, HD, KVH, row_tokens
     )
     both_rows, down_grad_own = lax.optimization_barrier((both_rows, down_grad_own))
     both_grad = scatter_col([both_rows[None]], 5)[0][0]
     key_grad, value_grad = both_grad[:, : KVH * HD], both_grad[:, KVH * HD :]
-    query_wide = rounded_wide(query_grad.reshape(own_rows, HQ, HD))
+    query_wide = query_grad.reshape(own_rows, HQ, HD).astype(F32)
     query_base_grad = (
         rotate_back(query_wide, cosines, sines).reshape(own_rows, HQ * HD).astype(BF16)
     )

time: 560 us -> 544 us (0.971)
  Pallas kernels: 346 us -> 414 us
  waiting for transfers between devices: 43.8 us -> 1.51 us
  matrix products: 62.9 us -> 32.7 us
  other arithmetic: 37.7 us -> 27.3 us
    all_gather x3, waiting for transfers between devices: 42.3 us -> 0.04 us  [gather_row(): return lax.all_gather(block, 'row', axis=block.ndim - 1, tiled=True)]
    dot_general x6 -> x0, matrix products: 38.5 us -> none  [the longest x1 12.7 us: shards(): jnp.einsum('tkgd,skd->kgts', grad_heads, values_window, preferred_element...]
    pallas_call x0 -> x2, Pallas kernels: none -> 38.4 us  [the longest x1 23.7 us: attention_backward(): pl.pallas_call(functools.partial(attention_backward_kernel, 1.0 / math.sq...]
    pallas_call x1 -> x2, Pallas kernels: 35.5 us -> 70.6 us  [plane_gather(): pl.pallas_call(functools.partial(plane_gather_kernel, count), out_shape=o...]
    pallas_call x1, Pallas kernels: 37.6 us -> 28.4 us  [grid_gather(): pl.pallas_call(functools.partial(grid_gather_kernel, count, extra, places...]
    dynamic_update_slice x1 -> x0, local copies, waits for them, and re-layouts: 8.09 us -> none  [shards(): lax.dynamic_update_slice_in_dim(jnp.zeros((row_tokens, 2 * KVH * HD), BF1...]
    reduce_sum x1 -> x0, other arithmetic: 7.7 us -> none  [shards(): totals = jnp.sum(expanded, axis=-1, keepdims=True)]
    convert_element_type x1 -> x0, other arithmetic: 7.58 us -> none  [shards(): score_grad = (probs * (prob_grad - jnp.sum(probs * prob_grad, axis=-1, ke...]
  transfers between devices with their start and end apart: 6 -> 6, of which waited for: 2 -> 0; matrix products, arithmetic and copies ran while one was open for 23% -> 17% of each run, Pallas kernels for 56% -> 72%
where the time goes in v6:
time: 544 us; the launch traced here: 533 us
  Pallas kernels  414 us (76%)
  local copies, waits for them, and re-layouts  42.8 us (8%)
  matrix products  32.7 us (6%)
  other arithmetic  27.3 us (5%)
  between operations  15.1 us (3%)
    pallas_call x1, Pallas kernels, grid_scatter(): pl.pallas_call(functools.partial(grid_scatter_kernel, count, places), out...  78.1 us
    pallas_call x2, Pallas kernels, plane_gather(): pl.pallas_call(functools.partial(plane_gather_kernel, count), out_shape=o...  70.6 us
    pallas_call x1, Pallas kernels, ffn_backward(): pl.pallas_call(ffn_backward_kernel, out_shape=[jax.ShapeDtypeStruct((tota...  69.6 us
    pallas_call x3, Pallas kernels, weight_grad(): pl.pallas_call(weight_grad_kernel, grid=(depth // tile,), out_shape=jax.S...  39.3 us
    pallas_call x1, Pallas kernels, ffn_gate(): pl.pallas_call(ffn_gate_kernel, out_shape=[jax.ShapeDtypeStruct((rows * 8...  37.1 us
    pallas_call x1, Pallas kernels, ffn_up(): pl.pallas_call(ffn_up_kernel, out_shape=[jax.ShapeDtypeStruct((rows * 8,...  35.8 us
    pallas_call x1, Pallas kernels, grid_gather(): pl.pallas_call(functools.partial(grid_gather_kernel, count, extra, places...  28.4 us
    pallas_call x1, Pallas kernels, attention_backward(): pl.pallas_call(functools.partial(attention_backward_kernel, 1.0 / math.sq...  23.7 us
  transfers between devices with their start and end apart: 6, of which 0 were waited for; matrix products, arithmetic and copies ran while one was open for 17% of the time, Pallas kernels for 72%

profile of v6, /device:TPU:8, one launch (start us, length us, event | category | flops | bytes accessed | tf_op | source)
XLA Modules:
  0.0 533.4 jit_solution(6987212597470091565)
XLA Ops:
  7.2 3.4 concatenate.35
  11.3 28.4 %grid_gather.1 = (bf16[192,1536]{1,0:T(8,128)(2,1)}, bf16[32,1536]{1,0:T(8,128)(2,1)}, bf16[32,1536]{1,0:T(8,128)(2,1)}, bf16[32,1536]{1,0:T(8,128)(2,1)}, bf16[192,1536]{1,0:T(8,128)(2,1)}) custom-call(bf16[192,384]{1,0:T(8,128)(2,1)} %bitcast.124, bf16[32,384]{1,0:T(8,128)(2,1)} %bitcast.131, bf16[32,384]{1,0:T(8,128)(2,1)} %bitcast.132, ...), custom_call_target="tpu_custom_call" | custom-call | tf_op jit(solution)/shard_map/grid_gather/pallas_call | solution.py:1307
  41.3 36.8 %plane_gather.2 = (bf16[1,1536,1536]{2,1,0:T(8,128)(2,1)}, bf16[1,256,1536]{2,1,0:T(8,128)(2,1)}, bf16[1,256,1536]{2,1,0:T(8,128)(2,1)}, bf16[1,256,1536]{2,1,0:T(8,128)(2,1)}) custom-call(bf16[1,192,1536]{2,1,0:T(8,128)(2,1)} %bitcast.118, bf16[1,32,1536]{2,1,0:T(8,128)(2,1)} %bitcast.126, bf16[1,32,1536]{2,1,0:T(8,128)(2,1)} %bitcast.127, ...), custom_call_target="tpu_custom_call" | custom-call | tf_op jit(solution)/shard_map/plane_gather/pallas_call | solution.py:175
  87.9 5.0 fusion.8
  92.8 3.0 copy.56
  98.6 3.0 copy.57
  103.9 33.8 %plane_gather.3 = (bf16[1,2048,512]{2,1,0:T(8,128)(2,1)}, bf16[1,1536,1536]{2,1,0:T(8,128)(2,1)}) custom-call(bf16[1,256,512]{2,1,0:T(8,128)(2,1)} %maximum_bitcast_fusion.refs_0_, bf16[1,192,1536]{2,1,0:T(8,128)(2,1)} %bitcast.119), custom_call_target="tpu_custom_call" | custom-call | tf_op jit(solution)/shard_map/plane_gather/pallas_call | solution.py:175
  138.3 2.7 dynamic-slice_bitcast_fusion.keys.values
  142.2 14.7 %attention_forward.1 = bf16[256,1536]{1,0:T(8,128)(2,1)} custom-call(s32[2]{0:T(128)} %pad_add_fusion.places, s32[256,1]{1,0:T(8,128)} %copy.62.starts, bf16[256,1536]{1,0:T(8,128)(2,1)} %add_convert_fusion.1.query, bf16[1280,512]{1,0:T(8,128)(2,1)} %dynamic-slice_bitcast_fusion.keys.values, bf16[1280,512]{1,0:T(8,128)(2,1)} %dynamic-slice_bitcast_fusion.keys.values), custom_call_target="tpu_custom_call" | custom-call | tf_op jit(solution)/shard_map/attention_forward/pallas_call | solution.py:1015
  156.9 4.3 multiply_reduce_fusion.2
  162.5 37.1 %ffn_gate.1 = (bf16[2048,1536]{1,0:T(8,128)(2,1)}, f32[2048,1120]{1,0:T(8,128)}) custom-call(bf16[256,1536]{1,0:T(8,128)(2,1)} %multiply_convert_fusion.normed, bf16[1120,1536]{1,0:T(8,128)(2,1)} %all-gather.6.cloned.1.call-done.gate_t), custom_call_target="tpu_custom_call" | custom-call | tf_op jit(solution)/shard_map/ffn_gate/pallas_call | solution.py:489
  199.6 35.8 %ffn_up.1 = (bf16[2048,1536]{1,0:T(8,128)(2,1)}, bf16[2048,1120]{1,0:T(8,128)(2,1)}, bf16[2048,1120]{1,0:T(8,128)(2,1)}, bf16[2048,1120]{1,0:T(8,128)(2,1)}) custom-call(bf16[256,1536]{1,0:T(8,128)(2,1)} %cotangent.1, bf16[1120,1536]{1,0:T(8,128)(2,1)} %all-gather.4.cloned.1.call-done.up_t, bf16[2048,1536]{1,0:T(8,128)(2,1)} %get-tuple-element.70.normed_rows.left, ...), custom_call_target="tpu_custom_call" | custom-call | tf_op jit(solution)/shard_map/ffn_up/pallas_call | solution.py:619
  235.4 13.1 %weight_grad.3 = bf16[1536,1120]{1,0:T(8,128)(2,1)} custom-call(bf16[2048,1536]{1,0:T(8,128)(2,1)} %get-tuple-element.74.left.out_rows, bf16[2048,1120]{1,0:T(8,128)(2,1)} %get-tuple-element.73.right.hidden), custom_call_target="tpu_custom_call" | custom-call | flops 7046430720 | bytes 14319616 | tf_op jit(solution)/shard_map/weight_grad/pallas_call | solution.py:911
  248.6 69.6 %ffn_backward.1 = (bf16[2048,1120]{1,0:T(8,128)(2,1)}, bf16[2048,1120]{1,0:T(8,128)(2,1)}, f32[256,1536]{1,0:T(8,128)}, f32[256,1536]{1,0:T(8,128)}) custom-call(bf16[2048,1536]{1,0:T(8,128)(2,1)} %get-tuple-element.74.left.out_rows, bf16[2048,1120]{1,0:T(8,128)(2,1)} %get-tuple-element.73.right.hidden, bf16[2048,1120]{1,0:T(8,128)(2,1)} %get-tuple-element.75.silu, ...), custom_call_target="tpu_custom_call" | custom-call | tf_op jit(solution)/shard_map/ffn_backward/pallas_call | solution.py:868
  318.2 12.9 %weight_grad.4 = bf16[1536,1120]{1,0:T(8,128)(2,1)} custom-call(bf16[2048,1536]{1,0:T(8,128)(2,1)} %get-tuple-element.70.normed_rows.left, bf16[2048,1120]{1,0:T(8,128)(2,1)} %get-tuple-element.79.right), custom_call_target="tpu_custom_call" | custom-call | flops 7046430720 | bytes 14319616 | tf_op jit(solution)/shard_map/weight_grad/pallas_call | solution.py:911
  331.2 13.3 %weight_grad.5 = bf16[1536,1120]{1,0:T(8,128)(2,1)} custom-call(bf16[2048,1536]{1,0:T(8,128)(2,1)} %get-tuple-element.70.normed_rows.left, bf16[2048,1120]{1,0:T(8,128)(2,1)} %get-tuple-element.81.right), custom_call_target="tpu_custom_call" | custom-call | flops 7046430720 | bytes 14319616 | tf_op jit(solution)/shard_map/weight_grad/pallas_call | solution.py:911
  346.4 4.2 multiply_add_fusion
  350.7 4.7 fusion.14.cotangent
  355.3 23.7 %attention_backward.1 = (bf16[256,1536]{1,0:T(8,128)(2,1)}, bf16[2048,512]{1,0:T(8,128)(2,1)}) custom-call(s32[2]{0:T(128)} %pad_add_fusion.places, s32[256,1]{1,0:T(8,128)} %copy.62.starts, bf16[256,1536]{1,0:T(8,128)(2,1)} %add_convert_fusion.1.query, bf16[256,1536]{1,0:T(8,128)(2,1)} %fusion.14.cotangent, ...), custom_call_target="tpu_custom_call" | custom-call | tf_op jit(solution)/shard_map/attention_backward/pallas_call | solution.py:1034
  379.1 2.6 copy.65
  384.6 3.0 copy.66
  387.6 2.8 fusion.54
  391.1 5.2 convolution_convert_fusion.1.refs_0_
  396.3 3.6 convolution_convert_fusion.refs_1_
  399.9 2.5 fusion.4
  402.5 16.6 %plane_scatter.1 = f32[1,256,512]{2,1,0:T(8,128)} custom-call(bf16[1,2048,512]{2,1,0:T(8,128)(2,1)} %bitcast.111), custom_call_target="tpu_custom_call" | custom-call | tf_op jit(solution)/shard_map/plane_scatter/pallas_call | solution.py:330
  422.6 2.2 convolution_add_fusion.1
  429.9 2.8 copy.70
  435.5 78.1 %grid_scatter.1 = (f32[192,384]{1,0:T(8,128)}, f32[192,384]{1,0:T(8,128)}, f32[32,384]{1,0:T(8,128)}, f32[32,384]{1,0:T(8,128)}, f32[32,384]{1,0:T(8,128)}) custom-call(bf16[1536,1536]{1,0:T(8,128)(2,1)} %convolution_convert_fusion.1.refs_0_, bf16[1536,1536]{1,0:T(8,128)(2,1)} %convolution_convert_fusion.refs_1_, ...), custom_call_target="tpu_custom_call" | custom-call | tf_op jit(solution)/shard_map/grid_scatter/pallas_call | solution.py:1597
  514.4 2.4 copy.68
  518.0 3.0 fusion.25
  521.0 2.5 copy.69
  (150 shorter events, 41.7 us)
Async XLA Ops:
  7.2 155.3 %all-gather.6.cloned.1.call-start = ((), (), s32[]{:S(2)}) async-start(), calls=%async_computation.4 | async-start | bytes 4300800 | tf_op jit(solution)/shard_map/all_gather | solution.py:1053
  39.7 159.9 %all-gather.4.cloned.1.call-start = ((), (), s32[]{:S(2)}) async-start(), calls=%async_computation.3 | async-start | bytes 4300800 | tf_op jit(solution)/shard_map/all_gather | solution.py:1053
  40.5 208.1 %all-gather.8.cloned.1.call-start = ((), (), s32[]{:S(2)}) async-start(), calls=%async_computation.5 | async-start | bytes 4300800 | tf_op jit(solution)/shard_map/all_gather | solution.py:1053
  41.2 361.2 %reduce-scatter.4.cloned.1.call-start = ((), (), s32[]{:S(2)}) async-start(), calls=%async_computation.6 | async-start | bytes 4423680 | tf_op jit(solution)/shard_map/reduce_scatter | solution.py:1057
  79.9 1.1 copy-start.1
  80.0 1.3 copy-start.24
  80.0 2.6 copy-start.12
  81.2 6.6 %copy-start.20 = (f32[256]{0:T(256)}, f32[256]{0:T(256)S(1)}, u32[]{:S(2)}) copy-start(f32[256]{0:T(256)S(1)} %add_rsqrt_fusion.1) | copy-start | bytes 3076
  83.7 18.2 %copy-start.7 = (f32[256,128]{1,0:T(8,128)}, f32[256,128]{1,0:T(8,128)S(1)}, u32[]{:S(2)}) copy-start(f32[256,128]{1,0:T(8,128)S(1)} %copy.60) | copy-start | bytes 393220
  101.6 1.1 copy-start.25
  103.9 37.1 %copy-start.3 = (f32[256,1536]{1,0:T(8,128)S(1)}, f32[256,1536]{1,0:T(8,128)}, u32[]{:S(2)}) copy-start(f32[256,1536]{1,0:T(8,128)} %fusion.8) | copy-start | bytes 4718596
  137.7 3.3 copy-start.4
  161.2 183.3 %copy-start = (f32[256,1536]{1,0:T(8,128)}, f32[256,1536]{1,0:T(8,128)S(1)}, u32[]{:S(2)}) copy-start(f32[256,1536]{1,0:T(8,128)S(1)} %get-tuple-element.173) | copy-start | bytes 4718596
  248.5 184.2 %reduce-scatter.6.cloned.1.call-start = ((), (), s32[]{:S(2)}) async-start(), calls=%async_computation.7 | async-start | bytes 4423680 | tf_op jit(solution)/shard_map/reduce_scatter | solution.py:1057
  331.2 189.8 %reduce-scatter.8.cloned.1.call-start = ((), (), s32[]{:S(2)}) async-start(), calls=%async_computation.8 | async-start | bytes 4423680 | tf_op jit(solution)/shard_map/reduce_scatter | solution.py:1057
  387.6 3.5 copy-start.22
  391.1 5.2 copy-start.6
  391.1 8.8 %slice-start = ((s8[4718592]{0:T(1024)(128)(4,1)}), s8[4194304]{0:T(1024)(128)(4,1)S(1)}, s32[]{:S(2)}) async-start(s8[4718592]{0:T(1024)(128)(4,1)} %bitcast.136), calls=%async_computation.9 | async-start | bytes 8388608
  396.3 3.6 copy-start.5
  396.3 3.6 slice-start.1
  402.5 18.4 %copy-start.8 = (f32[256,128]{1,0:T(8,128)S(1)}, f32[256,128]{1,0:T(8,128)}, u32[]{:S(2)}) copy-start(f32[256,128]{1,0:T(8,128)} %copy-done.7) | copy-start | bytes 393220
  422.6 2.2 copy-start.2
  422.6 2.2 copy-start.11
  422.6 2.2 copy-start.23
  424.8 1.8 copy-start.18
  424.9 1.8 copy-start.19
  427.0 1.7 copy-start.9
  429.9 2.8 copy-start.13
  520.9 2.5 copy-start.15
  520.9 3.2 copy-start.17
  520.9 3.9 copy-start.16
  520.9 4.5 copy-start.14
  (2 other events, 2.3 us)
Sparse Core Ops, SparseCore 0:
  39.9 67.2 all-gather.5
  108.8 66.6 all-gather.3
  177.1 66.6 all-gather.7
  248.7 67.8 reduce-scatter.3
  331.3 66.8 reduce-scatter.5
  400.3 66.6 reduce-scatter.7
